TPU v7x, 8 devices: a whole 2x2x1 slice. The times are simulated.
8 devices in a mesh: dp: 8 (over z, y, x, core).
Axes of the slice: x: 2, y: 2, z: 1, core: 2. Of those that a mesh axis runs over, the one named last changes fastest.
Arguments:
- g_mat: bfloat16 [8, 19660800], P('dp')
- g_vec: bfloat16 [8, 24320], P('dp')
- p_mat: float32 [19660800], P('dp')
- m_mat: float32 [19660800], P('dp')
- v_mat: float32 [19660800], P('dp')
- p_vec: float32 [24320], replicated
- m_vec: float32 [24320], replicated
- v_vec: float32 [24320], replicated
- learn_rate: float32 [], replicated
Outputs:
- output 1: float32 [19660800], P('dp')
- output 2: float32 [19660800], P('dp')
- output 3: float32 [19660800], P('dp')
- output 4: float32 [24320], replicated
- output 5: float32 [24320], replicated
- output 6: float32 [24320], replicated
- output 7: bfloat16 [19660800], replicated
All inputs are finite; a program needn't handle non-finite values.
Results may differ from a plain program's by a relative error of at most 0.001.
Values are sent between devices in bfloat16 or wider.
A program may use at most 1 GiB of HBM per device.

v0:
```python
import jax
import jax.numpy as jnp
from jax import lax
from jax.sharding import PartitionSpec as P

STEP = 10
ADAM_BETA1 = 0.9
ADAM_BETA2 = 0.98
ADAM_EPS = 1e-8
WEIGHT_DECAY = 0.01
MAX_NORM = 1.0
NORM_EPS = 1e-6
BIAS_ONE = 1.0 - ADAM_BETA1 ** STEP
BIAS_TWO = 1.0 - ADAM_BETA2 ** STEP


def adam_update(grad_vals, param_vals, moment_one, moment_two, learn_rate, decay_rate):
    new_one = ADAM_BETA1 * moment_one + (1.0 - ADAM_BETA1) * grad_vals
    new_two = ADAM_BETA2 * moment_two + (1.0 - ADAM_BETA2) * grad_vals * grad_vals
    direction = (new_one / BIAS_ONE) / (jnp.sqrt(new_two / BIAS_TWO) + ADAM_EPS)
    return param_vals - learn_rate * (direction + decay_rate * param_vals), new_one, new_two


def solution(mesh):
    axis_name = mesh.axis_names[0]
    group_size = mesh.shape[axis_name]

    def local_step(g_mat, g_vec, p_mat, m_mat, v_mat, p_vec, m_vec, v_vec, learn_rate):
        send_rows = g_mat.reshape(group_size, -1)
        recv_rows = lax.all_to_all(send_rows, axis_name, 0, 0, tiled=True)
        grad_mat = jnp.sum(recv_rows.astype(jnp.float32), axis=0) / group_size
        grad_vec = lax.psum(g_vec[0].astype(jnp.float32), axis_name) / group_size
        norm_sq = lax.psum(jnp.sum(grad_mat * grad_mat), axis_name) + jnp.sum(grad_vec * grad_vec)
        clip_scale = jnp.minimum(1.0, MAX_NORM / (jnp.sqrt(norm_sq) + NORM_EPS))
        new_p_mat, new_m_mat, new_v_mat = adam_update(grad_mat * clip_scale, p_mat, m_mat, v_mat, learn_rate, WEIGHT_DECAY)
        new_p_vec, new_m_vec, new_v_vec = adam_update(grad_vec * clip_scale, p_vec, m_vec, v_vec, learn_rate, 0.0)
        full_params = lax.all_gather(new_p_mat.astype(jnp.bfloat16), axis_name, tiled=True)
        return new_p_mat, new_m_mat, new_v_mat, new_p_vec, new_m_vec, new_v_vec, full_params

    return jax.shard_map(
        local_step,
        mesh=mesh,
        in_specs=(P(axis_name, None), P(axis_name, None), P(axis_name), P(axis_name), P(axis_name), P(), P(), P(), P()),
        out_specs=(P(axis_name), P(axis_name), P(axis_name), P(), P(), P(), P()),
        check_vma=False,
    )
```

profile of v0, /device:TPU:0, one launch (start us, length us, event | category | flops | bytes accessed | tf_op | source)
XLA Modules:
  0.0 1337.2 jit_solution(10894490044179662926)
XLA Ops:
  7.2 0.5 broadcast.9
  7.7 227.9 %reduce.3 = bf16[8,2457600]{1,0:T(8,128)(2,1)} reduce(bf16[8,1,2457600]{2,1,0:T(2,128)(2,1)} %bitcast, bf16[]{:T(256)} %broadcast.9), dimensions={1}, to_apply=%bitcast.reduce_sub_computation | reduce | bytes 78643200 | tf_op jit(solution)/shard_map/all_to_all | solution.py:30
  235.6 201.9 %reshape.23 = bf16[8,2,1228800]{2,1,0:T(2,128)(2,1)} reshape(bf16[8,2457600]{1,0:T(8,128)(2,1)} %reduce.3) | data formatting | bytes 78643200
  437.5 0.0 copy-start.4
  437.5 6.5 all-to-all-start
  444.0 0.0 all-reduce.2.cloned.1.call-start
  444.1 0.0 copy-done.4
  444.1 0.9 convert_reduce_fusion.1
  445.0 0.0 all-reduce.2.cloned.1.call-update
  445.0 0.0 all-gather.2.cloned.1.call-start
  445.7 426.8 %all-to-all-done = bf16[8,2,1228800]{2,1,0:T(2,128)(2,1)} async-done(((bf16[8,2,1228800]{2,1,0:T(2,128)(2,1)}), bf16[8,2,1228800]{2,1,0:T(2,128)(2,1)}, u32[]{:S(2)}, u32[]{:S(2)}) %all-to-all-start) | async-done | bytes 39321632 | tf_op jit(solution)/shard_map/all_to_all | solution.py:30
  872.5 82.1 %reshape.24 = bf16[8,1,2457600]{2,1,0:T(2,128)(2,1)} reshape(bf16[8,2,1228800]{2,1,0:T(2,128)(2,1)} %all-to-all-done) | data formatting | bytes 78643200
  954.6 108.6 %convert_reduce_fusion = f32[2457600]{0:T(1024)} fusion(bf16[8,1,2457600]{2,1,0:T(2,128)(2,1)} %reshape.24), kind=kLoop, calls=%fused_computation | loop fusion | flops 36864000 | bytes 49152000 | tf_op jit(solution)/shard_map/reduce_sum | solution.py:31
  1063.2 6.2 multiply_reduce_fusion
  1069.3 0.0 all-reduce.2.cloned.1.call-done
  1069.3 1.5 multiply_reduce_fusion.1
  1070.9 22.4 %psum.14 = f32[]{:T(128)} all-reduce(f32[]{:T(128)} %multiply_reduce_fusion), channel_id=1, replica_groups=mesh['dp'=8] {'dp'}, use_global_device_ids=true, to_apply=%region_2.0 | all-reduce | flops 1 | bytes 8 | tf_op jit(solution)/shard_map/psum | solution.py:33
  1094.7 0.0 copy-start
  1094.7 0.0 copy-start.1
  1094.7 0.0 copy-start.2
  1094.7 0.0 copy-start.3
  1094.7 26.6 %fusion.2 = (bf16[2457600]{0:T(1024)(128)(2,1)}, f32[2457600]{0:T(1024)}, f32[2457600]{0:T(1024)}, f32[2457600]{0:T(1024)}) fusion(f32[2457600]{0:T(1024)} %param.11, f32[]{:T(128)S(6)} %copy.18, f32[2457600]{0:T(1024)} %convert_reduce_fusion, f32[]{:T(128)S(6)} %mul.103, f32[2457600]{0:T(1024)} %param.12, f32[2457600]{0:T(1024)} %param.13), kind=kLoop, calls=%fused_computation.12 | loop fusion | flops 41779200 | bytes 73728008 | tf_op jit(solution)/shard_map/convert_element_type | solution.py:37
  1121.3 0.0 all-gather.2.cloned.1.call-update
  1121.3 0.0 copy-done
  1121.4 0.0 copy-done.1
  1121.4 0.0 copy-done.2
  1121.4 0.0 copy-done.3
  1121.4 0.8 multiply_subtract_fusion.1
  1122.1 181.1 %all-gather.2.cloned.1.call-done = bf16[19660800]{0:T(1024)(128)(2,1)} async-done(((bf16[2457600]{0:T(1024)(128)(2,1)}), bf16[19660800]{0:T(1024)(128)(2,1)}) %all-gather.2.cloned.1.call-update) | async-done | bytes 39321616 | tf_op jit(solution)/shard_map/all_gather | solution.py:37
  1303.2 26.8 %copy.19 = bf16[19660800]{0:T(1024)(128)(2,1)} copy(bf16[19660800]{0:T(1024)(128)(2,1)} %all-gather.2.cloned.1.call-done) | data formatting | bytes 78643200
Async XLA Ops:
  437.5 6.6 copy-start.4
  437.5 435.0 %all-to-all-start = ((bf16[8,2,1228800]{2,1,0:T(2,128)(2,1)}), bf16[8,2,1228800]{2,1,0:T(2,128)(2,1)}, u32[]{:S(2)}, u32[]{:S(2)}) async-start(bf16[8,2,1228800]{2,1,0:T(2,128)(2,1)} %reshape.23), calls=%async_computation | async-start | bytes 78643200 | tf_op jit(solution)/shard_map/all_to_all | solution.py:30
  444.0 625.3 %all-reduce.2.cloned.1.call-start = ((), (), s32[]{:S(2)}) async-start(), calls=%async_computation.1 | async-start | bytes 196608 | tf_op jit(solution)/shard_map/psum | solution.py:32
  445.0 858.2 %all-gather.2.cloned.1.call-start = ((), (), s32[]{:S(2)}) async-start(), calls=%async_computation.2 | async-start | bytes 44236800 | tf_op jit(solution)/shard_map/all_gather | solution.py:37
  1094.7 26.7 %copy-start = (f32[24320]{0:T(1024)S(1)}, f32[24320]{0:T(1024)}, u32[]{:S(2)}) copy-start(f32[24320]{0:T(1024)} %all-reduce.2.cloned.1.call-done) | copy-start | bytes 291844
  1094.7 26.7 %copy-start.1 = (f32[24320]{0:T(1024)S(1)}, f32[24320]{0:T(1024)}, u32[]{:S(2)}) copy-start(f32[24320]{0:T(1024)} %param.14) | copy-start | bytes 291844
  1094.7 26.7 %copy-start.2 = (f32[24320]{0:T(1024)S(1)}, f32[24320]{0:T(1024)}, u32[]{:S(2)}) copy-start(f32[24320]{0:T(1024)} %param.15) | copy-start | bytes 291844
  1094.7 26.7 %copy-start.3 = (f32[24320]{0:T(1024)S(1)}, f32[24320]{0:T(1024)}, u32[]{:S(2)}) copy-start(f32[24320]{0:T(1024)} %param.16) | copy-start | bytes 291844
Sparse Core Ops, SparseCore 0:
  448.5 201.6 all-reduce.1
  1121.5 181.6 all-gather.1
where the time goes:
time: 1350 us; the launch traced here: 1340 us
  waiting for transfers between devices  608 us (45%)
  other arithmetic  372 us (28%)
  local copies, waits for them, and re-layouts  311 us (23%)
  blocking collectives  22.4 us (2%)
  between operations  16.6 us (1%)
    all_to_all x1, waiting for transfers between devices, local_step(): recv_rows = lax.all_to_all(send_rows, axis_name, 0, 0, tiled=True)  427 us
    unnamed x13, local copies, waits for them, and re-layouts  311 us
    all_to_all x1, other arithmetic, local_step(): recv_rows = lax.all_to_all(send_rows, axis_name, 0, 0, tiled=True)  228 us
    all_gather x1, waiting for transfers between devices, local_step(): lax.all_gather(new_p_mat.astype(jnp.bfloat16), axis_name, tiled=True)  181 us
    reduce_sum x1, other arithmetic, local_step(): grad_mat = jnp.sum(recv_rows.astype(jnp.float32), axis=0) / group_size  109 us
  transfers between devices with their start and end apart: 3, of which 2 were waited for; matrix products, arithmetic and copies ran while one was open for 15% of the time, Pallas kernels for 0%

commit v1 on v0

v1 whole, which is shorter than its diff:
```python
import functools

import jax
import jax.numpy as jnp
from jax import lax
from jax.experimental import pallas as pl
from jax.experimental.pallas import tpu as pltpu
from jax.sharding import PartitionSpec as P

STEP = 10
ADAM_BETA1 = 0.9
ADAM_BETA2 = 0.98
ADAM_EPS = 1e-8
WEIGHT_DECAY = 0.01
MAX_NORM = 1.0
NORM_EPS = 1e-6
BIAS_ONE = 1.0 - ADAM_BETA1 ** STEP
BIAS_TWO = 1.0 - ADAM_BETA2 ** STEP

MESH = pl.DeviceIdType.MESH
LANES = 128
DEVICES = 8
CHUNKS = 10
BLOCK = 96


def adam_update(grad_vals, param_vals, moment_one, moment_two, learn_rate, decay_rate):
    new_one = ADAM_BETA1 * moment_one + (1.0 - ADAM_BETA1) * grad_vals
    new_two = ADAM_BETA2 * moment_two + (1.0 - ADAM_BETA2) * grad_vals * grad_vals
    direction = (new_one / BIAS_ONE) / (jnp.sqrt(new_two / BIAS_TWO) + ADAM_EPS)
    return param_vals - learn_rate * (direction + decay_rate * param_vals), new_one, new_two


def places(axis_name):
    me = lax.axis_index(axis_name)
    core, x, y = me % 2, (me // 2) % 2, me // 4

    def dev(yy, xx, cc):
        return 4 * yy + 2 * xx + cc

    return me, core, x, y, dev


def reduce_kernel(axis_name, half_rows, g_ref, gv_ref, gsum_ref, vsum_ref, clip_ref, stage_ref,
                  first, own_first, direct, own_direct, fsum, psum, raw, packed, vrecv, nsend, nrecv,
                  raw_sem, pack_sem, first_recv, direct_recv, psum_recv, send_sem, fsum_send,
                  vec_send, vec_recv, nrm_send, nrm_recv, out_sem):
    me, core, x, y, dev = places(axis_name)
    sib = dev(y, x, 1 - core)
    xs = [dev(y, 1 - x, 0), dev(y, 1 - x, 1)]
    ys = [dev(1 - y, x, 0), dev(1 - y, x, 1)]
    ds = [dev(1 - y, 1 - x, 0), dev(1 - y, 1 - x, 1)]
    x_mine, x_sib = dev(y, 1 - x, core), dev(y, 1 - x, 1 - core)
    y_mine, y_sib = dev(1 - y, x, core), dev(1 - y, x, 1 - core)
    rows = half_rows // CHUNKS
    vals = rows * LANES

    first_plan = [
        (2 * ds[0], ys[0], first, (0, core), first_recv),
        (2 * ds[0] + 1, xs[0], first, (1, core), first_recv),
        (2 * ds[1], ys[1], first, (0, core), first_recv),
        (2 * ds[1] + 1, xs[1], first, (1, core), first_recv),
        (2 * x_sib, sib, first, (0, 2), first_recv),
        (2 * y_sib + 1, sib, first, (1, 2), first_recv),
        (2 * x_mine, None, own_first, (0,), None),
        (2 * y_mine + 1, None, own_first, (1,), None),
    ]
    direct_plan = [
        (2 * ys[0], ys[0], direct, (0, core), direct_recv),
        (2 * xs[0] + 1, xs[0], direct, (1, core), direct_recv),
        (2 * ys[1], ys[1], direct, (0, core), direct_recv),
        (2 * xs[1] + 1, xs[1], direct, (1, core), direct_recv),
        (2 * sib, sib, direct, (0, 2), direct_recv),
        (2 * sib + 1, sib, direct, (1, 2), direct_recv),
        (2 * me, None, own_direct, (0,), None),
        (2 * me + 1, None, own_direct, (1,), None),
    ]

    def load_raw(plan, h, c):
        start = pl.multiple_of((plan[h][0] * CHUNKS + c) * vals, vals)
        return pltpu.make_async_copy(g_ref.at[:, pl.ds(start, vals)], raw.at[h], raw_sem.at[h])

    def stage_at(phase, h, c):
        return stage_ref.at[6 * phase + h, pl.ds(pl.multiple_of(c * rows, rows), rows), :]

    def to_stage(phase, h, c):
        return pltpu.make_async_copy(packed.at[h], stage_at(phase, h, c), pack_sem.at[h])

    def send(phase, plan, h, c):
        _, target, buf, slot, sems = plan[h]
        return pltpu.make_async_remote_copy(
            src_ref=stage_at(phase, h, c),
            dst_ref=buf.at[(*slot, pl.ds(pl.multiple_of(c * rows, rows), rows))],
            send_sem=send_sem.at[6 * phase + h, c],
            recv_sem=sems.at[(*slot, c)],
            device_id=(target,),
            device_id_type=MESH,
        )

    def pack(plan, h, c):
        _, target, buf, slot, _ = plan[h]

        def body(i, _):
            piece = raw[h, :, pl.ds(pl.multiple_of(i * BLOCK * LANES, BLOCK * LANES), BLOCK * LANES)]
            piece = piece.astype(jnp.float32).reshape(BLOCK, LANES).astype(jnp.bfloat16)
            if target is None:
                buf[(*slot, pl.ds(pl.multiple_of(c * rows + i * BLOCK, BLOCK), BLOCK), slice(None))] = piece
            else:
                packed[h, pl.ds(pl.multiple_of(i * BLOCK, BLOCK), BLOCK), :] = piece
            return 0

        lax.fori_loop(0, rows // BLOCK, body, 0)

    for h in range(8):
        load_raw(first_plan, h, 0).start()

    vrecv[me] = gv_ref[...]

    barrier = pltpu.get_barrier_semaphore()
    for o in range(1, DEVICES):
        pl.semaphore_signal(barrier, inc=1, device_id=((me + o) % DEVICES,), device_id_type=MESH)
    pl.semaphore_wait(barrier, DEVICES - 1)

    def vec_copy(o):
        return pltpu.make_async_remote_copy(
            src_ref=gv_ref, dst_ref=vrecv.at[me], send_sem=vec_send.at[o], recv_sem=vec_recv.at[me],
            device_id=((me + o) % DEVICES,), device_id_type=MESH)

    def vec_wait(o):
        src = (me + o) % DEVICES
        pltpu.make_async_copy(gv_ref, vrecv.at[src], vec_recv.at[src]).wait()

    for o in range(1, DEVICES):
        vec_copy(o).start()

    def send_phase(phase, plan, next_plan):
        def step(c, _):
            for h in range(8):
                load_raw(plan, h, c).wait()
                pack(plan, h, c)
                if next_plan is None:
                    @pl.when(c + 1 < CHUNKS)
                    def _():
                        load_raw(plan, h, c + 1).start()
                else:
                    @pl.when(c + 1 < CHUNKS)
                    def _():
                        load_raw(plan, h, c + 1).start()

                    @pl.when(c + 1 >= CHUNKS)
                    def _():
                        load_raw(next_plan, h, 0).start()
                if 1 <= h <= 6:
                    to_stage(phase, h - 1, c).start()
            for h in range(6):
                to_stage(phase, h, c).wait()
                send(phase, plan, h, c).start()
            return 0

        lax.fori_loop(0, CHUNKS, step, 0)

    send_phase(0, first_plan, direct_plan)
    send_phase(1, direct_plan, None)

    def got(buf, sems, slot, c):
        at = buf.at[(*slot, pl.ds(pl.multiple_of(c * rows, rows), rows))]
        pltpu.make_async_copy(at, at, sems.at[(*slot, c)]).wait()

    def fsum_copy(side, c):
        at = (side, pl.ds(pl.multiple_of(c * rows, rows), rows))
        return pltpu.make_async_remote_copy(
            src_ref=fsum.at[at], dst_ref=psum.at[at], send_sem=fsum_send.at[side, c], recv_sem=psum_recv.at[side, c],
            device_id=((x_mine, y_mine)[side],), device_id_type=MESH)

    def relay_step(c, _):
        for side in range(2):
            for slot in range(3):
                got(first, first_recv, (side, slot), c)

            def body(i, _, side=side):
                at = pl.ds(pl.multiple_of(c * rows + i * BLOCK, BLOCK), BLOCK)
                total = first[side, 0, at, :].astype(jnp.float32) + first[side, 1, at, :].astype(jnp.float32)
                total = total + (first[side, 2, at, :].astype(jnp.float32) + own_first[side, at, :].astype(jnp.float32))
                fsum[side, at, :] = total
                return 0

            lax.fori_loop(0, rows // BLOCK, body, 0)
            if side == 1:
                fsum_copy(0, c).start()
            else:
                @pl.when(c > 0)
                def _():
                    fsum_copy(1, c - 1).start()
        return 0

    lax.fori_loop(0, CHUNKS, relay_step, 0)

    for o in range(1, DEVICES):
        vec_wait(o)
    vec_total = vrecv[0].astype(jnp.float32)
    for d in range(1, DEVICES):
        vec_total = vec_total + vrecv[d].astype(jnp.float32)
    vec_mean = vec_total / DEVICES
    vsum_ref[...] = vec_mean
    fsum_copy(1, CHUNKS - 1).start()

    def out_copy(side, c):
        at = pl.ds(pl.multiple_of(c * rows, rows), rows)
        to = pl.ds(pl.multiple_of(side * half_rows + c * rows, rows), rows)
        return pltpu.make_async_copy(psum.at[side, at], gsum_ref.at[to], out_sem.at[side, c])

    def final_step(c, acc):
        for side in range(2):
            got(psum, psum_recv, (side,), c)
            for slot in range(3):
                got(direct, direct_recv, (side, slot), c)

            def body(i, acc, side=side):
                at = pl.ds(pl.multiple_of(c * rows + i * BLOCK, BLOCK), BLOCK)
                total = direct[side, 0, at, :].astype(jnp.float32) + direct[side, 1, at, :].astype(jnp.float32)
                total = total + (direct[side, 2, at, :].astype(jnp.float32) + own_direct[side, at, :].astype(jnp.float32))
                mean = (psum[side, at, :] + total) / DEVICES
                psum[side, at, :] = mean
                return acc + jnp.sum((mean * mean).reshape(BLOCK // 8, 8, LANES), axis=0)

            acc = lax.fori_loop(0, rows // BLOCK, body, acc)
            if side == 1:
                out_copy(0, c).start()
            else:
                @pl.when(c > 0)
                def _():
                    out_copy(1, c - 1).start()
        return acc

    acc = lax.fori_loop(0, CHUNKS, final_step, jnp.zeros((8, LANES), jnp.float32))
    nsend[...] = acc
    nrecv[me] = acc
    out_copy(1, CHUNKS - 1).start()

    def drain(c, _):
        for h in range(6):
            send(0, first_plan, h, c).wait_send()
            send(1, direct_plan, h, c).wait_send()
        return 0

    lax.fori_loop(0, CHUNKS, drain, 0)

    def nrm_copy(o):
        return pltpu.make_async_remote_copy(
            src_ref=nsend, dst_ref=nrecv.at[me], send_sem=nrm_send.at[o], recv_sem=nrm_recv.at[me],
            device_id=((me + o) % DEVICES,), device_id_type=MESH)

    def nrm_wait(o):
        src = (me + o) % DEVICES
        pltpu.make_async_copy(nsend, nrecv.at[src], nrm_recv.at[src]).wait()

    for o in range(1, DEVICES):
        nrm_copy(o).start()

    def drain_rest(c, _):
        for side in range(2):
            fsum_copy(side, c).wait_send()
            out_copy(side, c).wait()
        return 0

    lax.fori_loop(0, CHUNKS, drain_rest, 0)
    for o in range(1, DEVICES):
        vec_copy(o).wait_send()
    for o in range(1, DEVICES):
        nrm_wait(o)
    tile = jnp.sum((vec_mean * vec_mean).reshape(-1, 8, LANES), axis=0)
    for d in range(DEVICES):
        tile = tile + nrecv[d]
    norm_sq = jnp.full((8, LANES), jnp.sum(tile), jnp.float32)
    clip_ref[...] = jnp.minimum(1.0, MAX_NORM / (jnp.sqrt(norm_sq) + NORM_EPS))
    for o in range(1, DEVICES):
        nrm_copy(o).wait_send()


def reduce_gradients(axis_name, g_mat, g_vec_rows):
    half_rows = g_mat.shape[1] // (2 * DEVICES * LANES)
    rows = half_rows // CHUNKS
    vec_rows = g_vec_rows.shape[0]
    bf16, f32 = jnp.bfloat16, jnp.float32
    dma = pltpu.SemaphoreType.DMA
    hbm, vmem = pl.BlockSpec(memory_space=pltpu.HBM), pl.BlockSpec(memory_space=pltpu.VMEM)
    return pl.pallas_call(
        functools.partial(reduce_kernel, axis_name, half_rows),
        out_shape=(
            jax.ShapeDtypeStruct((2 * half_rows, LANES), f32),
            jax.ShapeDtypeStruct((vec_rows, LANES), f32),
            jax.ShapeDtypeStruct((8, LANES), f32),
            jax.ShapeDtypeStruct((12, half_rows, LANES), bf16),
        ),
        in_specs=[hbm, vmem],
        out_specs=(hbm, vmem, vmem, hbm),
        scratch_shapes=[
            pltpu.VMEM((2, 3, half_rows, LANES), bf16),
            pltpu.VMEM((2, half_rows, LANES), bf16),
            pltpu.VMEM((2, 3, half_rows, LANES), bf16),
            pltpu.VMEM((2, half_rows, LANES), bf16),
            pltpu.VMEM((2, half_rows, LANES), f32),
            pltpu.VMEM((2, half_rows, LANES), f32),
            pltpu.VMEM((8, 1, rows * LANES), bf16),
            pltpu.VMEM((6, rows, LANES), bf16),
            pltpu.VMEM((DEVICES, vec_rows, LANES), bf16),
            pltpu.VMEM((8, LANES), f32),
            pltpu.VMEM((DEVICES, 8, LANES), f32),
            dma((8,)),
            dma((6,)),
            dma((2, 3, CHUNKS)),
            dma((2, 3, CHUNKS)),
            dma((2, CHUNKS)),
            dma((12, CHUNKS)),
            dma((2, CHUNKS)),
            dma((DEVICES,)),
            dma((DEVICES,)),
            dma((DEVICES,)),
            dma((DEVICES,)),
            dma((2, CHUNKS)),
        ],
        compiler_params=pltpu.CompilerParams(
            collective_id=0, has_side_effects=True, vmem_limit_bytes=67043328
        ),
        name="reduce_gradients",
    )(g_mat, g_vec_rows)


def solution(mesh):
    axis_name = mesh.axis_names[0]

    def local_step(g_mat, g_vec, p_mat, m_mat, v_mat, p_vec, m_vec, v_vec, learn_rate):
        vec_size = g_vec.shape[1]
        vec_rows = -(-vec_size // (16 * LANES)) * 16
        g_vec_rows = jnp.pad(g_vec[0], (0, vec_rows * LANES - vec_size)).reshape(vec_rows, LANES)
        grad_mat, grad_vec, clip, _ = reduce_gradients(axis_name, g_mat, g_vec_rows)
        clip_scale = clip[0, 0]
        grad_mat = grad_mat.reshape(-1)
        grad_vec = grad_vec.reshape(-1)[:vec_size]
        new_p_mat, new_m_mat, new_v_mat = adam_update(grad_mat * clip_scale, p_mat, m_mat, v_mat, learn_rate, WEIGHT_DECAY)
        new_p_vec, new_m_vec, new_v_vec = adam_update(grad_vec * clip_scale, p_vec, m_vec, v_vec, learn_rate, 0.0)
        full_params = lax.all_gather(new_p_mat.astype(jnp.bfloat16), axis_name, tiled=True)
        return new_p_mat, new_m_mat, new_v_mat, new_p_vec, new_m_vec, new_v_vec, full_params

    return jax.shard_map(
        local_step,
        mesh=mesh,
        in_specs=(P(axis_name, None), P(axis_name, None), P(axis_name), P(axis_name), P(axis_name), P(), P(), P(), P()),
        out_specs=(P(axis_name), P(axis_name), P(axis_name), P(), P(), P(), P()),
        check_vma=False,
    )
```

time: 1350 us -> 588 us (0.44)
  waiting for transfers between devices: 608 us -> 179 us
  other arithmetic: 372 us -> 29.8 us
  Pallas kernels: 0 us -> 335 us
  local copies, waits for them, and re-layouts: 311 us -> 28.7 us
  blocking collectives: 22.4 us -> 0 us
    all_to_all x1 -> x0, waiting for transfers between devices: 427 us -> none  [local_step(): recv_rows = lax.all_to_all(send_rows, axis_name, 0, 0, tiled=True)]
    pallas_call x0 -> x1, Pallas kernels: none -> 335 us  [reduce_gradients(): pl.pallas_call(functools.partial(reduce_kernel, axis_name, half_rows), ou...]
    unnamed x13 -> x9, local copies, waits for them, and re-layouts: 311 us -> 26.8 us
    all_to_all x1 -> x0, other arithmetic: 228 us -> none  [local_step(): recv_rows = lax.all_to_all(send_rows, axis_name, 0, 0, tiled=True)]
    reduce_sum x3 -> x0, other arithmetic: 116 us -> none  [the longest x1 109 us: local_step(): grad_mat = jnp.sum(recv_rows.astype(jnp.float32), axis=0) / group_size]
    psum x1 -> x0, blocking collectives: 22.4 us -> none  [local_step(): lax.psum(jnp.sum(grad_mat * grad_mat), axis_name)]
  transfers between devices with their start and end apart: 3 -> 1, of which waited for: 2 -> 1; matrix products, arithmetic and copies ran while one was open for 15% -> 0% of each run, Pallas kernels for 0% -> 0%
where the time goes in v1:
time: 588 us; the launch traced here: 587 us
  Pallas kernels  335 us (57%)
  waiting for transfers between devices  179 us (30%)
  other arithmetic  29.8 us (5%)
  local copies, waits for them, and re-layouts  28.7 us (5%)
  between operations  14.8 us (3%)
    pallas_call x1, Pallas kernels, reduce_gradients(): pl.pallas_call(functools.partial(reduce_kernel, axis_name, half_rows), ou...  335 us
    all_gather x1, waiting for transfers between devices, local_step(): lax.all_gather(new_p_mat.astype(jnp.bfloat16), axis_name, tiled=True)  179 us
    convert_element_type x1, other arithmetic, local_step(): new_p_mat.astype(jnp.bfloat16)  27.3 us
    unnamed x9, local copies, waits for them, and re-layouts  26.8 us
  transfers between devices with their start and end apart: 1, of which 1 were waited for; matrix products, arithmetic and copies ran while one was open for 0% of the time, Pallas kernels for 0%

profile of v1, /device:TPU:0, one launch (start us, length us, event | category | flops | bytes accessed | tf_op | source)
XLA Modules:
  0.0 587.3 jit_solution(17421985999137498192)
XLA Ops:
  7.2 0.0 all-gather.2.cloned.1.call-start
  7.2 1.2 reduce
  8.4 0.6 pad_bitcast_fusion.gv_ref
  9.0 334.6 %reduce_gradients.1 = (f32[19200,128]{1,0:T(8,128)}, f32[192,128]{1,0:T(8,128)}, f32[8,128]{1,0:T(8,128)}, bf16[12,9600,128]{2,1,0:T(8,128)(2,1)}) custom-call(bf16[1,19660800]{1,0:T(2,128)(2,1)} %g_ref.1, bf16[192,128]{1,0:T(8,128)(2,1)} %pad_bitcast_fusion.gv_ref), custom_call_target="tpu_custom_call" | custom-call | tf_op jit(solution)/shard_map/reduce_gradients/pallas_call | solution.py:287
  343.7 1.3 slice.7
  345.6 0.0 copy-start
  345.6 0.0 copy-start.1
  345.6 0.0 copy-start.2
  345.6 0.0 copy-start.3
  345.6 27.3 %fusion.4 = (bf16[2457600]{0:T(1024)(128)(2,1)}, f32[2457600]{0:T(1024)}, f32[2457600]{0:T(1024)}, f32[2457600]{0:T(1024)}) fusion(f32[2457600]{0:T(1024)} %param.11, f32[]{:T(128)S(6)} %copy.17, f32[19200,128]{1,0:T(8,128)} %get-tuple-element.10, f32[]{:T(128)} %bitcast.1, f32[2457600]{0:T(1024)} %param.12, f32[2457600]{0:T(1024)} %param.13), kind=kLoop, calls=%fused_computation.12 | loop fusion | flops 41779200 | bytes 73728008 | tf_op jit(solution)/shard_map/convert_element_type | solution.py:342
  372.9 0.0 all-gather.2.cloned.1.call-update
  372.9 0.0 copy-done
  373.0 0.0 copy-done.1
  373.0 0.0 copy-done.2
  373.0 0.0 copy-done.3
  373.0 1.4 multiply_subtract_fusion.1
  374.4 179.3 %all-gather.2.cloned.1.call-done = bf16[19660800]{0:T(1024)(128)(2,1)} async-done(((bf16[2457600]{0:T(1024)(128)(2,1)}), bf16[19660800]{0:T(1024)(128)(2,1)}) %all-gather.2.cloned.1.call-update) | async-done | bytes 39321616 | tf_op jit(solution)/shard_map/all_gather | solution.py:342
  553.7 26.8 %copy.18 = bf16[19660800]{0:T(1024)(128)(2,1)} copy(bf16[19660800]{0:T(1024)(128)(2,1)} %all-gather.2.cloned.1.call-done) | data formatting | bytes 78643200
Async XLA Ops:
  7.2 546.5 %all-gather.2.cloned.1.call-start = ((), (), s32[]{:S(2)}) async-start(), calls=%async_computation | async-start | bytes 44236800 | tf_op jit(solution)/shard_map/all_gather | solution.py:342
  345.6 27.4 %copy-start = (f32[24320]{0:T(1024)S(1)}, f32[24320]{0:T(1024)}, u32[]{:S(2)}) copy-start(f32[24320]{0:T(1024)} %param.14) | copy-start | bytes 291844
  345.6 27.4 %copy-start.1 = (f32[24320]{0:T(1024)S(1)}, f32[24320]{0:T(1024)}, u32[]{:S(2)}) copy-start(f32[24320]{0:T(1024)} %param.15) | copy-start | bytes 291844
  345.6 27.4 %copy-start.2 = (f32[24320]{0:T(1024)S(1)}, f32[24320]{0:T(1024)}, u32[]{:S(2)}) copy-start(f32[24320]{0:T(1024)} %param.16) | copy-start | bytes 291844
  345.6 27.4 %copy-start.3 = (f32[192,128]{1,0:T(8,128)S(1)}, f32[192,128]{1,0:T(8,128)}, u32[]{:S(2)}) copy-start(f32[192,128]{1,0:T(8,128)} %get-tuple-element.12) | copy-start | bytes 294916
Sparse Core Ops, SparseCore 0:
  373.1 180.5 all-gather.1

commit v2 on v1

--- a/solution.py
+++ b/solution.py
@@ -6,6 +6,7 @@
 from jax.experimental import pallas as pl
 from jax.experimental.pallas import tpu as pltpu
 from jax.sharding import PartitionSpec as P
+
 
 STEP = 10
 ADAM_BETA1 = 0.9
@@ -22,6 +23,11 @@
 DEVICES = 8
 CHUNKS = 10
 BLOCK = 96
+ADAM_ROWS = 480
+SIZES = (1920, 7680, 7680, 1920)
+NEAR_GROUPS = ((0, 1), (2,), (3,))
+FAR_GROUPS = ((1, 2), (0, 3))
+VMEM_ALL = 67043328
 
 
 def adam_update(grad_vals, param_vals, moment_one, moment_two, learn_rate, decay_rate):
@@ -41,9 +47,9 @@
     return me, core, x, y, dev
 
 
-def reduce_kernel(axis_name, half_rows, g_ref, gv_ref, gsum_ref, vsum_ref, clip_ref, stage_ref,
-                  first, own_first, direct, own_direct, fsum, psum, raw, packed, vrecv, nsend, nrecv,
-                  raw_sem, pack_sem, first_recv, direct_recv, psum_recv, send_sem, fsum_send,
+def reduce_kernel(axis_name, half_rows, g_ref, gv_raw_ref, gsum_ref, vsum_ref, clip_ref, stage_ref,
+                  first, own_first, direct, own_direct, fsum, psum, raw, packed, vraw, gv_ref, vrecv, nsend, nrecv,
+                  vraw_sem, raw_sem, pack_sem, first_recv, direct_recv, psum_recv, send_sem, fsum_send,
                   vec_send, vec_recv, nrm_send, nrm_recv, out_sem):
     me, core, x, y, dev = places(axis_name)
     sib = dev(y, x, 1 - core)
@@ -111,10 +117,16 @@
 
         lax.fori_loop(0, rows // BLOCK, body, 0)
 
+    vec_size, vec_rows = gv_raw_ref.shape[1], gv_ref.shape[0]
+    vec_load = pltpu.make_async_copy(gv_raw_ref, vraw.at[:, pl.ds(0, vec_size)], vraw_sem)
+    vec_load.start()
     for h in range(8):
         load_raw(first_plan, h, 0).start()
-
-    vrecv[me] = gv_ref[...]
+    vraw[:, vec_size:] = jnp.zeros((1, vec_rows * LANES - vec_size), jnp.bfloat16)
+    vec_load.wait()
+    vec_mine = vraw[...].astype(jnp.float32).reshape(vec_rows, LANES).astype(jnp.bfloat16)
+    gv_ref[...] = vec_mine
+    vrecv[me] = vec_mine
 
     barrier = pltpu.get_barrier_semaphore()
     for o in range(1, DEVICES):
@@ -277,10 +289,10 @@
         nrm_copy(o).wait_send()
 
 
-def reduce_gradients(axis_name, g_mat, g_vec_rows):
+def reduce_gradients(axis_name, g_mat, g_vec):
     half_rows = g_mat.shape[1] // (2 * DEVICES * LANES)
     rows = half_rows // CHUNKS
-    vec_rows = g_vec_rows.shape[0]
+    vec_rows = -(-g_vec.shape[1] // (16 * LANES)) * 16
     bf16, f32 = jnp.bfloat16, jnp.float32
     dma = pltpu.SemaphoreType.DMA
     hbm, vmem = pl.BlockSpec(memory_space=pltpu.HBM), pl.BlockSpec(memory_space=pltpu.VMEM)
@@ -292,7 +304,7 @@
             jax.ShapeDtypeStruct((8, LANES), f32),
             jax.ShapeDtypeStruct((12, half_rows, LANES), bf16),
         ),
-        in_specs=[hbm, vmem],
+        in_specs=[hbm, hbm],
         out_specs=(hbm, vmem, vmem, hbm),
         scratch_shapes=[
             pltpu.VMEM((2, 3, half_rows, LANES), bf16),
@@ -303,9 +315,12 @@
             pltpu.VMEM((2, half_rows, LANES), f32),
             pltpu.VMEM((8, 1, rows * LANES), bf16),
             pltpu.VMEM((6, rows, LANES), bf16),
+            pltpu.VMEM((1, vec_rows * LANES), bf16),
+            pltpu.VMEM((vec_rows, LANES), bf16),
             pltpu.VMEM((DEVICES, vec_rows, LANES), bf16),
             pltpu.VMEM((8, LANES), f32),
             pltpu.VMEM((DEVICES, 8, LANES), f32),
+            dma,
             dma((8,)),
             dma((6,)),
             dma((2, 3, CHUNKS)),
@@ -320,27 +335,125 @@
             dma((2, CHUNKS)),
         ],
         compiler_params=pltpu.CompilerParams(
-            collective_id=0, has_side_effects=True, vmem_limit_bytes=67043328
+            collective_id=0, has_side_effects=True, vmem_limit_bytes=VMEM_ALL
         ),
         name="reduce_gradients",
-    )(g_mat, g_vec_rows)
+    )(g_mat, g_vec)
+
+
+def adam_kernel(lr_ref, clip_ref, g_ref, p_ref, m_ref, v_ref, *refs):
+    new_p_ref, new_m_ref, new_v_ref, narrow_ref = refs[-4:]
+    grad = g_ref[...] * clip_ref[0:1, :]
+    new_p, new_m, new_v = adam_update(grad, p_ref[...], m_ref[...], v_ref[...], lr_ref[0], WEIGHT_DECAY)
+    new_p_ref[...] = new_p
+    new_m_ref[...] = new_m
+    new_v_ref[...] = new_v
+    narrow_ref[...] = new_p.astype(jnp.bfloat16)
+
+
+def adam_chunk(start, size, learn_rate, clip, grad, params, state):
+    rows = grad.shape[0]
+    here = pl.BlockSpec((ADAM_ROWS, LANES), lambda i: (start // ADAM_ROWS + i, 0))
+    kept = pl.BlockSpec(memory_space=pltpu.HBM)
+    whole = jax.ShapeDtypeStruct((rows, LANES), jnp.float32)
+    return pl.pallas_call(
+        adam_kernel,
+        grid=(size // ADAM_ROWS,),
+        out_shape=(whole, whole, whole, jax.ShapeDtypeStruct((size, LANES), jnp.bfloat16)),
+        in_specs=[pl.BlockSpec(memory_space=pltpu.SMEM), pl.BlockSpec((8, LANES), lambda i: (0, 0)), here, here, here, here]
+        + [kept] * len(state),
+        out_specs=(here, here, here, pl.BlockSpec((ADAM_ROWS, LANES), lambda i: (i, 0))),
+        input_output_aliases={6 + k: k for k in range(len(state))},
+        cost_estimate=pl.CostEstimate(flops=size * LANES * 60, bytes_accessed=size * LANES * 30, transcendentals=0),
+        compiler_params=pltpu.CompilerParams(vmem_limit_bytes=VMEM_ALL),
+    )(learn_rate, clip, grad, *params, *state)
+
+
+def place_kernel(axis_name, offsets, piece_rows, *refs):
+    count = len(offsets)
+    sources, out_ref, buffers, sems = refs[-2 * count - 3 : -count - 3], refs[-count - 3], refs[-count - 2 : -2], refs[-2:]
+    _, core, x, y, dev = places(axis_name)
+    owners = {"me": dev(y, x, core), "sib": dev(y, x, 1 - core),
+              "x": dev(y, 1 - x, core), "x_sib": dev(y, 1 - x, 1 - core),
+              "y": dev(1 - y, x, core), "y_sib": dev(1 - y, x, 1 - core),
+              "d": dev(1 - y, 1 - x, core), "d_sib": dev(1 - y, 1 - x, 1 - core)}
+    loads, stores = [], []
+    for k, (who, start) in enumerate(offsets):
+        size = sources[k].shape[0]
+        at = pl.multiple_of(owners[who] * piece_rows + start, 16)
+        loads.append(pltpu.make_async_copy(sources[k], buffers[k], sems[0].at[k]))
+        stores.append(pltpu.make_async_copy(buffers[k], out_ref.at[pl.ds(at, size)], sems[1].at[k]))
+    for load in loads:
+        load.start()
+    for load, store in zip(loads, stores):
+        load.wait()
+        store.start()
+    for store in stores:
+        store.wait()
+
+
+def place(axis_name, piece_rows, full, items):
+    hbm = pl.BlockSpec(memory_space=pltpu.HBM)
+    sources = [source for _, _, source in items]
+    moved = sum(source.shape[0] for source in sources)
+    started = () if full is None else (full,)
+    return pl.pallas_call(
+        functools.partial(place_kernel, axis_name, tuple((who, start) for who, start, _ in items), piece_rows),
+        out_shape=jax.ShapeDtypeStruct((DEVICES * piece_rows, LANES), jnp.bfloat16),
+        in_specs=[hbm] * (len(started) + len(sources)),
+        out_specs=hbm,
+        input_output_aliases={0: 0} if started else {},
+        scratch_shapes=[pltpu.VMEM(source.shape, jnp.bfloat16) for source in sources]
+        + [pltpu.SemaphoreType.DMA((len(sources),))] * 2,
+        cost_estimate=pl.CostEstimate(flops=moved * LANES * 15, bytes_accessed=moved * LANES * 4, transcendentals=0),
+        compiler_params=pltpu.CompilerParams(vmem_limit_bytes=VMEM_ALL),
+    )(*started, *sources)
 
 
 def solution(mesh):
     axis_name = mesh.axis_names[0]
+    to_sib = [(d, 4 * (d // 4) + 2 * (d // 2 % 2) + (1 - d % 2)) for d in range(DEVICES)]
+    to_x = [(d, 4 * (d // 4) + 2 * (1 - d // 2 % 2) + d % 2) for d in range(DEVICES)]
+    to_y = [(d, 4 * (1 - d // 4) + 2 * (d // 2 % 2) + d % 2) for d in range(DEVICES)]
+
+    def move(array, pairs):
+        return lax.ppermute(array, axis_name, pairs)
 
     def local_step(g_mat, g_vec, p_mat, m_mat, v_mat, p_vec, m_vec, v_vec, learn_rate):
         vec_size = g_vec.shape[1]
-        vec_rows = -(-vec_size // (16 * LANES)) * 16
-        g_vec_rows = jnp.pad(g_vec[0], (0, vec_rows * LANES - vec_size)).reshape(vec_rows, LANES)
-        grad_mat, grad_vec, clip, _ = reduce_gradients(axis_name, g_mat, g_vec_rows)
-        clip_scale = clip[0, 0]
-        grad_mat = grad_mat.reshape(-1)
+        grad_mat, grad_vec, clip, _ = reduce_gradients(axis_name, g_mat, g_vec)
+        piece_rows = grad_mat.shape[0]
+        params = [array.reshape(piece_rows, LANES) for array in (p_mat, m_mat, v_mat)]
+        rate = learn_rate.reshape(1)
+
+        state, starts, own = (), [], []
+        for size in SIZES:
+            starts.append(sum(SIZES[: len(starts)]))
+            *state, narrow = adam_chunk(starts[-1], size, rate, clip, grad_mat, params, state)
+            own.append(narrow)
+
+        sib, from_x, from_y = [], [], []
+        for chunk in own:
+            from_x.append(move(chunk, to_x))
+            from_y.append(move(chunk, to_y))
+            sib.append(move(chunk, to_sib))
+        near, far = [], []
+        for j, start in enumerate(starts):
+            diag = move(from_y[j], to_x) if j % 2 == 0 else move(from_x[j], to_y)
+            near.append([("me", start, own[j]), ("sib", start, sib[j]),
+                         ("x", start, from_x[j]), ("x_sib", start, move(from_x[j], to_sib)),
+                         ("y", start, from_y[j]), ("y_sib", start, move(from_y[j], to_sib))])
+            far.append([("d", start, diag), ("d_sib", start, move(diag, to_sib))])
+        full = None
+        for group in NEAR_GROUPS:
+            full = place(axis_name, piece_rows, full, sum((near[j] for j in group), []))
+        for group in FAR_GROUPS:
+            full = place(axis_name, piece_rows, full, sum((far[j] for j in group), []))
+
         grad_vec = grad_vec.reshape(-1)[:vec_size]
-        new_p_mat, new_m_mat, new_v_mat = adam_update(grad_mat * clip_scale, p_mat, m_mat, v_mat, learn_rate, WEIGHT_DECAY)
-        new_p_vec, new_m_vec, new_v_vec = adam_update(grad_vec * clip_scale, p_vec, m_vec, v_vec, learn_rate, 0.0)
-        full_params = lax.all_gather(new_p_mat.astype(jnp.bfloat16), axis_name, tiled=True)
-        return new_p_mat, new_m_mat, new_v_mat, new_p_vec, new_m_vec, new_v_vec, full_params
+        new_p_vec, new_m_vec, new_v_vec = adam_update(grad_vec * clip[0, 0], p_vec, m_vec, v_vec, learn_rate, 0.0)
+        new_p, new_m, new_v = (array.reshape(-1) for array in state)
+        return new_p, new_m, new_v, new_p_vec, new_m_vec, new_v_vec, full.reshape(-1)
 
     return jax.shard_map(
         local_step,

time: 588 us -> 623 us (1.060)
  Pallas kernels: 335 us -> 411 us
  other arithmetic: 29.8 us -> 2.4 us
  local copies, waits for them, and re-layouts: 28.7 us -> 3.86 us
  starting transfers between devices: 0.04 us -> 14.3 us
  between operations: 14.8 us -> 1.43 us
  waiting for transfers between devices: 179 us -> 189 us
    ppermute x0 -> x28, waiting for transfers between devices: none -> 189 us  [move(): return lax.ppermute(array, axis_name, pairs)]
    all_gather x1 -> x0, waiting for transfers between devices: 179 us -> none  [local_step(): lax.all_gather(new_p_mat.astype(jnp.bfloat16), axis_name, tiled=True)]
    pallas_call x0 -> x9, Pallas kernels: none -> 76 us  [the longest x4 44.3 us: adam_chunk(): pl.pallas_call(adam_kernel, grid=(size // ADAM_ROWS,), out_shape=(whole,...]
    convert_element_type x1 -> x0, other arithmetic: 27.3 us -> none  [local_step(): new_p_mat.astype(jnp.bfloat16)]
    unnamed x9 -> x28, local copies, waits for them, and re-layouts: 26.8 us -> 2.61 us
    ppermute x0 -> x28, starting transfers between devices: none -> 14.3 us  [move(): return lax.ppermute(array, axis_name, pairs)]
  transfers between devices with their start and end apart: 1 -> 28, of which waited for: 1 -> 9; matrix products, arithmetic and copies ran while one was open for 0% -> 1% of each run, Pallas kernels for 0% -> 11%
where the time goes in v2:
time: 623 us; the launch traced here: 621 us
  Pallas kernels  411 us (66%)
  waiting for transfers between devices  189 us (30%)
  starting transfers between devices  14.3 us (2%)
    pallas_call x1, Pallas kernels, reduce_gradients(): pl.pallas_call(functools.partial(reduce_kernel, axis_name, half_rows), ou...  335 us
    ppermute x28, waiting for transfers between devices, move(): return lax.ppermute(array, axis_name, pairs)  189 us
    pallas_call x4, Pallas kernels, adam_chunk(): pl.pallas_call(adam_kernel, grid=(size // ADAM_ROWS,), out_shape=(whole,...  44.3 us
    pallas_call x5, Pallas kernels, place(): pl.pallas_call(functools.partial(place_kernel, axis_name, tuple(((who, st...  31.7 us
    ppermute x28, starting transfers between devices, move(): return lax.ppermute(array, axis_name, pairs)  14.3 us
  transfers between devices with their start and end apart: 28, of which 9 were waited for; matrix products, arithmetic and copies ran while one was open for 1% of the time, Pallas kernels for 11%

profile of v2, /device:TPU:0, one launch (start us, length us, event | category | flops | bytes accessed | tf_op | source)
XLA Modules:
  0.0 621.5 jit_solution(1392612078483079236)
XLA Ops:
  1.3 334.8 %reduce_gradients.1 = (f32[19200,128]{1,0:T(8,128)}, f32[192,128]{1,0:T(8,128)}, f32[8,128]{1,0:T(8,128)}, bf16[12,9600,128]{2,1,0:T(8,128)(2,1)}) custom-call(bf16[1,19660800]{1,0:T(2,128)(2,1)} %g_ref.1, bf16[1,24320]{1,0:T(2,128)(2,1)} %gv_raw_ref.1), custom_call_target="tpu_custom_call" | custom-call | tf_op jit(solution)/shard_map/reduce_gradients/pallas_call | solution.py:299
  336.1 4.8 shard_map.144
  340.9 0.1 collective-permute-start
  341.0 1.1 collective-permute-start.1
  342.1 0.9 collective-permute-start.3
  343.0 17.3 %shard_map.145 = (f32[19200,128]{1,0:T(8,128)}, f32[19200,128]{1,0:T(8,128)}, f32[19200,128]{1,0:T(8,128)}, bf16[7680,128]{1,0:T(8,128)(2,1)}) custom-call(f32[1]{0:T(128)} %bitcast.17.lr_ref, f32[8,128]{1,0:T(8,128)} %get-tuple-element.26.clip_ref, ...), custom_call_target="tpu_custom_call", output_to_operand_aliasing={{0}: (6, {}), {1}: (7, {}), {2}: (8, {})} | custom-call | flops 58982400 | bytes 29491200 | tf_op jit(solution)/shard_map/pallas_call | solution.py:359
  360.4 17.3 %shard_map.146 = (f32[19200,128]{1,0:T(8,128)}, f32[19200,128]{1,0:T(8,128)}, f32[19200,128]{1,0:T(8,128)}, bf16[7680,128]{1,0:T(8,128)(2,1)}) custom-call(f32[1]{0:T(128)} %bitcast.18.lr_ref, f32[8,128]{1,0:T(8,128)} %get-tuple-element.26.clip_ref, ...), custom_call_target="tpu_custom_call", output_to_operand_aliasing={{0}: (6, {}), {1}: (7, {}), {2}: (8, {})} | custom-call | flops 58982400 | bytes 29491200 | tf_op jit(solution)/shard_map/pallas_call | solution.py:359
  377.6 4.8 shard_map.147
  382.5 1.4 collective-permute-start.16
  383.9 0.0 collective-permute-done.refs_1_
  383.9 0.7 collective-permute-start.18
  384.5 0.0 collective-permute-done.3.refs_4_
  384.5 1.2 collective-permute-start.6
  385.7 0.2 collective-permute-start.2
  385.9 10.9 %collective-permute-done.16.refs_3_ = bf16[1920,128]{1,0:T(8,128)(2,1)S(1)} collective-permute-done((bf16[1920,128]{1,0:T(8,128)(2,1)}, bf16[1920,128]{1,0:T(8,128)(2,1)S(1)}, u32[]{:S(2)}, u32[]{:S(2)}) %collective-permute-start.16) | collective-permute-done | bytes 491552 | tf_op jit(solution)/shard_map/ppermute | solution.py:420
  396.8 0.7 collective-permute-done.18.refs_5_
  397.5 0.0 collective-permute-start.17
  397.5 0.9 collective-permute-start.8
  398.5 0.4 collective-permute-done.4.refs_5_
  398.9 1.1 collective-permute-start.13
  400.0 0.9 collective-permute-start.24
  401.0 48.1 %collective-permute-done.24.refs_1_ = bf16[1920,128]{1,0:T(8,128)(2,1)} collective-permute-done((bf16[1920,128]{1,0:T(8,128)(2,1)}, bf16[1920,128]{1,0:T(8,128)(2,1)}, u32[]{:S(2)}, u32[]{:S(2)}) %collective-permute-start.24) | collective-permute-done | bytes 491552 | tf_op jit(solution)/shard_map/ppermute | solution.py:420
  449.1 1.1 collective-permute-start.26
  450.2 45.5 %collective-permute-done.26.refs_3_ = bf16[1920,128]{1,0:T(8,128)(2,1)} collective-permute-done((bf16[1920,128]{1,0:T(8,128)(2,1)S(1)}, bf16[1920,128]{1,0:T(8,128)(2,1)}, u32[]{:S(2)}, u32[]{:S(2)}) %collective-permute-start.26) | collective-permute-done | bytes 491552 | tf_op jit(solution)/shard_map/ppermute | solution.py:420
  495.7 0.7 collective-permute-start.11
  496.5 0.2 collective-permute-start.7
  496.7 1.1 copy-done
  497.8 1.1 collective-permute-start.20
  498.9 0.9 collective-permute-start.22
  499.7 0.2 collective-permute-done.10.refs_2_
  499.9 0.1 collective-permute-start.9
  500.1 41.6 %collective-permute-done.11.refs_3_ = bf16[7680,128]{1,0:T(8,128)(2,1)S(1)} collective-permute-done((bf16[7680,128]{1,0:T(8,128)(2,1)}, bf16[7680,128]{1,0:T(8,128)(2,1)S(1)}, u32[]{:S(2)}, u32[]{:S(2)}) %collective-permute-start.11) | collective-permute-done | bytes 1966112 | tf_op jit(solution)/shard_map/ppermute | solution.py:420
  541.7 0.5 collective-permute-start.14
  542.2 0.6 collective-permute-done.20.refs_1_
  542.8 40.6 %collective-permute-done.22.refs_3_ = bf16[7680,128]{1,0:T(8,128)(2,1)} collective-permute-done((bf16[7680,128]{1,0:T(8,128)(2,1)S(1)}, bf16[7680,128]{1,0:T(8,128)(2,1)}, u32[]{:S(2)}, u32[]{:S(2)}) %collective-permute-start.22) | collective-permute-done | bytes 1966112 | tf_op jit(solution)/shard_map/ppermute | solution.py:420
  583.4 1.3 slice.8
  584.7 0.5 collective-permute-start.19
  585.2 0.1 collective-permute-start.25
  585.3 0.5 collective-permute-start.27
  585.8 0.2 copy-done.6
  586.0 0.6 copy-done.7
  586.6 0.7 copy-done.8
  587.3 2.4 multiply_subtract_fusion
  589.7 11.2 %shard_map.148.refs_0_ = bf16[153600,128]{1,0:T(8,128)(2,1)} custom-call(bf16[1920,128]{1,0:T(8,128)(2,1)} %get-tuple-element.41.refs_0_, bf16[1920,128]{1,0:T(8,128)(2,1)} %collective-permute-done.refs_1_, bf16[1920,128]{1,0:T(8,128)(2,1)} %collective-permute-done.1.refs_2_, bf16[1920,128]{1,0:T(8,128)(2,1)} %copy-done.12, ...), custom_call_target="tpu_custom_call" | custom-call | flops 110592000 | bytes 29491200 | tf_op jit(solution)/shard_map/pallas_call | solution.py:400
  600.9 8.8 %shard_map.149.refs_0_ = bf16[153600,128]{1,0:T(8,128)(2,1)} custom-call(bf16[153600,128]{1,0:T(8,128)(2,1)} %shard_map.148.refs_0_, bf16[7680,128]{1,0:T(8,128)(2,1)} %get-tuple-element.43.refs_1_, bf16[7680,128]{1,0:T(8,128)(2,1)} %copy-done.3, bf16[7680,128]{1,0:T(8,128)(2,1)} %copy-done.4, ...), custom_call_target="tpu_custom_call", output_to_operand_aliasing={{}: (0, {})} | custom-call | flops 88473600 | bytes 23592960 | tf_op jit(solution)/shard_map/pallas_call | solution.py:400
  609.8 2.7 shard_map.150.refs_0_
  612.5 6.5 %shard_map.151.refs_0_ = bf16[153600,128]{1,0:T(8,128)(2,1)} custom-call(bf16[153600,128]{1,0:T(8,128)(2,1)} %shard_map.150.refs_0_, bf16[7680,128]{1,0:T(8,128)(2,1)} %collective-permute-done.20.refs_1_, bf16[7680,128]{1,0:T(8,128)(2,1)} %collective-permute-done.21.refs_2_, ...), custom_call_target="tpu_custom_call", output_to_operand_aliasing={{}: (0, {})} | custom-call | flops 58982400 | bytes 15728640 | tf_op jit(solution)/shard_map/pallas_call | solution.py:400
  619.1 2.4 shard_map.152
  (48 shorter events, 0.1 us)
Async XLA Ops:
  340.9 43.0 %collective-permute-start = (bf16[1920,128]{1,0:T(8,128)(2,1)}, bf16[1920,128]{1,0:T(8,128)(2,1)}, u32[]{:S(2)}, u32[]{:S(2)}) collective-permute-start(bf16[1920,128]{1,0:T(8,128)(2,1)} %get-tuple-element.41.refs_0_), channel_id=1, source_target_pairs={{0,1},{1,0},{2,3},{3,2},{4,5},{5,4},{6,7},{7,6}} | collective-permute-start | bytes 1474568 | tf_op jit(solution)/shard_map/ppermute | solution.py:420
  341.0 43.5 %collective-permute-start.1 = (bf16[1920,128]{1,0:T(8,128)(2,1)}, bf16[1920,128]{1,0:T(8,128)(2,1)}, u32[]{:S(2)}, u32[]{:S(2)}) collective-permute-start(bf16[1920,128]{1,0:T(8,128)(2,1)} %get-tuple-element.41.refs_0_), channel_id=1, source_target_pairs={{0,2},{1,3},{2,0},{3,1},{4,6},{5,7},{6,4},{7,5}} | collective-permute-start | bytes 1474568 | tf_op jit(solution)/shard_map/ppermute | solution.py:420
  342.1 42.4 %collective-permute-start.3 = (bf16[1920,128]{1,0:T(8,128)(2,1)}, bf16[1920,128]{1,0:T(8,128)(2,1)}, u32[]{:S(2)}, u32[]{:S(2)}) collective-permute-start(bf16[1920,128]{1,0:T(8,128)(2,1)} %get-tuple-element.41.refs_0_), channel_id=1, source_target_pairs={{0,4},{1,5},{2,6},{3,7},{4,0},{5,1},{6,2},{7,3}} | collective-permute-start | bytes 1474568 | tf_op jit(solution)/shard_map/ppermute | solution.py:420
  382.5 3.2 collective-permute-start.15
  382.5 14.3 %collective-permute-start.16 = (bf16[1920,128]{1,0:T(8,128)(2,1)}, bf16[1920,128]{1,0:T(8,128)(2,1)S(1)}, u32[]{:S(2)}, u32[]{:S(2)}) collective-permute-start(bf16[1920,128]{1,0:T(8,128)(2,1)} %get-tuple-element.44.refs_1_), channel_id=1, source_target_pairs={{0,2},{1,3},{2,0},{3,1},{4,6},{5,7},{6,4},{7,5}} | collective-permute-start | bytes 1474568 | tf_op jit(solution)/shard_map/ppermute | solution.py:420
  383.9 13.6 %collective-permute-start.18 = (bf16[1920,128]{1,0:T(8,128)(2,1)}, bf16[1920,128]{1,0:T(8,128)(2,1)}, u32[]{:S(2)}, u32[]{:S(2)}) collective-permute-start(bf16[1920,128]{1,0:T(8,128)(2,1)} %get-tuple-element.44.refs_1_), channel_id=1, source_target_pairs={{0,4},{1,5},{2,6},{3,7},{4,0},{5,1},{6,2},{7,3}} | collective-permute-start | bytes 1474568 | tf_op jit(solution)/shard_map/ppermute | solution.py:420
  384.5 111.2 %collective-permute-start.5 = (bf16[7680,128]{1,0:T(8,128)(2,1)}, bf16[7680,128]{1,0:T(8,128)(2,1)}, u32[]{:S(2)}, u32[]{:S(2)}) collective-permute-start(bf16[7680,128]{1,0:T(8,128)(2,1)} %get-tuple-element.42.refs_6_), channel_id=1, source_target_pairs={{0,1},{1,0},{2,3},{3,2},{4,5},{5,4},{6,7},{7,6}} | collective-permute-start | bytes 5898248 | tf_op jit(solution)/shard_map/ppermute | solution.py:420
  384.5 111.9 %collective-permute-start.6 = (bf16[7680,128]{1,0:T(8,128)(2,1)}, bf16[7680,128]{1,0:T(8,128)(2,1)S(1)}, u32[]{:S(2)}, u32[]{:S(2)}) collective-permute-start(bf16[7680,128]{1,0:T(8,128)(2,1)} %get-tuple-element.42.refs_6_), channel_id=1, source_target_pairs={{0,2},{1,3},{2,0},{3,1},{4,6},{5,7},{6,4},{7,5}} | collective-permute-start | bytes 5898248 | tf_op jit(solution)/shard_map/ppermute | solution.py:420
  385.7 64.5 %copy-start.9 = (bf16[1920,128]{1,0:T(8,128)(2,1)}, bf16[1920,128]{1,0:T(8,128)(2,1)S(1)}, u32[]{:S(2)}) copy-start(bf16[1920,128]{1,0:T(8,128)(2,1)S(1)} %collective-permute-done.15.refs_2_) | copy-start | bytes 1474564
  385.7 11.8 %collective-permute-start.2 = (bf16[1920,128]{1,0:T(8,128)(2,1)}, bf16[1920,128]{1,0:T(8,128)(2,1)S(1)}, u32[]{:S(2)}, u32[]{:S(2)}) collective-permute-start(bf16[1920,128]{1,0:T(8,128)(2,1)} %collective-permute-done.1.refs_2_), channel_id=1, source_target_pairs={{0,1},{1,0},{2,3},{3,2},{4,5},{5,4},{6,7},{7,6}} | collective-permute-start | bytes 1474568 | tf_op jit(solution)/shard_map/ppermute | solution.py:420
  396.8 53.4 %copy-start.10 = (bf16[1920,128]{1,0:T(8,128)(2,1)}, bf16[1920,128]{1,0:T(8,128)(2,1)S(1)}, u32[]{:S(2)}) copy-start(bf16[1920,128]{1,0:T(8,128)(2,1)S(1)} %collective-permute-done.16.refs_3_) | copy-start | bytes 1474564
  396.8 2.1 collective-permute-start.4
  397.5 2.5 collective-permute-start.17
  397.5 52.7 %copy-start.12 = (bf16[1920,128]{1,0:T(8,128)(2,1)}, bf16[1920,128]{1,0:T(8,128)(2,1)S(1)}, u32[]{:S(2)}) copy-start(bf16[1920,128]{1,0:T(8,128)(2,1)S(1)} %collective-permute-done.2.refs_3_) | copy-start | bytes 1474564
  397.5 99.2 %collective-permute-start.8 = (bf16[7680,128]{1,0:T(8,128)(2,1)}, bf16[7680,128]{1,0:T(8,128)(2,1)S(1)}, u32[]{:S(2)}, u32[]{:S(2)}) collective-permute-start(bf16[7680,128]{1,0:T(8,128)(2,1)} %get-tuple-element.42.refs_6_), channel_id=1, source_target_pairs={{0,4},{1,5},{2,6},{3,7},{4,0},{5,1},{6,2},{7,3}} | collective-permute-start | bytes 5898248 | tf_op jit(solution)/shard_map/ppermute | solution.py:420
  398.9 97.5 %copy-start.13 = (bf16[1920,128]{1,0:T(8,128)(2,1)}, bf16[1920,128]{1,0:T(8,128)(2,1)S(1)}, u32[]{:S(2)}) copy-start(bf16[1920,128]{1,0:T(8,128)(2,1)S(1)} %collective-permute-done.4.refs_5_) | copy-start | bytes 1474564
  398.9 100.0 %collective-permute-start.13 = (bf16[7680,128]{1,0:T(8,128)(2,1)}, bf16[7680,128]{1,0:T(8,128)(2,1)S(1)}, u32[]{:S(2)}, u32[]{:S(2)}) collective-permute-start(bf16[7680,128]{1,0:T(8,128)(2,1)} %get-tuple-element.43.refs_1_), channel_id=1, source_target_pairs={{0,4},{1,5},{2,6},{3,7},{4,0},{5,1},{6,2},{7,3}} | collective-permute-start | bytes 5898248 | tf_op jit(solution)/shard_map/ppermute | solution.py:420
  400.0 50.2 %copy-start.11 = (bf16[1920,128]{1,0:T(8,128)(2,1)}, bf16[1920,128]{1,0:T(8,128)(2,1)S(1)}, u32[]{:S(2)}) copy-start(bf16[1920,128]{1,0:T(8,128)(2,1)S(1)} %collective-permute-done.17.refs_4_) | copy-start | bytes 1474564
  400.0 49.1 %collective-permute-start.24 = (bf16[1920,128]{1,0:T(8,128)(2,1)}, bf16[1920,128]{1,0:T(8,128)(2,1)}, u32[]{:S(2)}, u32[]{:S(2)}) collective-permute-start(bf16[1920,128]{1,0:T(8,128)(2,1)} %collective-permute-done.3.refs_4_), channel_id=1, source_target_pairs={{0,2},{1,3},{2,0},{3,1},{4,6},{5,7},{6,4},{7,5}} | collective-permute-start | bytes 1474568 | tf_op jit(solution)/shard_map/ppermute | solution.py:420
  449.1 46.6 %collective-permute-start.26 = (bf16[1920,128]{1,0:T(8,128)(2,1)S(1)}, bf16[1920,128]{1,0:T(8,128)(2,1)}, u32[]{:S(2)}, u32[]{:S(2)}) collective-permute-start(bf16[1920,128]{1,0:T(8,128)(2,1)S(1)} %collective-permute-done.16.refs_3_), channel_id=1, source_target_pairs={{0,4},{1,5},{2,6},{3,7},{4,0},{5,1},{6,2},{7,3}} | collective-permute-start | bytes 1474568 | tf_op jit(solution)/shard_map/ppermute | solution.py:420
  495.7 4.2 collective-permute-start.10
  495.7 45.9 %collective-permute-start.11 = (bf16[7680,128]{1,0:T(8,128)(2,1)}, bf16[7680,128]{1,0:T(8,128)(2,1)S(1)}, u32[]{:S(2)}, u32[]{:S(2)}) collective-permute-start(bf16[7680,128]{1,0:T(8,128)(2,1)} %get-tuple-element.43.refs_1_), channel_id=1, source_target_pairs={{0,2},{1,3},{2,0},{3,1},{4,6},{5,7},{6,4},{7,5}} | collective-permute-start | bytes 5898248 | tf_op jit(solution)/shard_map/ppermute | solution.py:420
  496.5 1.3 copy-start
  496.5 45.2 %collective-permute-start.7 = (bf16[7680,128]{1,0:T(8,128)(2,1)S(1)}, bf16[7680,128]{1,0:T(8,128)(2,1)S(1)}, u32[]{:S(2)}, u32[]{:S(2)}) collective-permute-start(bf16[7680,128]{1,0:T(8,128)(2,1)S(1)} %collective-permute-done.6.refs_8_), channel_id=1, source_target_pairs={{0,1},{1,0},{2,3},{3,2},{4,5},{5,4},{6,7},{7,6}} | collective-permute-start | bytes 5898248 | tf_op jit(solution)/shard_map/ppermute | solution.py:420
  497.8 45.1 %copy-start.1 = (bf16[7680,128]{1,0:T(8,128)(2,1)}, bf16[7680,128]{1,0:T(8,128)(2,1)S(1)}, u32[]{:S(2)}) copy-start(bf16[7680,128]{1,0:T(8,128)(2,1)S(1)} %collective-permute-done.8.refs_10_) | copy-start | bytes 5898244
  497.8 45.1 %collective-permute-start.20 = (bf16[7680,128]{1,0:T(8,128)(2,1)S(1)}, bf16[7680,128]{1,0:T(8,128)(2,1)}, u32[]{:S(2)}, u32[]{:S(2)}) collective-permute-start(bf16[7680,128]{1,0:T(8,128)(2,1)S(1)} %collective-permute-done.6.refs_8_), channel_id=1, source_target_pairs={{0,4},{1,5},{2,6},{3,7},{4,0},{5,1},{6,2},{7,3}} | collective-permute-start | bytes 5898248 | tf_op jit(solution)/shard_map/ppermute | solution.py:420
  498.9 85.8 %copy-start.2 = (bf16[7680,128]{1,0:T(8,128)(2,1)}, bf16[7680,128]{1,0:T(8,128)(2,1)S(1)}, u32[]{:S(2)}) copy-start(bf16[7680,128]{1,0:T(8,128)(2,1)S(1)} %collective-permute-done.13.refs_5_) | copy-start | bytes 5898244
  498.9 84.6 %collective-permute-start.22 = (bf16[7680,128]{1,0:T(8,128)(2,1)S(1)}, bf16[7680,128]{1,0:T(8,128)(2,1)}, u32[]{:S(2)}, u32[]{:S(2)}) collective-permute-start(bf16[7680,128]{1,0:T(8,128)(2,1)S(1)} %collective-permute-done.13.refs_5_), channel_id=1, source_target_pairs={{0,2},{1,3},{2,0},{3,1},{4,6},{5,7},{6,4},{7,5}} | collective-permute-start | bytes 5898248 | tf_op jit(solution)/shard_map/ppermute | solution.py:420
  499.9 83.5 %copy-start.3 = (bf16[7680,128]{1,0:T(8,128)(2,1)}, bf16[7680,128]{1,0:T(8,128)(2,1)S(1)}, u32[]{:S(2)}) copy-start(bf16[7680,128]{1,0:T(8,128)(2,1)S(1)} %collective-permute-done.10.refs_2_) | copy-start | bytes 5898244
  499.9 84.8 %collective-permute-start.9 = (bf16[7680,128]{1,0:T(8,128)(2,1)S(1)}, bf16[7680,128]{1,0:T(8,128)(2,1)S(1)}, u32[]{:S(2)}, u32[]{:S(2)}) collective-permute-start(bf16[7680,128]{1,0:T(8,128)(2,1)S(1)} %collective-permute-done.8.refs_10_), channel_id=1, source_target_pairs={{0,1},{1,0},{2,3},{3,2},{4,5},{5,4},{6,7},{7,6}} | collective-permute-start | bytes 5898248 | tf_op jit(solution)/shard_map/ppermute | solution.py:420
  541.7 43.6 %copy-start.4 = (bf16[7680,128]{1,0:T(8,128)(2,1)}, bf16[7680,128]{1,0:T(8,128)(2,1)S(1)}, u32[]{:S(2)}) copy-start(bf16[7680,128]{1,0:T(8,128)(2,1)S(1)} %collective-permute-done.11.refs_3_) | copy-start | bytes 5898244
  541.7 43.6 %collective-permute-start.12 = (bf16[7680,128]{1,0:T(8,128)(2,1)S(1)}, bf16[7680,128]{1,0:T(8,128)(2,1)S(1)}, u32[]{:S(2)}, u32[]{:S(2)}) collective-permute-start(bf16[7680,128]{1,0:T(8,128)(2,1)S(1)} %collective-permute-done.11.refs_3_), channel_id=1, source_target_pairs={{0,1},{1,0},{2,3},{3,2},{4,5},{5,4},{6,7},{7,6}} | collective-permute-start | bytes 5898248 | tf_op jit(solution)/shard_map/ppermute | solution.py:420
  541.7 41.8 %copy-start.5 = (bf16[7680,128]{1,0:T(8,128)(2,1)}, bf16[7680,128]{1,0:T(8,128)(2,1)S(1)}, u32[]{:S(2)}) copy-start(bf16[7680,128]{1,0:T(8,128)(2,1)S(1)} %collective-permute-done.7.refs_9_) | copy-start | bytes 5898244
  541.7 43.6 %collective-permute-start.14 = (bf16[7680,128]{1,0:T(8,128)(2,1)S(1)}, bf16[7680,128]{1,0:T(8,128)(2,1)S(1)}, u32[]{:S(2)}, u32[]{:S(2)}) collective-permute-start(bf16[7680,128]{1,0:T(8,128)(2,1)S(1)} %collective-permute-done.13.refs_5_), channel_id=1, source_target_pairs={{0,1},{1,0},{2,3},{3,2},{4,5},{5,4},{6,7},{7,6}} | collective-permute-start | bytes 5898248 | tf_op jit(solution)/shard_map/ppermute | solution.py:420
  542.8 69.7 %collective-permute-start.21 = (bf16[7680,128]{1,0:T(8,128)(2,1)}, bf16[7680,128]{1,0:T(8,128)(2,1)}, u32[]{:S(2)}, u32[]{:S(2)}) collective-permute-start(bf16[7680,128]{1,0:T(8,128)(2,1)} %collective-permute-done.20.refs_1_), channel_id=1, source_target_pairs={{0,1},{1,0},{2,3},{3,2},{4,5},{5,4},{6,7},{7,6}} | collective-permute-start | bytes 5898248 | tf_op jit(solution)/shard_map/ppermute | solution.py:420
  583.4 29.1 %collective-permute-start.23 = (bf16[7680,128]{1,0:T(8,128)(2,1)}, bf16[7680,128]{1,0:T(8,128)(2,1)}, u32[]{:S(2)}, u32[]{:S(2)}) collective-permute-start(bf16[7680,128]{1,0:T(8,128)(2,1)} %collective-permute-done.22.refs_3_), channel_id=1, source_target_pairs={{0,1},{1,0},{2,3},{3,2},{4,5},{5,4},{6,7},{7,6}} | collective-permute-start | bytes 5898248 | tf_op jit(solution)/shard_map/ppermute | solution.py:420
  584.7 1.3 copy-start.6
  584.7 25.1 %collective-permute-start.19 = (bf16[1920,128]{1,0:T(8,128)(2,1)}, bf16[1920,128]{1,0:T(8,128)(2,1)}, u32[]{:S(2)}, u32[]{:S(2)}) collective-permute-start(bf16[1920,128]{1,0:T(8,128)(2,1)} %collective-permute-done.18.refs_5_), channel_id=1, source_target_pairs={{0,1},{1,0},{2,3},{3,2},{4,5},{5,4},{6,7},{7,6}} | collective-permute-start | bytes 1474568 | tf_op jit(solution)/shard_map/ppermute | solution.py:420
  585.2 1.3 copy-start.7
  585.2 33.9 %collective-permute-start.25 = (bf16[1920,128]{1,0:T(8,128)(2,1)}, bf16[1920,128]{1,0:T(8,128)(2,1)}, u32[]{:S(2)}, u32[]{:S(2)}) collective-permute-start(bf16[1920,128]{1,0:T(8,128)(2,1)} %collective-permute-done.24.refs_1_), channel_id=1, source_target_pairs={{0,1},{1,0},{2,3},{3,2},{4,5},{5,4},{6,7},{7,6}} | collective-permute-start | bytes 1474568 | tf_op jit(solution)/shard_map/ppermute | solution.py:420
  585.3 2.0 copy-start.8
  585.3 33.8 %collective-permute-start.27 = (bf16[1920,128]{1,0:T(8,128)(2,1)}, bf16[1920,128]{1,0:T(8,128)(2,1)}, u32[]{:S(2)}, u32[]{:S(2)}) collective-permute-start(bf16[1920,128]{1,0:T(8,128)(2,1)} %collective-permute-done.26.refs_3_), channel_id=1, source_target_pairs={{0,1},{1,0},{2,3},{3,2},{4,5},{5,4},{6,7},{7,6}} | collective-permute-start | bytes 1474568 | tf_op jit(solution)/shard_map/ppermute | solution.py:420

commit v3 on v2

--- a/solution.py
+++ b/solution.py
@@ -24,16 +24,16 @@
 CHUNKS = 10
 BLOCK = 96
 ADAM_ROWS = 480
-SIZES = (1920, 7680, 7680, 1920)
-NEAR_GROUPS = ((0, 1), (2,), (3,))
-FAR_GROUPS = ((1, 2), (0, 3))
+SIZES = (1440, 2880, 5280, 5280, 2880, 1440)
+NEAR_GROUPS = ((0, 1), (2,), (3,), (4, 5))
+FAR_GROUPS = ((1, 2), (3, 4), (0, 5))
 VMEM_ALL = 67043328
 
 
 def adam_update(grad_vals, param_vals, moment_one, moment_two, learn_rate, decay_rate):
     new_one = ADAM_BETA1 * moment_one + (1.0 - ADAM_BETA1) * grad_vals
     new_two = ADAM_BETA2 * moment_two + (1.0 - ADAM_BETA2) * grad_vals * grad_vals
-    direction = (new_one / BIAS_ONE) / (jnp.sqrt(new_two / BIAS_TWO) + ADAM_EPS)
+    direction = (new_one * (1.0 / BIAS_ONE)) / (jnp.sqrt(new_two * (1.0 / BIAS_TWO)) + ADAM_EPS)
     return param_vals - learn_rate * (direction + decay_rate * param_vals), new_one, new_two
 
 
@@ -128,6 +128,38 @@
     gv_ref[...] = vec_mine
     vrecv[me] = vec_mine
 
+    def pack_all(phase, plan, next_plan, c):
+        for h in range(8):
+            load_raw(plan, h, c).wait()
+            pack(plan, h, c)
+
+            @pl.when(c + 1 < CHUNKS)
+            def _():
+                load_raw(plan, h, c + 1).start()
+
+            if next_plan is not None:
+                @pl.when(c + 1 >= CHUNKS)
+                def _():
+                    load_raw(next_plan, h, 0).start()
+
+            if 1 <= h <= 6:
+                to_stage(phase, h - 1, c).start()
+
+    def send_all(phase, plan, c):
+        for h in range(6):
+            to_stage(phase, h, c).wait()
+            send(phase, plan, h, c).start()
+
+    def step(phase, plan, next_plan):
+        def body(c, _):
+            pack_all(phase, plan, next_plan, c)
+            send_all(phase, plan, c)
+            return 0
+
+        return body
+
+    pack_all(0, first_plan, direct_plan, 0)
+
     barrier = pltpu.get_barrier_semaphore()
     for o in range(1, DEVICES):
         pl.semaphore_signal(barrier, inc=1, device_id=((me + o) % DEVICES,), device_id_type=MESH)
@@ -145,34 +177,9 @@
     for o in range(1, DEVICES):
         vec_copy(o).start()
 
-    def send_phase(phase, plan, next_plan):
-        def step(c, _):
-            for h in range(8):
-                load_raw(plan, h, c).wait()
-                pack(plan, h, c)
-                if next_plan is None:
-                    @pl.when(c + 1 < CHUNKS)
-                    def _():
-                        load_raw(plan, h, c + 1).start()
-                else:
-                    @pl.when(c + 1 < CHUNKS)
-                    def _():
-                        load_raw(plan, h, c + 1).start()
-
-                    @pl.when(c + 1 >= CHUNKS)
-                    def _():
-                        load_raw(next_plan, h, 0).start()
-                if 1 <= h <= 6:
-                    to_stage(phase, h - 1, c).start()
-            for h in range(6):
-                to_stage(phase, h, c).wait()
-                send(phase, plan, h, c).start()
-            return 0
-
-        lax.fori_loop(0, CHUNKS, step, 0)
-
-    send_phase(0, first_plan, direct_plan)
-    send_phase(1, direct_plan, None)
+    send_all(0, first_plan, 0)
+    lax.fori_loop(1, CHUNKS, step(0, first_plan, direct_plan), 0)
+    lax.fori_loop(0, CHUNKS, step(1, direct_plan, None), 0)
 
     def got(buf, sems, slot, c):
         at = buf.at[(*slot, pl.ds(pl.multiple_of(c * rows, rows), rows))]
@@ -341,29 +348,66 @@
     )(g_mat, g_vec)
 
 
-def adam_kernel(lr_ref, clip_ref, g_ref, p_ref, m_ref, v_ref, *refs):
-    new_p_ref, new_m_ref, new_v_ref, narrow_ref = refs[-4:]
-    grad = g_ref[...] * clip_ref[0:1, :]
-    new_p, new_m, new_v = adam_update(grad, p_ref[...], m_ref[...], v_ref[...], lr_ref[0], WEIGHT_DECAY)
-    new_p_ref[...] = new_p
-    new_m_ref[...] = new_m
-    new_v_ref[...] = new_v
-    narrow_ref[...] = new_p.astype(jnp.bfloat16)
+def adam_kernel(start, lr_ref, clip_ref, *refs):
+    inputs, outputs, (wide, narrow, load_sem, store_sem) = refs[:4], refs[-8:-4], refs[-4:]
+    count = narrow.shape[0] // ADAM_ROWS
+
+    def rows(i, base=0):
+        return pl.ds(pl.multiple_of(base + i * ADAM_ROWS, ADAM_ROWS), ADAM_ROWS)
+
+    def load(k, i):
+        return pltpu.make_async_copy(inputs[k].at[rows(i, start)], wide.at[k, rows(i)], load_sem.at[k, i])
+
+    def store(k, i):
+        if k == 3:
+            return pltpu.make_async_copy(narrow.at[rows(i)], outputs[3].at[rows(i)], store_sem.at[3, i])
+        return pltpu.make_async_copy(wide.at[k + 1, rows(i)], outputs[k].at[rows(i, start)], store_sem.at[k, i])
+
+    for i in range(count):
+        for k in range(4):
+            load(k, i).start()
+
+    def step(i, _):
+        for k in range(4):
+            load(k, i).wait()
+        at = rows(i)
+        grad = wide[0, at, :] * clip_ref[0:1, :]
+        new_p, new_m, new_v = adam_update(grad, wide[1, at, :], wide[2, at, :], wide[3, at, :], lr_ref[0], WEIGHT_DECAY)
+        wide[1, at, :] = new_p
+        wide[2, at, :] = new_m
+        wide[3, at, :] = new_v
+        narrow[at, :] = new_p.astype(jnp.bfloat16)
+
+        @pl.when(i > 0)
+        def _():
+            for k in (3, 0, 1, 2):
+                store(k, i - 1).start()
+
+        return 0
+
+    lax.fori_loop(0, count, step, 0)
+    for k in (3, 0, 1, 2):
+        store(k, count - 1).start()
+    for i in range(count):
+        for k in range(4):
+            store(k, i).wait()
 
 
 def adam_chunk(start, size, learn_rate, clip, grad, params, state):
-    rows = grad.shape[0]
-    here = pl.BlockSpec((ADAM_ROWS, LANES), lambda i: (start // ADAM_ROWS + i, 0))
-    kept = pl.BlockSpec(memory_space=pltpu.HBM)
-    whole = jax.ShapeDtypeStruct((rows, LANES), jnp.float32)
+    hbm = pl.BlockSpec(memory_space=pltpu.HBM)
+    whole = jax.ShapeDtypeStruct(grad.shape, jnp.float32)
     return pl.pallas_call(
-        adam_kernel,
-        grid=(size // ADAM_ROWS,),
+        functools.partial(adam_kernel, start),
         out_shape=(whole, whole, whole, jax.ShapeDtypeStruct((size, LANES), jnp.bfloat16)),
-        in_specs=[pl.BlockSpec(memory_space=pltpu.SMEM), pl.BlockSpec((8, LANES), lambda i: (0, 0)), here, here, here, here]
-        + [kept] * len(state),
-        out_specs=(here, here, here, pl.BlockSpec((ADAM_ROWS, LANES), lambda i: (i, 0))),
+        in_specs=[pl.BlockSpec(memory_space=pltpu.SMEM), pl.BlockSpec(memory_space=pltpu.VMEM)] + [hbm] * (4 + len(state)),
+        out_specs=(hbm, hbm, hbm, hbm),
         input_output_aliases={6 + k: k for k in range(len(state))},
+        scratch_shapes=[
+            pltpu.VMEM((4, size, LANES), jnp.float32),
+            pltpu.VMEM((size, LANES), jnp.bfloat16),
+            pltpu.SemaphoreType.DMA((4, size // ADAM_ROWS)),
+            pltpu.SemaphoreType.DMA((4, size // ADAM_ROWS)),
+        ],
         cost_estimate=pl.CostEstimate(flops=size * LANES * 60, bytes_accessed=size * LANES * 30, transcendentals=0),
         compiler_params=pltpu.CompilerParams(vmem_limit_bytes=VMEM_ALL),
     )(learn_rate, clip, grad, *params, *state)

time: 623 us -> 583 us (0.936)
  waiting for transfers between devices: 189 us -> 146 us
  starting transfers between devices: 14.3 us -> 21.8 us
    ppermute x28 -> x42, waiting for transfers between devices: 189 us -> 146 us  [move(): return lax.ppermute(array, axis_name, pairs)]
    ppermute x28 -> x42, starting transfers between devices: 14.3 us -> 21.8 us  [move(): return lax.ppermute(array, axis_name, pairs)]
    pallas_call x4 -> x6, Pallas kernels: 44.3 us -> 37.1 us  [adam_chunk(): pl.pallas_call(functools.partial(adam_kernel, start), out_shape=(whole, w...]
    pallas_call x5 -> x7, Pallas kernels: 31.7 us -> 33.4 us  [place(): pl.pallas_call(functools.partial(place_kernel, axis_name, tuple(((who, st...]
  transfers between devices with their start and end apart: 28 -> 42, of which waited for: 9 -> 13; matrix products, arithmetic and copies ran while one was open for 1% -> 1% of each run, Pallas kernels for 11% -> 11%
where the time goes in v3:
time: 583 us; the launch traced here: 582 us
  Pallas kernels  407 us (70%)
  waiting for transfers between devices  146 us (25%)
  starting transfers between devices  21.8 us (4%)
    pallas_call x1, Pallas kernels, reduce_gradients(): pl.pallas_call(functools.partial(reduce_kernel, axis_name, half_rows), ou...  336 us
    ppermute x42, waiting for transfers between devices, move(): return lax.ppermute(array, axis_name, pairs)  146 us
    pallas_call x6, Pallas kernels, adam_chunk(): pl.pallas_call(functools.partial(adam_kernel, start), out_shape=(whole, w...  37.1 us
    pallas_call x7, Pallas kernels, place(): pl.pallas_call(functools.partial(place_kernel, axis_name, tuple(((who, st...  33.4 us
    ppermute x42, starting transfers between devices, move(): return lax.ppermute(array, axis_name, pairs)  21.8 us
  transfers between devices with their start and end apart: 42, of which 13 were waited for; matrix products, arithmetic and copies ran while one was open for 1% of the time, Pallas kernels for 11%

profile of v3, /device:TPU:0, one launch (start us, length us, event | category | flops | bytes accessed | tf_op | source)
XLA Modules:
  0.0 582.4 jit_solution(11330409398200557905)
XLA Ops:
  1.3 336.1 %reduce_gradients.1 = (f32[19200,128]{1,0:T(8,128)}, f32[192,128]{1,0:T(8,128)}, f32[8,128]{1,0:T(8,128)}, bf16[12,9600,128]{2,1,0:T(8,128)(2,1)}) custom-call(bf16[1,19660800]{1,0:T(2,128)(2,1)} %g_ref.1, bf16[1,24320]{1,0:T(2,128)(2,1)} %gv_raw_ref.1), custom_call_target="tpu_custom_call" | custom-call | tf_op jit(solution)/shard_map/reduce_gradients/pallas_call | solution.py:306
  337.4 4.2 shard_map.144
  341.7 1.1 collective-permute-start.1
  342.9 0.9 collective-permute-start.3
  343.8 5.4 shard_map.145
  349.2 9.0 %shard_map.146 = (f32[19200,128]{1,0:T(8,128)}, f32[19200,128]{1,0:T(8,128)}, f32[19200,128]{1,0:T(8,128)}, bf16[5280,128]{1,0:T(8,128)(2,1)}) custom-call(f32[1]{0:T(128)} %bitcast.18.lr_ref, f32[8,128]{1,0:T(8,128)} %get-tuple-element.34.clip_ref, ...), custom_call_target="tpu_custom_call", output_to_operand_aliasing={{0}: (6, {}), {1}: (7, {}), {2}: (8, {})} | custom-call | flops 40550400 | bytes 20275200 | tf_op jit(solution)/shard_map/pallas_call | solution.py:399
  358.2 9.0 %shard_map.147 = (f32[19200,128]{1,0:T(8,128)}, f32[19200,128]{1,0:T(8,128)}, f32[19200,128]{1,0:T(8,128)}, bf16[5280,128]{1,0:T(8,128)(2,1)}) custom-call(f32[1]{0:T(128)} %bitcast.19.lr_ref, f32[8,128]{1,0:T(8,128)} %get-tuple-element.34.clip_ref, ...), custom_call_target="tpu_custom_call", output_to_operand_aliasing={{0}: (6, {}), {1}: (7, {}), {2}: (8, {})} | custom-call | flops 40550400 | bytes 20275200 | tf_op jit(solution)/shard_map/pallas_call | solution.py:399
  367.1 5.4 shard_map.148
  372.6 4.2 shard_map.149
  376.8 1.4 collective-permute-start.26
  378.4 0.7 collective-permute-start.6
  379.0 1.1 collective-permute-start.28
  380.2 8.3 %collective-permute-done.26.refs_9_ = bf16[1440,128]{1,0:T(8,128)(2,1)S(1)} collective-permute-done((bf16[1440,128]{1,0:T(8,128)(2,1)}, bf16[1440,128]{1,0:T(8,128)(2,1)S(1)}, u32[]{:S(2)}, u32[]{:S(2)}) %collective-permute-start.26) | collective-permute-done | bytes 368672 | tf_op jit(solution)/shard_map/ppermute | solution.py:464
  388.5 1.3 collective-permute-done.28.refs_11_
  389.8 1.1 collective-permute-start.8
  391.4 0.9 collective-permute-start.21
  392.3 12.0 %collective-permute-done.6.refs_8_ = bf16[2880,128]{1,0:T(8,128)(2,1)S(1)} collective-permute-done((bf16[2880,128]{1,0:T(8,128)(2,1)}, bf16[2880,128]{1,0:T(8,128)(2,1)S(1)}, u32[]{:S(2)}, u32[]{:S(2)}) %collective-permute-start.6) | collective-permute-done | bytes 737312 | tf_op jit(solution)/shard_map/ppermute | solution.py:464
  404.3 1.1 collective-permute-start.23
  405.4 3.6 collective-permute-done.8.refs_10_
  409.0 1.4 collective-permute-start.11
  410.4 9.7 %collective-permute-done.21.refs_3_ = bf16[2880,128]{1,0:T(8,128)(2,1)S(1)} collective-permute-done((bf16[2880,128]{1,0:T(8,128)(2,1)}, bf16[2880,128]{1,0:T(8,128)(2,1)S(1)}, u32[]{:S(2)}, u32[]{:S(2)}) %collective-permute-start.21) | collective-permute-done | bytes 737312 | tf_op jit(solution)/shard_map/ppermute | solution.py:464
  420.1 3.3 collective-permute-done.23.refs_5_
  423.4 1.4 collective-permute-start.38
  424.8 0.7 collective-permute-start.40
  425.5 1.3 collective-permute-start.13
  426.8 29.7 %collective-permute-done.38.refs_1_ = bf16[1440,128]{1,0:T(8,128)(2,1)} collective-permute-done((bf16[1440,128]{1,0:T(8,128)(2,1)}, bf16[1440,128]{1,0:T(8,128)(2,1)}, u32[]{:S(2)}, u32[]{:S(2)}) %collective-permute-start.38) | collective-permute-done | bytes 368672 | tf_op jit(solution)/shard_map/ppermute | solution.py:464
  456.6 1.4 collective-permute-start.16
  458.0 0.7 collective-permute-start.18
  458.6 5.8 collective-permute-done.13.refs_5_
  464.4 0.7 collective-permute-start.30
  465.1 23.8 %collective-permute-done.16.refs_3_ = bf16[5280,128]{1,0:T(8,128)(2,1)S(1)} collective-permute-done((bf16[5280,128]{1,0:T(8,128)(2,1)}, bf16[5280,128]{1,0:T(8,128)(2,1)S(1)}, u32[]{:S(2)}, u32[]{:S(2)}) %collective-permute-start.16) | collective-permute-done | bytes 1351712 | tf_op jit(solution)/shard_map/ppermute | solution.py:464
  488.9 4.5 collective-permute-done.18.refs_5_
  493.9 0.7 collective-permute-start.36
  494.5 12.9 %collective-permute-done.30.refs_1_ = bf16[2880,128]{1,0:T(8,128)(2,1)S(1)} collective-permute-done((bf16[2880,128]{1,0:T(8,128)(2,1)S(1)}, bf16[2880,128]{1,0:T(8,128)(2,1)S(1)}, u32[]{:S(2)}, u32[]{:S(2)}) %collective-permute-start.30) | collective-permute-done | bytes 737312 | tf_op jit(solution)/shard_map/ppermute | solution.py:464
  507.5 0.7 collective-permute-start.32
  508.2 1.1 collective-permute-start.34
  509.3 4.0 collective-permute-done.36.refs_3_
  514.0 27.4 %collective-permute-done.32.refs_3_ = bf16[5280,128]{1,0:T(8,128)(2,1)} collective-permute-done((bf16[5280,128]{1,0:T(8,128)(2,1)S(1)}, bf16[5280,128]{1,0:T(8,128)(2,1)}, u32[]{:S(2)}, u32[]{:S(2)}) %collective-permute-start.32) | collective-permute-done | bytes 1351712 | tf_op jit(solution)/shard_map/ppermute | solution.py:464
  541.9 1.1 copy-done.6
  543.0 1.3 slice.8
  546.5 2.5 multiply_subtract_fusion
  549.0 5.6 shard_map.150.refs_0_
  554.5 6.5 %shard_map.151.refs_0_ = bf16[153600,128]{1,0:T(8,128)(2,1)} custom-call(bf16[153600,128]{1,0:T(8,128)(2,1)} %shard_map.150.refs_0_, bf16[5280,128]{1,0:T(8,128)(2,1)} %get-tuple-element.57.refs_1_, bf16[5280,128]{1,0:T(8,128)(2,1)} %collective-permute-done.10.refs_2_, bf16[5280,128]{1,0:T(8,128)(2,1)} %copy-done, ...), custom_call_target="tpu_custom_call", output_to_operand_aliasing={{}: (0, {})} | custom-call | flops 60825600 | bytes 16220160 | tf_op jit(solution)/shard_map/pallas_call | solution.py:444
  561.0 6.5 %shard_map.152.refs_0_ = bf16[153600,128]{1,0:T(8,128)(2,1)} custom-call(bf16[153600,128]{1,0:T(8,128)(2,1)} %shard_map.151.refs_0_, bf16[5280,128]{1,0:T(8,128)(2,1)} %get-tuple-element.58.refs_1_, bf16[5280,128]{1,0:T(8,128)(2,1)} %copy-done.2, bf16[5280,128]{1,0:T(8,128)(2,1)} %copy-done.3, ...), custom_call_target="tpu_custom_call", output_to_operand_aliasing={{}: (0, {})} | custom-call | flops 60825600 | bytes 16220160 | tf_op jit(solution)/shard_map/pallas_call | solution.py:444
  567.5 5.7 shard_map.153.refs_0_
  573.2 3.6 shard_map.154.refs_0_
  576.8 3.4 shard_map.155.refs_0_
  580.3 2.2 shard_map.156
  (100 shorter events, 4.9 us)
Async XLA Ops:
  341.6 36.6 %collective-permute-start = (bf16[1440,128]{1,0:T(8,128)(2,1)}, bf16[1440,128]{1,0:T(8,128)(2,1)}, u32[]{:S(2)}, u32[]{:S(2)}) collective-permute-start(bf16[1440,128]{1,0:T(8,128)(2,1)} %get-tuple-element.55.refs_0_), channel_id=1, source_target_pairs={{0,1},{1,0},{2,3},{3,2},{4,5},{5,4},{6,7},{7,6}} | collective-permute-start | bytes 1105928 | tf_op jit(solution)/shard_map/ppermute | solution.py:464
  341.7 36.6 %collective-permute-start.1 = (bf16[1440,128]{1,0:T(8,128)(2,1)}, bf16[1440,128]{1,0:T(8,128)(2,1)}, u32[]{:S(2)}, u32[]{:S(2)}) collective-permute-start(bf16[1440,128]{1,0:T(8,128)(2,1)} %get-tuple-element.55.refs_0_), channel_id=1, source_target_pairs={{0,2},{1,3},{2,0},{3,1},{4,6},{5,7},{6,4},{7,5}} | collective-permute-start | bytes 1105928 | tf_op jit(solution)/shard_map/ppermute | solution.py:464
  342.9 36.2 %collective-permute-start.3 = (bf16[1440,128]{1,0:T(8,128)(2,1)}, bf16[1440,128]{1,0:T(8,128)(2,1)}, u32[]{:S(2)}, u32[]{:S(2)}) collective-permute-start(bf16[1440,128]{1,0:T(8,128)(2,1)} %get-tuple-element.55.refs_0_), channel_id=1, source_target_pairs={{0,4},{1,5},{2,6},{3,7},{4,0},{5,1},{6,2},{7,3}} | collective-permute-start | bytes 1105928 | tf_op jit(solution)/shard_map/ppermute | solution.py:464
  376.8 3.4 collective-permute-start.25
  376.8 11.7 %collective-permute-start.26 = (bf16[1440,128]{1,0:T(8,128)(2,1)}, bf16[1440,128]{1,0:T(8,128)(2,1)S(1)}, u32[]{:S(2)}, u32[]{:S(2)}) collective-permute-start(bf16[1440,128]{1,0:T(8,128)(2,1)} %get-tuple-element.60.refs_7_), channel_id=1, source_target_pairs={{0,2},{1,3},{2,0},{3,1},{4,6},{5,7},{6,4},{7,5}} | collective-permute-start | bytes 1105928 | tf_op jit(solution)/shard_map/ppermute | solution.py:464
  378.2 13.3 %collective-permute-start.5 = (bf16[2880,128]{1,0:T(8,128)(2,1)}, bf16[2880,128]{1,0:T(8,128)(2,1)}, u32[]{:S(2)}, u32[]{:S(2)}) collective-permute-start(bf16[2880,128]{1,0:T(8,128)(2,1)} %get-tuple-element.56.refs_6_), channel_id=1, source_target_pairs={{0,1},{1,0},{2,3},{3,2},{4,5},{5,4},{6,7},{7,6}} | collective-permute-start | bytes 2211848 | tf_op jit(solution)/shard_map/ppermute | solution.py:464
  378.4 25.9 %collective-permute-start.6 = (bf16[2880,128]{1,0:T(8,128)(2,1)}, bf16[2880,128]{1,0:T(8,128)(2,1)S(1)}, u32[]{:S(2)}, u32[]{:S(2)}) collective-permute-start(bf16[2880,128]{1,0:T(8,128)(2,1)} %get-tuple-element.56.refs_6_), channel_id=1, source_target_pairs={{0,2},{1,3},{2,0},{3,1},{4,6},{5,7},{6,4},{7,5}} | collective-permute-start | bytes 2211848 | tf_op jit(solution)/shard_map/ppermute | solution.py:464
  379.0 10.7 %collective-permute-start.28 = (bf16[1440,128]{1,0:T(8,128)(2,1)}, bf16[1440,128]{1,0:T(8,128)(2,1)S(1)}, u32[]{:S(2)}, u32[]{:S(2)}) collective-permute-start(bf16[1440,128]{1,0:T(8,128)(2,1)} %get-tuple-element.60.refs_7_), channel_id=1, source_target_pairs={{0,4},{1,5},{2,6},{3,7},{4,0},{5,1},{6,2},{7,3}} | collective-permute-start | bytes 1105928 | tf_op jit(solution)/shard_map/ppermute | solution.py:464
  380.2 10.7 %collective-permute-start.2 = (bf16[1440,128]{1,0:T(8,128)(2,1)}, bf16[1440,128]{1,0:T(8,128)(2,1)S(1)}, u32[]{:S(2)}, u32[]{:S(2)}) collective-permute-start(bf16[1440,128]{1,0:T(8,128)(2,1)} %collective-permute-done.1.refs_2_), channel_id=1, source_target_pairs={{0,1},{1,0},{2,3},{3,2},{4,5},{5,4},{6,7},{7,6}} | collective-permute-start | bytes 1105928 | tf_op jit(solution)/shard_map/ppermute | solution.py:464
  388.5 75.9 %copy-start.18 = (bf16[1440,128]{1,0:T(8,128)(2,1)}, bf16[1440,128]{1,0:T(8,128)(2,1)S(1)}, u32[]{:S(2)}) copy-start(bf16[1440,128]{1,0:T(8,128)(2,1)S(1)} %collective-permute-done.26.refs_9_) | copy-start | bytes 1105924
  388.5 2.4 collective-permute-start.4
  389.8 19.2 %collective-permute-start.8 = (bf16[2880,128]{1,0:T(8,128)(2,1)}, bf16[2880,128]{1,0:T(8,128)(2,1)S(1)}, u32[]{:S(2)}, u32[]{:S(2)}) collective-permute-start(bf16[2880,128]{1,0:T(8,128)(2,1)} %get-tuple-element.56.refs_6_), channel_id=1, source_target_pairs={{0,4},{1,5},{2,6},{3,7},{4,0},{5,1},{6,2},{7,3}} | collective-permute-start | bytes 2211848 | tf_op jit(solution)/shard_map/ppermute | solution.py:464
  390.9 18.1 %collective-permute-start.20 = (bf16[2880,128]{1,0:T(8,128)(2,1)}, bf16[2880,128]{1,0:T(8,128)(2,1)}, u32[]{:S(2)}, u32[]{:S(2)}) collective-permute-start(bf16[2880,128]{1,0:T(8,128)(2,1)} %get-tuple-element.59.refs_1_), channel_id=1, source_target_pairs={{0,1},{1,0},{2,3},{3,2},{4,5},{5,4},{6,7},{7,6}} | collective-permute-start | bytes 2211848 | tf_op jit(solution)/shard_map/ppermute | solution.py:464
  390.9 67.0 %collective-permute-start.10 = (bf16[5280,128]{1,0:T(8,128)(2,1)}, bf16[5280,128]{1,0:T(8,128)(2,1)}, u32[]{:S(2)}, u32[]{:S(2)}) collective-permute-start(bf16[5280,128]{1,0:T(8,128)(2,1)} %get-tuple-element.57.refs_1_), channel_id=1, source_target_pairs={{0,1},{1,0},{2,3},{3,2},{4,5},{5,4},{6,7},{7,6}} | collective-permute-start | bytes 4055048 | tf_op jit(solution)/shard_map/ppermute | solution.py:464
  391.4 28.6 %collective-permute-start.21 = (bf16[2880,128]{1,0:T(8,128)(2,1)}, bf16[2880,128]{1,0:T(8,128)(2,1)S(1)}, u32[]{:S(2)}, u32[]{:S(2)}) collective-permute-start(bf16[2880,128]{1,0:T(8,128)(2,1)} %get-tuple-element.59.refs_1_), channel_id=1, source_target_pairs={{0,2},{1,3},{2,0},{3,1},{4,6},{5,7},{6,4},{7,5}} | collective-permute-start | bytes 2211848 | tf_op jit(solution)/shard_map/ppermute | solution.py:464
  404.3 109.1 %copy-start.14 = (bf16[2880,128]{1,0:T(8,128)(2,1)}, bf16[2880,128]{1,0:T(8,128)(2,1)S(1)}, u32[]{:S(2)}) copy-start(bf16[2880,128]{1,0:T(8,128)(2,1)S(1)} %collective-permute-done.6.refs_8_) | copy-start | bytes 2211844
  404.3 19.1 %collective-permute-start.23 = (bf16[2880,128]{1,0:T(8,128)(2,1)}, bf16[2880,128]{1,0:T(8,128)(2,1)S(1)}, u32[]{:S(2)}, u32[]{:S(2)}) collective-permute-start(bf16[2880,128]{1,0:T(8,128)(2,1)} %get-tuple-element.59.refs_1_), channel_id=1, source_target_pairs={{0,4},{1,5},{2,6},{3,7},{4,0},{5,1},{6,2},{7,3}} | collective-permute-start | bytes 2211848 | tf_op jit(solution)/shard_map/ppermute | solution.py:464
  409.0 104.9 %copy-start.15 = (bf16[2880,128]{1,0:T(8,128)(2,1)}, bf16[2880,128]{1,0:T(8,128)(2,1)S(1)}, u32[]{:S(2)}) copy-start(bf16[2880,128]{1,0:T(8,128)(2,1)S(1)} %collective-permute-done.8.refs_10_) | copy-start | bytes 2211844
  409.0 15.8 %collective-permute-start.27 = (bf16[1440,128]{1,0:T(8,128)(2,1)S(1)}, bf16[1440,128]{1,0:T(8,128)(2,1)S(1)}, u32[]{:S(2)}, u32[]{:S(2)}) collective-permute-start(bf16[1440,128]{1,0:T(8,128)(2,1)S(1)} %collective-permute-done.26.refs_9_), channel_id=1, source_target_pairs={{0,1},{1,0},{2,3},{3,2},{4,5},{5,4},{6,7},{7,6}} | collective-permute-start | bytes 1105928 | tf_op jit(solution)/shard_map/ppermute | solution.py:464
  409.0 49.6 %collective-permute-start.11 = (bf16[5280,128]{1,0:T(8,128)(2,1)}, bf16[5280,128]{1,0:T(8,128)(2,1)S(1)}, u32[]{:S(2)}, u32[]{:S(2)}) collective-permute-start(bf16[5280,128]{1,0:T(8,128)(2,1)} %get-tuple-element.57.refs_1_), channel_id=1, source_target_pairs={{0,2},{1,3},{2,0},{3,1},{4,6},{5,7},{6,4},{7,5}} | collective-permute-start | bytes 4055048 | tf_op jit(solution)/shard_map/ppermute | solution.py:464
  420.1 89.2 %copy-start.9 = (bf16[2880,128]{1,0:T(8,128)(2,1)}, bf16[2880,128]{1,0:T(8,128)(2,1)S(1)}, u32[]{:S(2)}) copy-start(bf16[2880,128]{1,0:T(8,128)(2,1)S(1)} %collective-permute-done.21.refs_3_) | copy-start | bytes 2211844
  420.1 5.4 collective-permute-start.29
  423.4 85.9 %copy-start.10 = (bf16[2880,128]{1,0:T(8,128)(2,1)}, bf16[2880,128]{1,0:T(8,128)(2,1)S(1)}, u32[]{:S(2)}) copy-start(bf16[2880,128]{1,0:T(8,128)(2,1)S(1)} %collective-permute-done.23.refs_5_) | copy-start | bytes 2211844
  423.4 33.2 %collective-permute-start.38 = (bf16[1440,128]{1,0:T(8,128)(2,1)}, bf16[1440,128]{1,0:T(8,128)(2,1)}, u32[]{:S(2)}, u32[]{:S(2)}) collective-permute-start(bf16[1440,128]{1,0:T(8,128)(2,1)} %collective-permute-done.3.refs_4_), channel_id=1, source_target_pairs={{0,2},{1,3},{2,0},{3,1},{4,6},{5,7},{6,4},{7,5}} | collective-permute-start | bytes 1105928 | tf_op jit(solution)/shard_map/ppermute | solution.py:464
  424.8 31.8 %collective-permute-start.40 = (bf16[1440,128]{1,0:T(8,128)(2,1)S(1)}, bf16[1440,128]{1,0:T(8,128)(2,1)}, u32[]{:S(2)}, u32[]{:S(2)}) collective-permute-start(bf16[1440,128]{1,0:T(8,128)(2,1)S(1)} %collective-permute-done.26.refs_9_), channel_id=1, source_target_pairs={{0,4},{1,5},{2,6},{3,7},{4,0},{5,1},{6,2},{7,3}} | collective-permute-start | bytes 1105928 | tf_op jit(solution)/shard_map/ppermute | solution.py:464
  425.5 38.9 %collective-permute-start.13 = (bf16[5280,128]{1,0:T(8,128)(2,1)}, bf16[5280,128]{1,0:T(8,128)(2,1)S(1)}, u32[]{:S(2)}, u32[]{:S(2)}) collective-permute-start(bf16[5280,128]{1,0:T(8,128)(2,1)} %get-tuple-element.57.refs_1_), channel_id=1, source_target_pairs={{0,4},{1,5},{2,6},{3,7},{4,0},{5,1},{6,2},{7,3}} | collective-permute-start | bytes 4055048 | tf_op jit(solution)/shard_map/ppermute | solution.py:464
  456.6 7.8 %collective-permute-start.15 = (bf16[5280,128]{1,0:T(8,128)(2,1)}, bf16[5280,128]{1,0:T(8,128)(2,1)S(1)}, u32[]{:S(2)}, u32[]{:S(2)}) collective-permute-start(bf16[5280,128]{1,0:T(8,128)(2,1)} %get-tuple-element.58.refs_1_), channel_id=1, source_target_pairs={{0,1},{1,0},{2,3},{3,2},{4,5},{5,4},{6,7},{7,6}} | collective-permute-start | bytes 4055048 | tf_op jit(solution)/shard_map/ppermute | solution.py:464
  456.6 32.3 %collective-permute-start.16 = (bf16[5280,128]{1,0:T(8,128)(2,1)}, bf16[5280,128]{1,0:T(8,128)(2,1)S(1)}, u32[]{:S(2)}, u32[]{:S(2)}) collective-permute-start(bf16[5280,128]{1,0:T(8,128)(2,1)} %get-tuple-element.58.refs_1_), channel_id=1, source_target_pairs={{0,2},{1,3},{2,0},{3,1},{4,6},{5,7},{6,4},{7,5}} | collective-permute-start | bytes 4055048 | tf_op jit(solution)/shard_map/ppermute | solution.py:464
  458.0 35.4 %collective-permute-start.18 = (bf16[5280,128]{1,0:T(8,128)(2,1)}, bf16[5280,128]{1,0:T(8,128)(2,1)S(1)}, u32[]{:S(2)}, u32[]{:S(2)}) collective-permute-start(bf16[5280,128]{1,0:T(8,128)(2,1)} %get-tuple-element.58.refs_1_), channel_id=1, source_target_pairs={{0,4},{1,5},{2,6},{3,7},{4,0},{5,1},{6,2},{7,3}} | collective-permute-start | bytes 4055048 | tf_op jit(solution)/shard_map/ppermute | solution.py:464
  458.6 34.7 %collective-permute-start.7 = (bf16[2880,128]{1,0:T(8,128)(2,1)S(1)}, bf16[2880,128]{1,0:T(8,128)(2,1)}, u32[]{:S(2)}, u32[]{:S(2)}) collective-permute-start(bf16[2880,128]{1,0:T(8,128)(2,1)S(1)} %collective-permute-done.6.refs_8_), channel_id=1, source_target_pairs={{0,1},{1,0},{2,3},{3,2},{4,5},{5,4},{6,7},{7,6}} | collective-permute-start | bytes 2211848 | tf_op jit(solution)/shard_map/ppermute | solution.py:464
  464.4 29.5 %collective-permute-start.9 = (bf16[2880,128]{1,0:T(8,128)(2,1)S(1)}, bf16[2880,128]{1,0:T(8,128)(2,1)S(1)}, u32[]{:S(2)}, u32[]{:S(2)}) collective-permute-start(bf16[2880,128]{1,0:T(8,128)(2,1)S(1)} %collective-permute-done.8.refs_10_), channel_id=1, source_target_pairs={{0,1},{1,0},{2,3},{3,2},{4,5},{5,4},{6,7},{7,6}} | collective-permute-start | bytes 2211848 | tf_op jit(solution)/shard_map/ppermute | solution.py:464
  464.4 77.5 %copy-start.2 = (bf16[5280,128]{1,0:T(8,128)(2,1)}, bf16[5280,128]{1,0:T(8,128)(2,1)S(1)}, u32[]{:S(2)}) copy-start(bf16[5280,128]{1,0:T(8,128)(2,1)S(1)} %collective-permute-done.15.refs_2_) | copy-start | bytes 4055044
  464.4 43.0 %collective-permute-start.30 = (bf16[2880,128]{1,0:T(8,128)(2,1)S(1)}, bf16[2880,128]{1,0:T(8,128)(2,1)S(1)}, u32[]{:S(2)}, u32[]{:S(2)}) collective-permute-start(bf16[2880,128]{1,0:T(8,128)(2,1)S(1)} %collective-permute-done.6.refs_8_), channel_id=1, source_target_pairs={{0,4},{1,5},{2,6},{3,7},{4,0},{5,1},{6,2},{7,3}} | collective-permute-start | bytes 2211848 | tf_op jit(solution)/shard_map/ppermute | solution.py:464
  488.9 18.6 %collective-permute-start.22 = (bf16[2880,128]{1,0:T(8,128)(2,1)S(1)}, bf16[2880,128]{1,0:T(8,128)(2,1)S(1)}, u32[]{:S(2)}, u32[]{:S(2)}) collective-permute-start(bf16[2880,128]{1,0:T(8,128)(2,1)S(1)} %collective-permute-done.21.refs_3_), channel_id=1, source_target_pairs={{0,1},{1,0},{2,3},{3,2},{4,5},{5,4},{6,7},{7,6}} | collective-permute-start | bytes 2211848 | tf_op jit(solution)/shard_map/ppermute | solution.py:464
  493.3 14.8 %collective-permute-start.24 = (bf16[2880,128]{1,0:T(8,128)(2,1)S(1)}, bf16[2880,128]{1,0:T(8,128)(2,1)S(1)}, u32[]{:S(2)}, u32[]{:S(2)}) collective-permute-start(bf16[2880,128]{1,0:T(8,128)(2,1)S(1)} %collective-permute-done.23.refs_5_), channel_id=1, source_target_pairs={{0,1},{1,0},{2,3},{3,2},{4,5},{5,4},{6,7},{7,6}} | collective-permute-start | bytes 2211848 | tf_op jit(solution)/shard_map/ppermute | solution.py:464
  493.4 20.5 %collective-permute-start.12 = (bf16[5280,128]{1,0:T(8,128)(2,1)S(1)}, bf16[5280,128]{1,0:T(8,128)(2,1)S(1)}, u32[]{:S(2)}, u32[]{:S(2)}) collective-permute-start(bf16[5280,128]{1,0:T(8,128)(2,1)S(1)} %collective-permute-done.11.refs_3_), channel_id=1, source_target_pairs={{0,1},{1,0},{2,3},{3,2},{4,5},{5,4},{6,7},{7,6}} | collective-permute-start | bytes 4055048 | tf_op jit(solution)/shard_map/ppermute | solution.py:464
  493.9 19.5 %collective-permute-start.36 = (bf16[2880,128]{1,0:T(8,128)(2,1)S(1)}, bf16[2880,128]{1,0:T(8,128)(2,1)}, u32[]{:S(2)}, u32[]{:S(2)}) collective-permute-start(bf16[2880,128]{1,0:T(8,128)(2,1)S(1)} %collective-permute-done.23.refs_5_), channel_id=1, source_target_pairs={{0,2},{1,3},{2,0},{3,1},{4,6},{5,7},{6,4},{7,5}} | collective-permute-start | bytes 2211848 | tf_op jit(solution)/shard_map/ppermute | solution.py:464
  507.4 5.9 %collective-permute-start.31 = (bf16[2880,128]{1,0:T(8,128)(2,1)S(1)}, bf16[2880,128]{1,0:T(8,128)(2,1)}, u32[]{:S(2)}, u32[]{:S(2)}) collective-permute-start(bf16[2880,128]{1,0:T(8,128)(2,1)S(1)} %collective-permute-done.30.refs_1_), channel_id=1, source_target_pairs={{0,1},{1,0},{2,3},{3,2},{4,5},{5,4},{6,7},{7,6}} | collective-permute-start | bytes 2211848 | tf_op jit(solution)/shard_map/ppermute | solution.py:464
  507.5 33.9 %collective-permute-start.32 = (bf16[5280,128]{1,0:T(8,128)(2,1)S(1)}, bf16[5280,128]{1,0:T(8,128)(2,1)}, u32[]{:S(2)}, u32[]{:S(2)}) collective-permute-start(bf16[5280,128]{1,0:T(8,128)(2,1)S(1)} %collective-permute-done.13.refs_5_), channel_id=1, source_target_pairs={{0,2},{1,3},{2,0},{3,1},{4,6},{5,7},{6,4},{7,5}} | collective-permute-start | bytes 4055048 | tf_op jit(solution)/shard_map/ppermute | solution.py:464
  508.2 33.2 %collective-permute-start.34 = (bf16[5280,128]{1,0:T(8,128)(2,1)S(1)}, bf16[5280,128]{1,0:T(8,128)(2,1)}, u32[]{:S(2)}, u32[]{:S(2)}) collective-permute-start(bf16[5280,128]{1,0:T(8,128)(2,1)S(1)} %collective-permute-done.16.refs_3_), channel_id=1, source_target_pairs={{0,4},{1,5},{2,6},{3,7},{4,0},{5,1},{6,2},{7,3}} | collective-permute-start | bytes 4055048 | tf_op jit(solution)/shard_map/ppermute | solution.py:464
  513.3 28.6 %collective-permute-start.14 = (bf16[5280,128]{1,0:T(8,128)(2,1)S(1)}, bf16[5280,128]{1,0:T(8,128)(2,1)S(1)}, u32[]{:S(2)}, u32[]{:S(2)}) collective-permute-start(bf16[5280,128]{1,0:T(8,128)(2,1)S(1)} %collective-permute-done.13.refs_5_), channel_id=1, source_target_pairs={{0,1},{1,0},{2,3},{3,2},{4,5},{5,4},{6,7},{7,6}} | collective-permute-start | bytes 4055048 | tf_op jit(solution)/shard_map/ppermute | solution.py:464
  513.4 30.9 %collective-permute-start.17 = (bf16[5280,128]{1,0:T(8,128)(2,1)S(1)}, bf16[5280,128]{1,0:T(8,128)(2,1)S(1)}, u32[]{:S(2)}, u32[]{:S(2)}) collective-permute-start(bf16[5280,128]{1,0:T(8,128)(2,1)S(1)} %collective-permute-done.16.refs_3_), channel_id=1, source_target_pairs={{0,1},{1,0},{2,3},{3,2},{4,5},{5,4},{6,7},{7,6}} | collective-permute-start | bytes 4055048 | tf_op jit(solution)/shard_map/ppermute | solution.py:464
  513.9 30.9 %collective-permute-start.19 = (bf16[5280,128]{1,0:T(8,128)(2,1)S(1)}, bf16[5280,128]{1,0:T(8,128)(2,1)S(1)}, u32[]{:S(2)}, u32[]{:S(2)}) collective-permute-start(bf16[5280,128]{1,0:T(8,128)(2,1)S(1)} %collective-permute-done.18.refs_5_), channel_id=1, source_target_pairs={{0,1},{1,0},{2,3},{3,2},{4,5},{5,4},{6,7},{7,6}} | collective-permute-start | bytes 4055048 | tf_op jit(solution)/shard_map/ppermute | solution.py:464
  541.4 31.8 %collective-permute-start.33 = (bf16[5280,128]{1,0:T(8,128)(2,1)}, bf16[5280,128]{1,0:T(8,128)(2,1)}, u32[]{:S(2)}, u32[]{:S(2)}) collective-permute-start(bf16[5280,128]{1,0:T(8,128)(2,1)} %collective-permute-done.32.refs_3_), channel_id=1, source_target_pairs={{0,1},{1,0},{2,3},{3,2},{4,5},{5,4},{6,7},{7,6}} | collective-permute-start | bytes 4055048 | tf_op jit(solution)/shard_map/ppermute | solution.py:464
  541.4 35.5 %collective-permute-start.35 = (bf16[5280,128]{1,0:T(8,128)(2,1)}, bf16[5280,128]{1,0:T(8,128)(2,1)}, u32[]{:S(2)}, u32[]{:S(2)}) collective-permute-start(bf16[5280,128]{1,0:T(8,128)(2,1)} %collective-permute-done.34.refs_1_), channel_id=1, source_target_pairs={{0,1},{1,0},{2,3},{3,2},{4,5},{5,4},{6,7},{7,6}} | collective-permute-start | bytes 4055048 | tf_op jit(solution)/shard_map/ppermute | solution.py:464
  543.0 33.8 %collective-permute-start.37 = (bf16[2880,128]{1,0:T(8,128)(2,1)}, bf16[2880,128]{1,0:T(8,128)(2,1)}, u32[]{:S(2)}, u32[]{:S(2)}) collective-permute-start(bf16[2880,128]{1,0:T(8,128)(2,1)} %collective-permute-done.36.refs_3_), channel_id=1, source_target_pairs={{0,1},{1,0},{2,3},{3,2},{4,5},{5,4},{6,7},{7,6}} | collective-permute-start | bytes 2211848 | tf_op jit(solution)/shard_map/ppermute | solution.py:464
  544.3 36.0 %collective-permute-start.39 = (bf16[1440,128]{1,0:T(8,128)(2,1)}, bf16[1440,128]{1,0:T(8,128)(2,1)}, u32[]{:S(2)}, u32[]{:S(2)}) collective-permute-start(bf16[1440,128]{1,0:T(8,128)(2,1)} %collective-permute-done.38.refs_1_), channel_id=1, source_target_pairs={{0,1},{1,0},{2,3},{3,2},{4,5},{5,4},{6,7},{7,6}} | collective-permute-start | bytes 1105928 | tf_op jit(solution)/shard_map/ppermute | solution.py:464
  545.4 34.9 %collective-permute-start.41 = (bf16[1440,128]{1,0:T(8,128)(2,1)}, bf16[1440,128]{1,0:T(8,128)(2,1)}, u32[]{:S(2)}, u32[]{:S(2)}) collective-permute-start(bf16[1440,128]{1,0:T(8,128)(2,1)} %collective-permute-done.40.refs_3_), channel_id=1, source_target_pairs={{0,1},{1,0},{2,3},{3,2},{4,5},{5,4},{6,7},{7,6}} | collective-permute-start | bytes 1105928 | tf_op jit(solution)/shard_map/ppermute | solution.py:464
  (18 other events, 457.9 us)

commit v4 on v3

--- a/solution.py
+++ b/solution.py
@@ -21,10 +21,11 @@
 MESH = pl.DeviceIdType.MESH
 LANES = 128
 DEVICES = 8
-CHUNKS = 10
-BLOCK = 96
+CHUNKS = 12
+BLOCK = 160
 ADAM_ROWS = 480
-SIZES = (1440, 2880, 5280, 5280, 2880, 1440)
+HEAD_ROWS = 480
+SIZES = (1440, 2400, 5280, 5760, 2880, 1440)
 NEAR_GROUPS = ((0, 1), (2,), (3,), (4, 5))
 FAR_GROUPS = ((1, 2), (3, 4), (0, 5))
 VMEM_ALL = 67043328
@@ -47,11 +48,17 @@
     return me, core, x, y, dev
 
 
-def reduce_kernel(axis_name, half_rows, g_ref, gv_raw_ref, gsum_ref, vsum_ref, clip_ref, stage_ref,
-                  first, own_first, direct, own_direct, fsum, psum, raw, packed, vraw, gv_ref, vrecv, nsend, nrecv,
+def reduce_kernel(axis_name, half_rows, lr_ref, g_ref, gv_raw_ref, p_ref, m_ref, v_ref,
+                  gsum_ref, vsum_ref, clip_ref, head_ref, stage_ref,
+                  first, own_first, direct, own_direct, fsum, psum, raw, packed, vraw, vsend, vrecv, vpart, vall, nsend, nrecv,
+                  clip, head_state, head,
                   vraw_sem, raw_sem, pack_sem, first_recv, direct_recv, psum_recv, send_sem, fsum_send,
-                  vec_send, vec_recv, nrm_send, nrm_recv, out_sem):
+                  vec_send, vec_recv, part_send, part_recv, nrm_send, nrm_recv, out_sem,
+                  late_sem, head_sem):
     me, core, x, y, dev = places(axis_name)
+    barrier = pltpu.get_barrier_semaphore()
+    for o in range(1, DEVICES):
+        pl.semaphore_signal(barrier, inc=1, device_id=((me + o) % DEVICES,), device_id_type=MESH)
     sib = dev(y, x, 1 - core)
     xs = [dev(y, 1 - x, 0), dev(y, 1 - x, 1)]
     ys = [dev(1 - y, x, 0), dev(1 - y, x, 1)]
@@ -117,16 +124,15 @@
 
         lax.fori_loop(0, rows // BLOCK, body, 0)
 
-    vec_size, vec_rows = gv_raw_ref.shape[1], gv_ref.shape[0]
+    vec_size, vec_rows = gv_raw_ref.shape[1], vsend.shape[1]
     vec_load = pltpu.make_async_copy(gv_raw_ref, vraw.at[:, pl.ds(0, vec_size)], vraw_sem)
     vec_load.start()
     for h in range(8):
         load_raw(first_plan, h, 0).start()
-    vraw[:, vec_size:] = jnp.zeros((1, vec_rows * LANES - vec_size), jnp.bfloat16)
+    vraw[:, vec_size:] = jnp.zeros((1, vraw.shape[1] - vec_size), jnp.bfloat16)
     vec_load.wait()
-    vec_mine = vraw[...].astype(jnp.float32).reshape(vec_rows, LANES).astype(jnp.bfloat16)
-    gv_ref[...] = vec_mine
-    vrecv[me] = vec_mine
+    vsend[...] = vraw[...].astype(jnp.float32).reshape(DEVICES, vec_rows, LANES).astype(jnp.bfloat16)
+    vrecv[me] = vsend[me]
 
     def pack_all(phase, plan, next_plan, c):
         for h in range(8):
@@ -160,26 +166,38 @@
 
     pack_all(0, first_plan, direct_plan, 0)
 
-    barrier = pltpu.get_barrier_semaphore()
-    for o in range(1, DEVICES):
-        pl.semaphore_signal(barrier, inc=1, device_id=((me + o) % DEVICES,), device_id_type=MESH)
     pl.semaphore_wait(barrier, DEVICES - 1)
 
     def vec_copy(o):
+        target = (me + o) % DEVICES
         return pltpu.make_async_remote_copy(
-            src_ref=gv_ref, dst_ref=vrecv.at[me], send_sem=vec_send.at[o], recv_sem=vec_recv.at[me],
+            src_ref=vsend.at[target], dst_ref=vrecv.at[me], send_sem=vec_send.at[o], recv_sem=vec_recv.at[me],
+            device_id=(target,), device_id_type=MESH)
+
+    def part_copy(o):
+        return pltpu.make_async_remote_copy(
+            src_ref=vpart, dst_ref=vall.at[me], send_sem=part_send.at[o], recv_sem=part_recv.at[me],
             device_id=((me + o) % DEVICES,), device_id_type=MESH)
 
-    def vec_wait(o):
+    def landed(buf, sems, o):
         src = (me + o) % DEVICES
-        pltpu.make_async_copy(gv_ref, vrecv.at[src], vec_recv.at[src]).wait()
+        pltpu.make_async_copy(buf.at[src], buf.at[src], sems.at[src]).wait()
 
     for o in range(1, DEVICES):
         vec_copy(o).start()
 
     send_all(0, first_plan, 0)
     lax.fori_loop(1, CHUNKS, step(0, first_plan, direct_plan), 0)
+    for o in range(1, DEVICES):
+        landed(vrecv, vec_recv, o)
+    vec_total = vrecv[0].astype(jnp.float32)
+    for d in range(1, DEVICES):
+        vec_total = vec_total + vrecv[d].astype(jnp.float32)
+    vpart[...] = vec_total / DEVICES
+    vall[me] = vec_total / DEVICES
     lax.fori_loop(0, CHUNKS, step(1, direct_plan, None), 0)
+    for o in range(1, DEVICES):
+        part_copy(o).start()
 
     def got(buf, sems, slot, c):
         at = buf.at[(*slot, pl.ds(pl.multiple_of(c * rows, rows), rows))]
@@ -214,14 +232,17 @@
 
     lax.fori_loop(0, CHUNKS, relay_step, 0)
 
-    for o in range(1, DEVICES):
-        vec_wait(o)
-    vec_total = vrecv[0].astype(jnp.float32)
-    for d in range(1, DEVICES):
-        vec_total = vec_total + vrecv[d].astype(jnp.float32)
-    vec_mean = vec_total / DEVICES
-    vsum_ref[...] = vec_mean
     fsum_copy(1, CHUNKS - 1).start()
+    for o in range(1, DEVICES):
+        landed(vall, part_recv, o)
+    vec_norm = jnp.sum((vall[...] * vall[...]).reshape(-1, 8, LANES), axis=0)
+    vec_out = pltpu.make_async_copy(vall, vsum_ref, late_sem.at[0])
+    vec_out.start()
+    head_rows = head.shape[0]
+    head_loads = [pltpu.make_async_copy(ref.at[pl.ds(0, head_rows)], head_state.at[k], head_sem.at[k])
+                  for k, ref in enumerate((p_ref, m_ref, v_ref))]
+    for load in head_loads:
+        load.start()
 
     def out_copy(side, c):
         at = pl.ds(pl.multiple_of(c * rows, rows), rows)
@@ -269,10 +290,6 @@
             src_ref=nsend, dst_ref=nrecv.at[me], send_sem=nrm_send.at[o], recv_sem=nrm_recv.at[me],
             device_id=((me + o) % DEVICES,), device_id_type=MESH)
 
-    def nrm_wait(o):
-        src = (me + o) % DEVICES
-        pltpu.make_async_copy(nsend, nrecv.at[src], nrm_recv.at[src]).wait()
-
     for o in range(1, DEVICES):
         nrm_copy(o).start()
 
@@ -285,34 +302,60 @@
     lax.fori_loop(0, CHUNKS, drain_rest, 0)
     for o in range(1, DEVICES):
         vec_copy(o).wait_send()
-    for o in range(1, DEVICES):
-        nrm_wait(o)
-    tile = jnp.sum((vec_mean * vec_mean).reshape(-1, 8, LANES), axis=0)
+        part_copy(o).wait_send()
+    for o in range(1, DEVICES):
+        landed(nrecv, nrm_recv, o)
+    tile = vec_norm
     for d in range(DEVICES):
         tile = tile + nrecv[d]
     norm_sq = jnp.full((8, LANES), jnp.sum(tile), jnp.float32)
-    clip_ref[...] = jnp.minimum(1.0, MAX_NORM / (jnp.sqrt(norm_sq) + NORM_EPS))
+    clip_tile = jnp.minimum(1.0, MAX_NORM / (jnp.sqrt(norm_sq) + NORM_EPS))
+    clip[...] = clip_tile
+
+    def head_copy(i):
+        at = pl.ds(i * HEAD_ROWS, HEAD_ROWS)
+        return pltpu.make_async_copy(head.at[at], head_ref.at[at], head_sem.at[3 + i])
+
+    for load in head_loads:
+        load.wait()
+    clip_out = pltpu.make_async_copy(clip, clip_ref, late_sem.at[1])
+    count = head_rows // HEAD_ROWS
+    for i in range(count):
+        at = pl.ds(i * HEAD_ROWS, HEAD_ROWS)
+        new_p, _, _ = adam_update(psum[0, at, :] * clip_tile[0:1, :], head_state[0, at, :], head_state[1, at, :],
+                                  head_state[2, at, :], lr_ref[0], WEIGHT_DECAY)
+        head[at, :] = new_p.astype(jnp.bfloat16)
+        if i == 0:
+            clip_out.start()
+        else:
+            head_copy(i - 1).start()
     for o in range(1, DEVICES):
         nrm_copy(o).wait_send()
-
-
-def reduce_gradients(axis_name, g_mat, g_vec):
+    vec_out.wait()
+    head_copy(count - 1).start()
+    clip_out.wait()
+    for i in range(count):
+        head_copy(i).wait()
+
+
+def reduce_gradients(axis_name, learn_rate, g_mat, g_vec, params):
     half_rows = g_mat.shape[1] // (2 * DEVICES * LANES)
     rows = half_rows // CHUNKS
-    vec_rows = -(-g_vec.shape[1] // (16 * LANES)) * 16
+    vec_rows = -(-g_vec.shape[1] // (8 * LANES * DEVICES)) * 8
     bf16, f32 = jnp.bfloat16, jnp.float32
     dma = pltpu.SemaphoreType.DMA
-    hbm, vmem = pl.BlockSpec(memory_space=pltpu.HBM), pl.BlockSpec(memory_space=pltpu.VMEM)
+    hbm = pl.BlockSpec(memory_space=pltpu.HBM)
     return pl.pallas_call(
         functools.partial(reduce_kernel, axis_name, half_rows),
         out_shape=(
             jax.ShapeDtypeStruct((2 * half_rows, LANES), f32),
-            jax.ShapeDtypeStruct((vec_rows, LANES), f32),
+            jax.ShapeDtypeStruct((DEVICES, vec_rows, LANES), f32),
             jax.ShapeDtypeStruct((8, LANES), f32),
+            jax.ShapeDtypeStruct((SIZES[0], LANES), bf16),
             jax.ShapeDtypeStruct((12, half_rows, LANES), bf16),
         ),
-        in_specs=[hbm, hbm],
-        out_specs=(hbm, vmem, vmem, hbm),
+        in_specs=[pl.BlockSpec(memory_space=pltpu.SMEM)] + [hbm] * 5,
+        out_specs=(hbm,) * 5,
         scratch_shapes=[
             pltpu.VMEM((2, 3, half_rows, LANES), bf16),
             pltpu.VMEM((2, half_rows, LANES), bf16),
@@ -322,11 +365,16 @@
             pltpu.VMEM((2, half_rows, LANES), f32),
             pltpu.VMEM((8, 1, rows * LANES), bf16),
             pltpu.VMEM((6, rows, LANES), bf16),
-            pltpu.VMEM((1, vec_rows * LANES), bf16),
-            pltpu.VMEM((vec_rows, LANES), bf16),
+            pltpu.VMEM((1, DEVICES * vec_rows * LANES), bf16),
             pltpu.VMEM((DEVICES, vec_rows, LANES), bf16),
+            pltpu.VMEM((DEVICES, vec_rows, LANES), bf16),
+            pltpu.VMEM((vec_rows, LANES), f32),
+            pltpu.VMEM((DEVICES, vec_rows, LANES), f32),
             pltpu.VMEM((8, LANES), f32),
             pltpu.VMEM((DEVICES, 8, LANES), f32),
+            pltpu.VMEM((8, LANES), f32),
+            pltpu.VMEM((3, SIZES[0], LANES), f32),
+            pltpu.VMEM((SIZES[0], LANES), bf16),
             dma,
             dma((8,)),
             dma((6,)),
@@ -339,13 +387,17 @@
             dma((DEVICES,)),
             dma((DEVICES,)),
             dma((DEVICES,)),
+            dma((DEVICES,)),
+            dma((DEVICES,)),
             dma((2, CHUNKS)),
+            dma((2,)),
+            dma((3 + SIZES[0] // HEAD_ROWS,)),
         ],
         compiler_params=pltpu.CompilerParams(
             collective_id=0, has_side_effects=True, vmem_limit_bytes=VMEM_ALL
         ),
         name="reduce_gradients",
-    )(g_mat, g_vec)
+    )(learn_rate, g_mat, g_vec, *params)
 
 
 def adam_kernel(start, lr_ref, clip_ref, *refs):
@@ -465,16 +517,17 @@
 
     def local_step(g_mat, g_vec, p_mat, m_mat, v_mat, p_vec, m_vec, v_vec, learn_rate):
         vec_size = g_vec.shape[1]
-        grad_mat, grad_vec, clip, _ = reduce_gradients(axis_name, g_mat, g_vec)
-        piece_rows = grad_mat.shape[0]
-        params = [array.reshape(piece_rows, LANES) for array in (p_mat, m_mat, v_mat)]
+        params = [array.reshape(-1, LANES) for array in (p_mat, m_mat, v_mat)]
+        piece_rows = params[0].shape[0]
         rate = learn_rate.reshape(1)
-
-        state, starts, own = (), [], []
-        for size in SIZES:
-            starts.append(sum(SIZES[: len(starts)]))
-            *state, narrow = adam_chunk(starts[-1], size, rate, clip, grad_mat, params, state)
-            own.append(narrow)
+        grad_mat, grad_vec, clip, head, _ = reduce_gradients(axis_name, rate, g_mat, g_vec, params)
+
+        starts = [sum(SIZES[:j]) for j in range(len(SIZES))]
+        state, own = (), [head] * len(SIZES)
+        for j in [*range(1, len(SIZES)), 0]:
+            *state, narrow = adam_chunk(starts[j], SIZES[j], rate, clip, grad_mat, params, state)
+            if j:
+                own[j] = narrow
 
         sib, from_x, from_y = [], [], []
         for chunk in own:

time: 583 us -> 593 us (1.017)
  waiting for transfers between devices: 146 us -> 157 us
    ppermute x42, waiting for transfers between devices: 146 us -> 157 us  [move(): return lax.ppermute(array, axis_name, pairs)]
  transfers between devices with their start and end apart: 42 -> 42, of which waited for: 13 -> 15; matrix products, arithmetic and copies ran while one was open for 1% -> 1% of each run, Pallas kernels for 11% -> 12%
where the time goes in v4:
time: 593 us; the launch traced here: 592 us
  Pallas kernels  403 us (68%)
  waiting for transfers between devices  157 us (26%)
  starting transfers between devices  22.3 us (4%)
    pallas_call x1, Pallas kernels, reduce_gradients(): pl.pallas_call(functools.partial(reduce_kernel, axis_name, half_rows), ou...  333 us
    ppermute x42, waiting for transfers between devices, move(): return lax.ppermute(array, axis_name, pairs)  157 us
    pallas_call x6, Pallas kernels, adam_chunk(): pl.pallas_call(functools.partial(adam_kernel, start), out_shape=(whole, w...  37.3 us
    pallas_call x7, Pallas kernels, place(): pl.pallas_call(functools.partial(place_kernel, axis_name, tuple(((who, st...  33.4 us
    ppermute x42, starting transfers between devices, move(): return lax.ppermute(array, axis_name, pairs)  22.3 us
  transfers between devices with their start and end apart: 42, of which 15 were waited for; matrix products, arithmetic and copies ran while one was open for 1% of the time, Pallas kernels for 12%

profile of v4, /device:TPU:0, one launch (start us, length us, event | category | flops | bytes accessed | tf_op | source)
XLA Modules:
  0.0 592.2 jit_solution(18091347672871483225)
XLA Ops:
  1.3 332.8 %reduce_gradients.1 = (f32[19200,128]{1,0:T(8,128)}, f32[8,24,128]{2,1,0:T(8,128)}, f32[8,128]{1,0:T(8,128)}, bf16[1440,128]{1,0:T(8,128)(2,1)}, bf16[12,9600,128]{2,1,0:T(8,128)(2,1)}) custom-call(f32[1]{0:T(128)} %bitcast.10.lr_ref, bf16[1,19660800]{1,0:T(2,128)(2,1)} %g_ref.1, bf16[1,24320]{1,0:T(2,128)(2,1)} %gv_raw_ref.1, f32[19200,128]{1,0:T(8,128)} %bitcast.18, ...), custom_call_target="tpu_custom_call" | custom-call | tf_op jit(solution)/shard_map/reduce_gradients/pallas_call | solution.py:348
  334.2 1.5 collective-permute-start.1
  336.2 4.9 shard_map.144
  341.1 9.0 %shard_map.145 = (f32[19200,128]{1,0:T(8,128)}, f32[19200,128]{1,0:T(8,128)}, f32[19200,128]{1,0:T(8,128)}, bf16[5280,128]{1,0:T(8,128)(2,1)}) custom-call(f32[1]{0:T(128)} %bitcast.12.lr_ref, f32[8,128]{1,0:T(8,128)} %get-tuple-element.34.clip_ref, ...), custom_call_target="tpu_custom_call", output_to_operand_aliasing={{0}: (6, {}), {1}: (7, {}), {2}: (8, {})} | custom-call | flops 40550400 | bytes 20275200 | tf_op jit(solution)/shard_map/pallas_call | solution.py:451
  350.1 9.6 %shard_map.146 = (f32[19200,128]{1,0:T(8,128)}, f32[19200,128]{1,0:T(8,128)}, f32[19200,128]{1,0:T(8,128)}, bf16[5760,128]{1,0:T(8,128)(2,1)}) custom-call(f32[1]{0:T(128)} %bitcast.13.lr_ref, f32[8,128]{1,0:T(8,128)} %get-tuple-element.34.clip_ref, ...), custom_call_target="tpu_custom_call", output_to_operand_aliasing={{0}: (6, {}), {1}: (7, {}), {2}: (8, {})} | custom-call | flops 44236800 | bytes 22118400 | tf_op jit(solution)/shard_map/pallas_call | solution.py:451
  359.7 5.4 shard_map.147
  365.2 4.2 shard_map.148
  369.9 1.2 collective-permute-start.26
  371.1 0.8 collective-permute-start.6
  371.9 1.5 collective-permute-start.8
  374.0 7.6 %collective-permute-done.26.refs_9_ = bf16[1440,128]{1,0:T(8,128)(2,1)S(1)} collective-permute-done((bf16[1440,128]{1,0:T(8,128)(2,1)}, bf16[1440,128]{1,0:T(8,128)(2,1)S(1)}, u32[]{:S(2)}, u32[]{:S(2)}) %collective-permute-start.26) | collective-permute-done | bytes 368672 | tf_op jit(solution)/shard_map/ppermute | solution.py:516
  381.6 13.7 %collective-permute-done.28.refs_11_ = bf16[1440,128]{1,0:T(8,128)(2,1)S(1)} collective-permute-done((bf16[1440,128]{1,0:T(8,128)(2,1)}, bf16[1440,128]{1,0:T(8,128)(2,1)S(1)}, u32[]{:S(2)}, u32[]{:S(2)}) %collective-permute-start.28) | collective-permute-done | bytes 368672 | tf_op jit(solution)/shard_map/ppermute | solution.py:516
  395.3 1.2 collective-permute-start.21
  396.5 0.8 collective-permute-start.23
  397.8 1.4 collective-permute-done.2.refs_3_
  401.2 11.3 %collective-permute-done.21.refs_3_ = bf16[2880,128]{1,0:T(8,128)(2,1)S(1)} collective-permute-done((bf16[2880,128]{1,0:T(8,128)(2,1)}, bf16[2880,128]{1,0:T(8,128)(2,1)S(1)}, u32[]{:S(2)}, u32[]{:S(2)}) %collective-permute-start.21) | collective-permute-done | bytes 737312 | tf_op jit(solution)/shard_map/ppermute | solution.py:516
  412.5 0.9 collective-permute-done.23.refs_5_
  413.5 0.8 collective-permute-start.38
  414.3 1.5 collective-permute-start.40
  415.8 9.0 %collective-permute-done.38.refs_1_ = bf16[1440,128]{1,0:T(8,128)(2,1)} collective-permute-done((bf16[1440,128]{1,0:T(8,128)(2,1)}, bf16[1440,128]{1,0:T(8,128)(2,1)}, u32[]{:S(2)}, u32[]{:S(2)}) %collective-permute-start.38) | collective-permute-done | bytes 368672 | tf_op jit(solution)/shard_map/ppermute | solution.py:516
  424.8 0.8 collective-permute-start.30
  425.6 1.5 collective-permute-start.11
  427.7 13.8 %collective-permute-done.30.refs_1_ = bf16[2400,128]{1,0:T(8,128)(2,1)S(1)} collective-permute-done((bf16[2400,128]{1,0:T(8,128)(2,1)S(1)}, bf16[2400,128]{1,0:T(8,128)(2,1)S(1)}, u32[]{:S(2)}, u32[]{:S(2)}) %collective-permute-start.30) | collective-permute-done | bytes 614432 | tf_op jit(solution)/shard_map/ppermute | solution.py:516
  441.5 0.8 collective-permute-start.16
  442.3 1.5 collective-permute-start.18
  443.8 14.6 %collective-permute-done.11.refs_3_ = bf16[5280,128]{1,0:T(8,128)(2,1)S(1)} collective-permute-done((bf16[5280,128]{1,0:T(8,128)(2,1)}, bf16[5280,128]{1,0:T(8,128)(2,1)S(1)}, u32[]{:S(2)}, u32[]{:S(2)}) %collective-permute-start.11) | collective-permute-done | bytes 1351712 | tf_op jit(solution)/shard_map/ppermute | solution.py:516
  458.4 12.1 %collective-permute-done.13.refs_5_ = bf16[5280,128]{1,0:T(8,128)(2,1)S(1)} collective-permute-done((bf16[5280,128]{1,0:T(8,128)(2,1)}, bf16[5280,128]{1,0:T(8,128)(2,1)S(1)}, u32[]{:S(2)}, u32[]{:S(2)}) %collective-permute-start.13) | collective-permute-done | bytes 1351712 | tf_op jit(solution)/shard_map/ppermute | solution.py:516
  471.0 18.5 %collective-permute-done.16.refs_3_ = bf16[5760,128]{1,0:T(8,128)(2,1)S(1)} collective-permute-done((bf16[5760,128]{1,0:T(8,128)(2,1)}, bf16[5760,128]{1,0:T(8,128)(2,1)S(1)}, u32[]{:S(2)}, u32[]{:S(2)}) %collective-permute-start.16) | collective-permute-done | bytes 1474592 | tf_op jit(solution)/shard_map/ppermute | solution.py:516
  489.5 1.2 collective-permute-start.34
  490.7 11.3 %collective-permute-done.18.refs_5_ = bf16[5760,128]{1,0:T(8,128)(2,1)S(1)} collective-permute-done((bf16[5760,128]{1,0:T(8,128)(2,1)}, bf16[5760,128]{1,0:T(8,128)(2,1)S(1)}, u32[]{:S(2)}, u32[]{:S(2)}) %collective-permute-start.18) | collective-permute-done | bytes 1474592 | tf_op jit(solution)/shard_map/ppermute | solution.py:516
  502.1 0.8 collective-permute-start.36
  502.9 1.2 collective-permute-start.32
  504.1 17.4 %collective-permute-done.36.refs_3_ = bf16[2880,128]{1,0:T(8,128)(2,1)} collective-permute-done((bf16[2880,128]{1,0:T(8,128)(2,1)S(1)}, bf16[2880,128]{1,0:T(8,128)(2,1)}, u32[]{:S(2)}, u32[]{:S(2)}) %collective-permute-start.36) | collective-permute-done | bytes 737312 | tf_op jit(solution)/shard_map/ppermute | solution.py:516
  522.1 10.3 %collective-permute-done.34.refs_1_ = bf16[5760,128]{1,0:T(8,128)(2,1)} collective-permute-done((bf16[5760,128]{1,0:T(8,128)(2,1)S(1)}, bf16[5760,128]{1,0:T(8,128)(2,1)}, u32[]{:S(2)}, u32[]{:S(2)}) %collective-permute-start.34) | collective-permute-done | bytes 1474592 | tf_op jit(solution)/shard_map/ppermute | solution.py:516
  532.4 14.5 %collective-permute-done.32.refs_3_ = bf16[5280,128]{1,0:T(8,128)(2,1)} collective-permute-done((bf16[5280,128]{1,0:T(8,128)(2,1)S(1)}, bf16[5280,128]{1,0:T(8,128)(2,1)}, u32[]{:S(2)}, u32[]{:S(2)}) %collective-permute-start.32) | collective-permute-done | bytes 1351712 | tf_op jit(solution)/shard_map/ppermute | solution.py:516
  547.0 1.1 copy-done.8
  548.6 1.2 slice.7
  549.8 1.1 copy-done.2
  550.9 1.1 copy-done.3
  552.0 2.4 multiply_subtract_fusion
  554.5 4.2 shard_map.149
  558.6 5.2 shard_map.150.refs_0_
  563.8 6.5 %shard_map.151.refs_0_ = bf16[153600,128]{1,0:T(8,128)(2,1)} custom-call(bf16[153600,128]{1,0:T(8,128)(2,1)} %shard_map.150.refs_0_, bf16[5280,128]{1,0:T(8,128)(2,1)} %get-tuple-element.57.refs_1_, bf16[5280,128]{1,0:T(8,128)(2,1)} %copy-done.4, bf16[5280,128]{1,0:T(8,128)(2,1)} %copy-done.5, ...), custom_call_target="tpu_custom_call", output_to_operand_aliasing={{}: (0, {})} | custom-call | flops 60825600 | bytes 16220160 | tf_op jit(solution)/shard_map/pallas_call | solution.py:496
  570.3 6.9 %shard_map.152.refs_0_ = bf16[153600,128]{1,0:T(8,128)(2,1)} custom-call(bf16[153600,128]{1,0:T(8,128)(2,1)} %shard_map.151.refs_0_, bf16[5760,128]{1,0:T(8,128)(2,1)} %get-tuple-element.58.refs_1_, bf16[5760,128]{1,0:T(8,128)(2,1)} %collective-permute-done.15.refs_2_, bf16[5760,128]{1,0:T(8,128)(2,1)} %copy-done, ...), custom_call_target="tpu_custom_call", output_to_operand_aliasing={{}: (0, {})} | custom-call | flops 66355200 | bytes 17694720 | tf_op jit(solution)/shard_map/pallas_call | solution.py:496
  577.2 5.7 shard_map.153.refs_0_
  582.9 3.5 shard_map.154.refs_0_
  586.5 3.5 shard_map.155.refs_0_
  590.0 2.2 shard_map.156
  (100 shorter events, 6.5 us)
Async XLA Ops:
  334.0 35.8 %collective-permute-start = (bf16[1440,128]{1,0:T(8,128)(2,1)}, bf16[1440,128]{1,0:T(8,128)(2,1)}, u32[]{:S(2)}, u32[]{:S(2)}) collective-permute-start(bf16[1440,128]{1,0:T(8,128)(2,1)} %get-tuple-element.55.refs_0_), channel_id=1, source_target_pairs={{0,1},{1,0},{2,3},{3,2},{4,5},{5,4},{6,7},{7,6}} | collective-permute-start | bytes 1105928 | tf_op jit(solution)/shard_map/ppermute | solution.py:516
  334.2 36.9 %collective-permute-start.1 = (bf16[1440,128]{1,0:T(8,128)(2,1)}, bf16[1440,128]{1,0:T(8,128)(2,1)}, u32[]{:S(2)}, u32[]{:S(2)}) collective-permute-start(bf16[1440,128]{1,0:T(8,128)(2,1)} %get-tuple-element.55.refs_0_), channel_id=1, source_target_pairs={{0,2},{1,3},{2,0},{3,1},{4,6},{5,7},{6,4},{7,5}} | collective-permute-start | bytes 1105928 | tf_op jit(solution)/shard_map/ppermute | solution.py:516
  335.7 36.2 %collective-permute-start.3 = (bf16[1440,128]{1,0:T(8,128)(2,1)}, bf16[1440,128]{1,0:T(8,128)(2,1)}, u32[]{:S(2)}, u32[]{:S(2)}) collective-permute-start(bf16[1440,128]{1,0:T(8,128)(2,1)} %get-tuple-element.55.refs_0_), channel_id=1, source_target_pairs={{0,4},{1,5},{2,6},{3,7},{4,0},{5,1},{6,2},{7,3}} | collective-permute-start | bytes 1105928 | tf_op jit(solution)/shard_map/ppermute | solution.py:516
  369.4 4.1 collective-permute-start.25
  369.4 27.1 %collective-permute-start.5 = (bf16[2400,128]{1,0:T(8,128)(2,1)}, bf16[2400,128]{1,0:T(8,128)(2,1)}, u32[]{:S(2)}, u32[]{:S(2)}) collective-permute-start(bf16[2400,128]{1,0:T(8,128)(2,1)} %get-tuple-element.56.refs_6_), channel_id=1, source_target_pairs={{0,1},{1,0},{2,3},{3,2},{4,5},{5,4},{6,7},{7,6}} | collective-permute-start | bytes 1843208 | tf_op jit(solution)/shard_map/ppermute | solution.py:516
  369.9 11.7 %collective-permute-start.26 = (bf16[1440,128]{1,0:T(8,128)(2,1)}, bf16[1440,128]{1,0:T(8,128)(2,1)S(1)}, u32[]{:S(2)}, u32[]{:S(2)}) collective-permute-start(bf16[1440,128]{1,0:T(8,128)(2,1)} %get-tuple-element.60.refs_7_), channel_id=1, source_target_pairs={{0,2},{1,3},{2,0},{3,1},{4,6},{5,7},{6,4},{7,5}} | collective-permute-start | bytes 1105928 | tf_op jit(solution)/shard_map/ppermute | solution.py:516
  371.1 26.2 %collective-permute-start.6 = (bf16[2400,128]{1,0:T(8,128)(2,1)}, bf16[2400,128]{1,0:T(8,128)(2,1)S(1)}, u32[]{:S(2)}, u32[]{:S(2)}) collective-permute-start(bf16[2400,128]{1,0:T(8,128)(2,1)} %get-tuple-element.56.refs_6_), channel_id=1, source_target_pairs={{0,2},{1,3},{2,0},{3,1},{4,6},{5,7},{6,4},{7,5}} | collective-permute-start | bytes 1843208 | tf_op jit(solution)/shard_map/ppermute | solution.py:516
  371.9 25.4 %collective-permute-start.8 = (bf16[2400,128]{1,0:T(8,128)(2,1)}, bf16[2400,128]{1,0:T(8,128)(2,1)S(1)}, u32[]{:S(2)}, u32[]{:S(2)}) collective-permute-start(bf16[2400,128]{1,0:T(8,128)(2,1)} %get-tuple-element.56.refs_6_), channel_id=1, source_target_pairs={{0,4},{1,5},{2,6},{3,7},{4,0},{5,1},{6,2},{7,3}} | collective-permute-start | bytes 1843208 | tf_op jit(solution)/shard_map/ppermute | solution.py:516
  373.4 21.8 %collective-permute-start.28 = (bf16[1440,128]{1,0:T(8,128)(2,1)}, bf16[1440,128]{1,0:T(8,128)(2,1)S(1)}, u32[]{:S(2)}, u32[]{:S(2)}) collective-permute-start(bf16[1440,128]{1,0:T(8,128)(2,1)} %get-tuple-element.60.refs_7_), channel_id=1, source_target_pairs={{0,4},{1,5},{2,6},{3,7},{4,0},{5,1},{6,2},{7,3}} | collective-permute-start | bytes 1105928 | tf_op jit(solution)/shard_map/ppermute | solution.py:516
  381.6 19.3 %collective-permute-start.20 = (bf16[2880,128]{1,0:T(8,128)(2,1)}, bf16[2880,128]{1,0:T(8,128)(2,1)S(1)}, u32[]{:S(2)}, u32[]{:S(2)}) collective-permute-start(bf16[2880,128]{1,0:T(8,128)(2,1)} %get-tuple-element.59.refs_1_), channel_id=1, source_target_pairs={{0,1},{1,0},{2,3},{3,2},{4,5},{5,4},{6,7},{7,6}} | collective-permute-start | bytes 2211848 | tf_op jit(solution)/shard_map/ppermute | solution.py:516
  395.3 17.2 %collective-permute-start.21 = (bf16[2880,128]{1,0:T(8,128)(2,1)}, bf16[2880,128]{1,0:T(8,128)(2,1)S(1)}, u32[]{:S(2)}, u32[]{:S(2)}) collective-permute-start(bf16[2880,128]{1,0:T(8,128)(2,1)} %get-tuple-element.59.refs_1_), channel_id=1, source_target_pairs={{0,2},{1,3},{2,0},{3,1},{4,6},{5,7},{6,4},{7,5}} | collective-permute-start | bytes 2211848 | tf_op jit(solution)/shard_map/ppermute | solution.py:516
  396.5 16.9 %collective-permute-start.23 = (bf16[2880,128]{1,0:T(8,128)(2,1)}, bf16[2880,128]{1,0:T(8,128)(2,1)S(1)}, u32[]{:S(2)}, u32[]{:S(2)}) collective-permute-start(bf16[2880,128]{1,0:T(8,128)(2,1)} %get-tuple-element.59.refs_1_), channel_id=1, source_target_pairs={{0,4},{1,5},{2,6},{3,7},{4,0},{5,1},{6,2},{7,3}} | collective-permute-start | bytes 2211848 | tf_op jit(solution)/shard_map/ppermute | solution.py:516
  397.3 1.9 collective-permute-start.2
  397.4 2.4 collective-permute-start.4
  399.2 14.2 %collective-permute-start.27 = (bf16[1440,128]{1,0:T(8,128)(2,1)S(1)}, bf16[1440,128]{1,0:T(8,128)(2,1)S(1)}, u32[]{:S(2)}, u32[]{:S(2)}) collective-permute-start(bf16[1440,128]{1,0:T(8,128)(2,1)S(1)} %collective-permute-done.26.refs_9_), channel_id=1, source_target_pairs={{0,1},{1,0},{2,3},{3,2},{4,5},{5,4},{6,7},{7,6}} | collective-permute-start | bytes 1105928 | tf_op jit(solution)/shard_map/ppermute | solution.py:516
  400.7 41.6 %collective-permute-start.10 = (bf16[5280,128]{1,0:T(8,128)(2,1)}, bf16[5280,128]{1,0:T(8,128)(2,1)S(1)}, u32[]{:S(2)}, u32[]{:S(2)}) collective-permute-start(bf16[5280,128]{1,0:T(8,128)(2,1)} %get-tuple-element.57.refs_1_), channel_id=1, source_target_pairs={{0,1},{1,0},{2,3},{3,2},{4,5},{5,4},{6,7},{7,6}} | collective-permute-start | bytes 4055048 | tf_op jit(solution)/shard_map/ppermute | solution.py:516
  400.9 13.4 %collective-permute-start.29 = (bf16[1440,128]{1,0:T(8,128)(2,1)S(1)}, bf16[1440,128]{1,0:T(8,128)(2,1)S(1)}, u32[]{:S(2)}, u32[]{:S(2)}) collective-permute-start(bf16[1440,128]{1,0:T(8,128)(2,1)S(1)} %collective-permute-done.28.refs_11_), channel_id=1, source_target_pairs={{0,1},{1,0},{2,3},{3,2},{4,5},{5,4},{6,7},{7,6}} | collective-permute-start | bytes 1105928 | tf_op jit(solution)/shard_map/ppermute | solution.py:516
  412.5 109.6 %copy-start.10 = (bf16[2880,128]{1,0:T(8,128)(2,1)}, bf16[2880,128]{1,0:T(8,128)(2,1)S(1)}, u32[]{:S(2)}) copy-start(bf16[2880,128]{1,0:T(8,128)(2,1)S(1)} %collective-permute-done.21.refs_3_) | copy-start | bytes 2211844
  412.5 13.1 %collective-permute-start.7 = (bf16[2400,128]{1,0:T(8,128)(2,1)S(1)}, bf16[2400,128]{1,0:T(8,128)(2,1)}, u32[]{:S(2)}, u32[]{:S(2)}) collective-permute-start(bf16[2400,128]{1,0:T(8,128)(2,1)S(1)} %collective-permute-done.6.refs_8_), channel_id=1, source_target_pairs={{0,1},{1,0},{2,3},{3,2},{4,5},{5,4},{6,7},{7,6}} | collective-permute-start | bytes 1843208 | tf_op jit(solution)/shard_map/ppermute | solution.py:516
  413.4 108.6 %copy-start.11 = (bf16[2880,128]{1,0:T(8,128)(2,1)}, bf16[2880,128]{1,0:T(8,128)(2,1)S(1)}, u32[]{:S(2)}) copy-start(bf16[2880,128]{1,0:T(8,128)(2,1)S(1)} %collective-permute-done.23.refs_5_) | copy-start | bytes 2211844
  413.4 13.7 %collective-permute-start.9 = (bf16[2400,128]{1,0:T(8,128)(2,1)S(1)}, bf16[2400,128]{1,0:T(8,128)(2,1)}, u32[]{:S(2)}, u32[]{:S(2)}) collective-permute-start(bf16[2400,128]{1,0:T(8,128)(2,1)S(1)} %collective-permute-done.8.refs_10_), channel_id=1, source_target_pairs={{0,1},{1,0},{2,3},{3,2},{4,5},{5,4},{6,7},{7,6}} | collective-permute-start | bytes 1843208 | tf_op jit(solution)/shard_map/ppermute | solution.py:516
  413.5 11.3 %collective-permute-start.38 = (bf16[1440,128]{1,0:T(8,128)(2,1)}, bf16[1440,128]{1,0:T(8,128)(2,1)}, u32[]{:S(2)}, u32[]{:S(2)}) collective-permute-start(bf16[1440,128]{1,0:T(8,128)(2,1)} %collective-permute-done.3.refs_4_), channel_id=1, source_target_pairs={{0,2},{1,3},{2,0},{3,1},{4,6},{5,7},{6,4},{7,5}} | collective-permute-start | bytes 1105928 | tf_op jit(solution)/shard_map/ppermute | solution.py:516
  414.3 11.3 %collective-permute-start.40 = (bf16[1440,128]{1,0:T(8,128)(2,1)S(1)}, bf16[1440,128]{1,0:T(8,128)(2,1)}, u32[]{:S(2)}, u32[]{:S(2)}) collective-permute-start(bf16[1440,128]{1,0:T(8,128)(2,1)S(1)} %collective-permute-done.26.refs_9_), channel_id=1, source_target_pairs={{0,4},{1,5},{2,6},{3,7},{4,0},{5,1},{6,2},{7,3}} | collective-permute-start | bytes 1105928 | tf_op jit(solution)/shard_map/ppermute | solution.py:516
  424.8 16.7 %collective-permute-start.30 = (bf16[2400,128]{1,0:T(8,128)(2,1)S(1)}, bf16[2400,128]{1,0:T(8,128)(2,1)S(1)}, u32[]{:S(2)}, u32[]{:S(2)}) collective-permute-start(bf16[2400,128]{1,0:T(8,128)(2,1)S(1)} %collective-permute-done.6.refs_8_), channel_id=1, source_target_pairs={{0,4},{1,5},{2,6},{3,7},{4,0},{5,1},{6,2},{7,3}} | collective-permute-start | bytes 1843208 | tf_op jit(solution)/shard_map/ppermute | solution.py:516
  425.6 44.9 %collective-permute-start.15 = (bf16[5760,128]{1,0:T(8,128)(2,1)}, bf16[5760,128]{1,0:T(8,128)(2,1)}, u32[]{:S(2)}, u32[]{:S(2)}) collective-permute-start(bf16[5760,128]{1,0:T(8,128)(2,1)} %get-tuple-element.58.refs_1_), channel_id=1, source_target_pairs={{0,1},{1,0},{2,3},{3,2},{4,5},{5,4},{6,7},{7,6}} | collective-permute-start | bytes 4423688 | tf_op jit(solution)/shard_map/ppermute | solution.py:516
  425.6 32.8 %collective-permute-start.11 = (bf16[5280,128]{1,0:T(8,128)(2,1)}, bf16[5280,128]{1,0:T(8,128)(2,1)S(1)}, u32[]{:S(2)}, u32[]{:S(2)}) collective-permute-start(bf16[5280,128]{1,0:T(8,128)(2,1)} %get-tuple-element.57.refs_1_), channel_id=1, source_target_pairs={{0,2},{1,3},{2,0},{3,1},{4,6},{5,7},{6,4},{7,5}} | collective-permute-start | bytes 4055048 | tf_op jit(solution)/shard_map/ppermute | solution.py:516
  427.2 43.3 %collective-permute-start.13 = (bf16[5280,128]{1,0:T(8,128)(2,1)}, bf16[5280,128]{1,0:T(8,128)(2,1)S(1)}, u32[]{:S(2)}, u32[]{:S(2)}) collective-permute-start(bf16[5280,128]{1,0:T(8,128)(2,1)} %get-tuple-element.57.refs_1_), channel_id=1, source_target_pairs={{0,4},{1,5},{2,6},{3,7},{4,0},{5,1},{6,2},{7,3}} | collective-permute-start | bytes 4055048 | tf_op jit(solution)/shard_map/ppermute | solution.py:516
  441.5 105.5 %copy-start.16 = (bf16[2400,128]{1,0:T(8,128)(2,1)}, bf16[2400,128]{1,0:T(8,128)(2,1)S(1)}, u32[]{:S(2)}) copy-start(bf16[2400,128]{1,0:T(8,128)(2,1)S(1)} %collective-permute-done.30.refs_1_) | copy-start | bytes 1843204
  441.5 48.0 %collective-permute-start.16 = (bf16[5760,128]{1,0:T(8,128)(2,1)}, bf16[5760,128]{1,0:T(8,128)(2,1)S(1)}, u32[]{:S(2)}, u32[]{:S(2)}) collective-permute-start(bf16[5760,128]{1,0:T(8,128)(2,1)} %get-tuple-element.58.refs_1_), channel_id=1, source_target_pairs={{0,2},{1,3},{2,0},{3,1},{4,6},{5,7},{6,4},{7,5}} | collective-permute-start | bytes 4423688 | tf_op jit(solution)/shard_map/ppermute | solution.py:516
  442.3 90.1 %copy-start.4 = (bf16[5280,128]{1,0:T(8,128)(2,1)}, bf16[5280,128]{1,0:T(8,128)(2,1)S(1)}, u32[]{:S(2)}) copy-start(bf16[5280,128]{1,0:T(8,128)(2,1)S(1)} %collective-permute-done.10.refs_2_) | copy-start | bytes 4055044
  442.3 59.8 %collective-permute-start.18 = (bf16[5760,128]{1,0:T(8,128)(2,1)}, bf16[5760,128]{1,0:T(8,128)(2,1)S(1)}, u32[]{:S(2)}, u32[]{:S(2)}) collective-permute-start(bf16[5760,128]{1,0:T(8,128)(2,1)} %get-tuple-element.58.refs_1_), channel_id=1, source_target_pairs={{0,4},{1,5},{2,6},{3,7},{4,0},{5,1},{6,2},{7,3}} | collective-permute-start | bytes 4423688 | tf_op jit(solution)/shard_map/ppermute | solution.py:516
  458.4 74.0 %copy-start.5 = (bf16[5280,128]{1,0:T(8,128)(2,1)}, bf16[5280,128]{1,0:T(8,128)(2,1)S(1)}, u32[]{:S(2)}) copy-start(bf16[5280,128]{1,0:T(8,128)(2,1)S(1)} %collective-permute-done.11.refs_3_) | copy-start | bytes 4055044
  458.4 44.5 %collective-permute-start.22 = (bf16[2880,128]{1,0:T(8,128)(2,1)S(1)}, bf16[2880,128]{1,0:T(8,128)(2,1)S(1)}, u32[]{:S(2)}, u32[]{:S(2)}) collective-permute-start(bf16[2880,128]{1,0:T(8,128)(2,1)S(1)} %collective-permute-done.21.refs_3_), channel_id=1, source_target_pairs={{0,1},{1,0},{2,3},{3,2},{4,5},{5,4},{6,7},{7,6}} | collective-permute-start | bytes 2211848 | tf_op jit(solution)/shard_map/ppermute | solution.py:516
  470.5 76.5 %copy-start.6 = (bf16[5280,128]{1,0:T(8,128)(2,1)}, bf16[5280,128]{1,0:T(8,128)(2,1)S(1)}, u32[]{:S(2)}) copy-start(bf16[5280,128]{1,0:T(8,128)(2,1)S(1)} %collective-permute-done.13.refs_5_) | copy-start | bytes 4055044
  470.5 32.4 %collective-permute-start.24 = (bf16[2880,128]{1,0:T(8,128)(2,1)S(1)}, bf16[2880,128]{1,0:T(8,128)(2,1)S(1)}, u32[]{:S(2)}, u32[]{:S(2)}) collective-permute-start(bf16[2880,128]{1,0:T(8,128)(2,1)S(1)} %collective-permute-done.23.refs_5_), channel_id=1, source_target_pairs={{0,1},{1,0},{2,3},{3,2},{4,5},{5,4},{6,7},{7,6}} | collective-permute-start | bytes 2211848 | tf_op jit(solution)/shard_map/ppermute | solution.py:516
  470.5 51.6 %collective-permute-start.12 = (bf16[5280,128]{1,0:T(8,128)(2,1)S(1)}, bf16[5280,128]{1,0:T(8,128)(2,1)S(1)}, u32[]{:S(2)}, u32[]{:S(2)}) collective-permute-start(bf16[5280,128]{1,0:T(8,128)(2,1)S(1)} %collective-permute-done.11.refs_3_), channel_id=1, source_target_pairs={{0,1},{1,0},{2,3},{3,2},{4,5},{5,4},{6,7},{7,6}} | collective-permute-start | bytes 4055048 | tf_op jit(solution)/shard_map/ppermute | solution.py:516
  489.5 42.9 %collective-permute-start.34 = (bf16[5760,128]{1,0:T(8,128)(2,1)S(1)}, bf16[5760,128]{1,0:T(8,128)(2,1)}, u32[]{:S(2)}, u32[]{:S(2)}) collective-permute-start(bf16[5760,128]{1,0:T(8,128)(2,1)S(1)} %collective-permute-done.16.refs_3_), channel_id=1, source_target_pairs={{0,4},{1,5},{2,6},{3,7},{4,0},{5,1},{6,2},{7,3}} | collective-permute-start | bytes 4423688 | tf_op jit(solution)/shard_map/ppermute | solution.py:516
  502.1 19.5 %collective-permute-start.36 = (bf16[2880,128]{1,0:T(8,128)(2,1)S(1)}, bf16[2880,128]{1,0:T(8,128)(2,1)}, u32[]{:S(2)}, u32[]{:S(2)}) collective-permute-start(bf16[2880,128]{1,0:T(8,128)(2,1)S(1)} %collective-permute-done.23.refs_5_), channel_id=1, source_target_pairs={{0,2},{1,3},{2,0},{3,1},{4,6},{5,7},{6,4},{7,5}} | collective-permute-start | bytes 2211848 | tf_op jit(solution)/shard_map/ppermute | solution.py:516
  502.9 18.7 %collective-permute-start.31 = (bf16[2400,128]{1,0:T(8,128)(2,1)S(1)}, bf16[2400,128]{1,0:T(8,128)(2,1)}, u32[]{:S(2)}, u32[]{:S(2)}) collective-permute-start(bf16[2400,128]{1,0:T(8,128)(2,1)S(1)} %collective-permute-done.30.refs_1_), channel_id=1, source_target_pairs={{0,1},{1,0},{2,3},{3,2},{4,5},{5,4},{6,7},{7,6}} | collective-permute-start | bytes 1843208 | tf_op jit(solution)/shard_map/ppermute | solution.py:516
  502.9 44.1 %collective-permute-start.32 = (bf16[5280,128]{1,0:T(8,128)(2,1)S(1)}, bf16[5280,128]{1,0:T(8,128)(2,1)}, u32[]{:S(2)}, u32[]{:S(2)}) collective-permute-start(bf16[5280,128]{1,0:T(8,128)(2,1)S(1)} %collective-permute-done.13.refs_5_), channel_id=1, source_target_pairs={{0,2},{1,3},{2,0},{3,1},{4,6},{5,7},{6,4},{7,5}} | collective-permute-start | bytes 4055048 | tf_op jit(solution)/shard_map/ppermute | solution.py:516
  521.5 28.2 %collective-permute-start.17 = (bf16[5760,128]{1,0:T(8,128)(2,1)S(1)}, bf16[5760,128]{1,0:T(8,128)(2,1)S(1)}, u32[]{:S(2)}, u32[]{:S(2)}) collective-permute-start(bf16[5760,128]{1,0:T(8,128)(2,1)S(1)} %collective-permute-done.16.refs_3_), channel_id=1, source_target_pairs={{0,1},{1,0},{2,3},{3,2},{4,5},{5,4},{6,7},{7,6}} | collective-permute-start | bytes 4423688 | tf_op jit(solution)/shard_map/ppermute | solution.py:516
  521.5 28.3 %collective-permute-start.19 = (bf16[5760,128]{1,0:T(8,128)(2,1)S(1)}, bf16[5760,128]{1,0:T(8,128)(2,1)S(1)}, u32[]{:S(2)}, u32[]{:S(2)}) collective-permute-start(bf16[5760,128]{1,0:T(8,128)(2,1)S(1)} %collective-permute-done.18.refs_5_), channel_id=1, source_target_pairs={{0,1},{1,0},{2,3},{3,2},{4,5},{5,4},{6,7},{7,6}} | collective-permute-start | bytes 4423688 | tf_op jit(solution)/shard_map/ppermute | solution.py:516
  522.1 24.9 %collective-permute-start.14 = (bf16[5280,128]{1,0:T(8,128)(2,1)S(1)}, bf16[5280,128]{1,0:T(8,128)(2,1)S(1)}, u32[]{:S(2)}, u32[]{:S(2)}) collective-permute-start(bf16[5280,128]{1,0:T(8,128)(2,1)S(1)} %collective-permute-done.13.refs_5_), channel_id=1, source_target_pairs={{0,1},{1,0},{2,3},{3,2},{4,5},{5,4},{6,7},{7,6}} | collective-permute-start | bytes 4055048 | tf_op jit(solution)/shard_map/ppermute | solution.py:516
  532.4 54.0 %collective-permute-start.35 = (bf16[5760,128]{1,0:T(8,128)(2,1)}, bf16[5760,128]{1,0:T(8,128)(2,1)}, u32[]{:S(2)}, u32[]{:S(2)}) collective-permute-start(bf16[5760,128]{1,0:T(8,128)(2,1)} %collective-permute-done.34.refs_1_), channel_id=1, source_target_pairs={{0,1},{1,0},{2,3},{3,2},{4,5},{5,4},{6,7},{7,6}} | collective-permute-start | bytes 4423688 | tf_op jit(solution)/shard_map/ppermute | solution.py:516
  547.0 36.0 %collective-permute-start.33 = (bf16[5280,128]{1,0:T(8,128)(2,1)}, bf16[5280,128]{1,0:T(8,128)(2,1)}, u32[]{:S(2)}, u32[]{:S(2)}) collective-permute-start(bf16[5280,128]{1,0:T(8,128)(2,1)} %collective-permute-done.32.refs_3_), channel_id=1, source_target_pairs={{0,1},{1,0},{2,3},{3,2},{4,5},{5,4},{6,7},{7,6}} | collective-permute-start | bytes 4055048 | tf_op jit(solution)/shard_map/ppermute | solution.py:516
  548.1 38.4 %collective-permute-start.37 = (bf16[2880,128]{1,0:T(8,128)(2,1)}, bf16[2880,128]{1,0:T(8,128)(2,1)}, u32[]{:S(2)}, u32[]{:S(2)}) collective-permute-start(bf16[2880,128]{1,0:T(8,128)(2,1)} %collective-permute-done.36.refs_3_), channel_id=1, source_target_pairs={{0,1},{1,0},{2,3},{3,2},{4,5},{5,4},{6,7},{7,6}} | collective-permute-start | bytes 2211848 | tf_op jit(solution)/shard_map/ppermute | solution.py:516
  549.8 40.2 %collective-permute-start.39 = (bf16[1440,128]{1,0:T(8,128)(2,1)}, bf16[1440,128]{1,0:T(8,128)(2,1)}, u32[]{:S(2)}, u32[]{:S(2)}) collective-permute-start(bf16[1440,128]{1,0:T(8,128)(2,1)} %collective-permute-done.38.refs_1_), channel_id=1, source_target_pairs={{0,1},{1,0},{2,3},{3,2},{4,5},{5,4},{6,7},{7,6}} | collective-permute-start | bytes 1105928 | tf_op jit(solution)/shard_map/ppermute | solution.py:516
  550.9 39.1 %collective-permute-start.41 = (bf16[1440,128]{1,0:T(8,128)(2,1)}, bf16[1440,128]{1,0:T(8,128)(2,1)}, u32[]{:S(2)}, u32[]{:S(2)}) collective-permute-start(bf16[1440,128]{1,0:T(8,128)(2,1)} %collective-permute-done.40.refs_3_), channel_id=1, source_target_pairs={{0,1},{1,0},{2,3},{3,2},{4,5},{5,4},{6,7},{7,6}} | collective-permute-start | bytes 1105928 | tf_op jit(solution)/shard_map/ppermute | solution.py:516
  (18 other events, 502.8 us)

commit v5 on v4

--- a/solution.py
+++ b/solution.py
@@ -25,10 +25,11 @@
 BLOCK = 160
 ADAM_ROWS = 480
 HEAD_ROWS = 480
-SIZES = (1440, 2400, 5280, 5760, 2880, 1440)
-NEAR_GROUPS = ((0, 1), (2,), (3,), (4, 5))
-FAR_GROUPS = ((1, 2), (3, 4), (0, 5))
+SIZES = (1440, 2400, 4800, 4800, 2400, 1440, 960, 960)
+NEAR_GROUPS = ((0, 1), (2,), (3,), (4, 5, 6, 7))
+FAR_GROUPS = ((2, 3), (1, 4), (0, 5), (6, 7))
 VMEM_ALL = 67043328
+VMEM_DIRECT = 20971520
 
 
 def adam_update(grad_vals, param_vals, moment_one, moment_two, learn_rate, decay_rate):
@@ -104,8 +105,8 @@
         return pltpu.make_async_remote_copy(
             src_ref=stage_at(phase, h, c),
             dst_ref=buf.at[(*slot, pl.ds(pl.multiple_of(c * rows, rows), rows))],
-            send_sem=send_sem.at[6 * phase + h, c],
-            recv_sem=sems.at[(*slot, c)],
+            send_sem=send_sem.at[6 * phase + h],
+            recv_sem=sems.at[slot],
             device_id=(target,),
             device_id_type=MESH,
         )
@@ -199,21 +200,21 @@
     for o in range(1, DEVICES):
         part_copy(o).start()
 
-    def got(buf, sems, slot, c):
-        at = buf.at[(*slot, pl.ds(pl.multiple_of(c * rows, rows), rows))]
-        pltpu.make_async_copy(at, at, sems.at[(*slot, c)]).wait()
+    def got_all(ref, sem):
+        pltpu.make_async_copy(ref, ref, sem).wait()
 
     def fsum_copy(side, c):
         at = (side, pl.ds(pl.multiple_of(c * rows, rows), rows))
         return pltpu.make_async_remote_copy(
-            src_ref=fsum.at[at], dst_ref=psum.at[at], send_sem=fsum_send.at[side, c], recv_sem=psum_recv.at[side, c],
+            src_ref=fsum.at[at], dst_ref=psum.at[at], send_sem=fsum_send.at[side], recv_sem=psum_recv.at[side, c],
             device_id=((x_mine, y_mine)[side],), device_id_type=MESH)
+
+    for side in range(2):
+        for slot in range(3):
+            got_all(first.at[side, slot], first_recv.at[side, slot])
 
     def relay_step(c, _):
         for side in range(2):
-            for slot in range(3):
-                got(first, first_recv, (side, slot), c)
-
             def body(i, _, side=side):
                 at = pl.ds(pl.multiple_of(c * rows + i * BLOCK, BLOCK), BLOCK)
                 total = first[side, 0, at, :].astype(jnp.float32) + first[side, 1, at, :].astype(jnp.float32)
@@ -247,13 +248,11 @@
     def out_copy(side, c):
         at = pl.ds(pl.multiple_of(c * rows, rows), rows)
         to = pl.ds(pl.multiple_of(side * half_rows + c * rows, rows), rows)
-        return pltpu.make_async_copy(psum.at[side, at], gsum_ref.at[to], out_sem.at[side, c])
+        return pltpu.make_async_copy(psum.at[side, at], gsum_ref.at[to], out_sem.at[side])
 
     def final_step(c, acc):
         for side in range(2):
-            got(psum, psum_recv, (side,), c)
-            for slot in range(3):
-                got(direct, direct_recv, (side, slot), c)
+            got_all(psum.at[side, pl.ds(pl.multiple_of(c * rows, rows), rows)], psum_recv.at[side, c])
 
             def body(i, acc, side=side):
                 at = pl.ds(pl.multiple_of(c * rows + i * BLOCK, BLOCK), BLOCK)
@@ -272,18 +271,16 @@
                     out_copy(1, c - 1).start()
         return acc
 
+    for side in range(2):
+        for slot in range(3):
+            got_all(direct.at[side, slot], direct_recv.at[side, slot])
     acc = lax.fori_loop(0, CHUNKS, final_step, jnp.zeros((8, LANES), jnp.float32))
     nsend[...] = acc
     nrecv[me] = acc
     out_copy(1, CHUNKS - 1).start()
 
-    def drain(c, _):
-        for h in range(6):
-            send(0, first_plan, h, c).wait_send()
-            send(1, direct_plan, h, c).wait_send()
-        return 0
-
-    lax.fori_loop(0, CHUNKS, drain, 0)
+    for k in range(12):
+        got_all(stage_ref.at[k], send_sem.at[k])
 
     def nrm_copy(o):
         return pltpu.make_async_remote_copy(
@@ -293,13 +290,9 @@
     for o in range(1, DEVICES):
         nrm_copy(o).start()
 
-    def drain_rest(c, _):
-        for side in range(2):
-            fsum_copy(side, c).wait_send()
-            out_copy(side, c).wait()
-        return 0
-
-    lax.fori_loop(0, CHUNKS, drain_rest, 0)
+    for side in range(2):
+        got_all(fsum.at[side], fsum_send.at[side])
+        got_all(psum.at[side], out_sem.at[side])
     for o in range(1, DEVICES):
         vec_copy(o).wait_send()
         part_copy(o).wait_send()
@@ -378,18 +371,18 @@
             dma,
             dma((8,)),
             dma((6,)),
-            dma((2, 3, CHUNKS)),
-            dma((2, 3, CHUNKS)),
+            dma((2, 3)),
+            dma((2, 3)),
             dma((2, CHUNKS)),
-            dma((12, CHUNKS)),
-            dma((2, CHUNKS)),
+            dma((12,)),
+            dma((2,)),
             dma((DEVICES,)),
             dma((DEVICES,)),
             dma((DEVICES,)),
             dma((DEVICES,)),
             dma((DEVICES,)),
             dma((DEVICES,)),
-            dma((2, CHUNKS)),
+            dma((2,)),
             dma((2,)),
             dma((3 + SIZES[0] // HEAD_ROWS,)),
         ],
@@ -465,9 +458,12 @@
     )(learn_rate, clip, grad, *params, *state)
 
 
-def place_kernel(axis_name, offsets, piece_rows, *refs):
+def place_kernel(axis_name, offsets, piece_rows, direct, *refs):
     count = len(offsets)
-    sources, out_ref, buffers, sems = refs[-2 * count - 3 : -count - 3], refs[-count - 3], refs[-count - 2 : -2], refs[-2:]
+    if direct:
+        sources, out_ref, sem = refs[-count - 2 : -2], refs[-2], refs[-1]
+    else:
+        sources, out_ref, buffers, sems = refs[-2 * count - 3 : -count - 3], refs[-count - 3], refs[-count - 2 : -2], refs[-2:]
     _, core, x, y, dev = places(axis_name)
     owners = {"me": dev(y, x, core), "sib": dev(y, x, 1 - core),
               "x": dev(y, 1 - x, core), "x_sib": dev(y, 1 - x, 1 - core),
@@ -477,32 +473,36 @@
     for k, (who, start) in enumerate(offsets):
         size = sources[k].shape[0]
         at = pl.multiple_of(owners[who] * piece_rows + start, 16)
+        if direct:
+            stores.append(pltpu.make_async_copy(sources[k], out_ref.at[pl.ds(at, size)], sem.at[k]))
+            continue
         loads.append(pltpu.make_async_copy(sources[k], buffers[k], sems[0].at[k]))
         stores.append(pltpu.make_async_copy(buffers[k], out_ref.at[pl.ds(at, size)], sems[1].at[k]))
     for load in loads:
         load.start()
-    for load, store in zip(loads, stores):
-        load.wait()
+    for k, store in enumerate(stores):
+        if not direct:
+            loads[k].wait()
         store.start()
     for store in stores:
         store.wait()
 
 
-def place(axis_name, piece_rows, full, items):
+def place(axis_name, piece_rows, full, items, name, direct=False):
     hbm = pl.BlockSpec(memory_space=pltpu.HBM)
     sources = [source for _, _, source in items]
     moved = sum(source.shape[0] for source in sources)
     started = () if full is None else (full,)
     return pl.pallas_call(
-        functools.partial(place_kernel, axis_name, tuple((who, start) for who, start, _ in items), piece_rows),
+        functools.partial(place_kernel, axis_name, tuple((who, start) for who, start, _ in items), piece_rows, direct),
         out_shape=jax.ShapeDtypeStruct((DEVICES * piece_rows, LANES), jnp.bfloat16),
-        in_specs=[hbm] * (len(started) + len(sources)),
+        in_specs=[hbm] * len(started) + [pl.BlockSpec(memory_space=pltpu.VMEM) if direct else hbm] * len(sources),
         out_specs=hbm,
         input_output_aliases={0: 0} if started else {},
-        scratch_shapes=[pltpu.VMEM(source.shape, jnp.bfloat16) for source in sources]
-        + [pltpu.SemaphoreType.DMA((len(sources),))] * 2,
+        scratch_shapes=[pltpu.VMEM(source.shape, jnp.bfloat16) for source in sources if not direct]
+        + [pltpu.SemaphoreType.DMA((len(sources),))] * (1 if direct else 2),
         cost_estimate=pl.CostEstimate(flops=moved * LANES * 15, bytes_accessed=moved * LANES * 4, transcendentals=0),
-        compiler_params=pltpu.CompilerParams(vmem_limit_bytes=VMEM_ALL),
+        compiler_params=pltpu.CompilerParams(vmem_limit_bytes=VMEM_DIRECT if direct or name == "near_3" else VMEM_ALL),
     )(*started, *sources)
 
 
@@ -542,10 +542,11 @@
                          ("y", start, from_y[j]), ("y_sib", start, move(from_y[j], to_sib))])
             far.append([("d", start, diag), ("d_sib", start, move(diag, to_sib))])
         full = None
-        for group in NEAR_GROUPS:
-            full = place(axis_name, piece_rows, full, sum((near[j] for j in group), []))
-        for group in FAR_GROUPS:
-            full = place(axis_name, piece_rows, full, sum((far[j] for j in group), []))
+        for k, group in enumerate(NEAR_GROUPS):
+            full = place(axis_name, piece_rows, full, sum((near[j] for j in group), []), f"near_{k}")
+        for k, group in enumerate(FAR_GROUPS):
+            full = place(axis_name, piece_rows, full, sum((far[j] for j in group), []), f"far_{k}",
+                         direct=True)
 
         grad_vec = grad_vec.reshape(-1)[:vec_size]
         new_p_vec, new_m_vec, new_v_vec = adam_update(grad_vec * clip[0, 0], p_vec, m_vec, v_vec, learn_rate, 0.0)

time: 593 us -> 629 us (1.061)
  local copies, waits for them, and re-layouts: 5.48 us -> 43.1 us
  waiting for transfers between devices: 157 us -> 144 us
    unnamed x48 -> x138, local copies, waits for them, and re-layouts: 4.28 us -> 41.9 us
    ppermute x42 -> x56, waiting for transfers between devices: 157 us -> 144 us  [move(): return lax.ppermute(array, axis_name, pairs)]
    pallas_call x6 -> x8, Pallas kernels: 37.3 us -> 42.9 us  [adam_chunk(): pl.pallas_call(functools.partial(adam_kernel, start), out_shape=(whole, w...]
    ppermute x42 -> x56, starting transfers between devices: 22.3 us -> 26.7 us  [move(): return lax.ppermute(array, axis_name, pairs)]
    pallas_call x7 -> x8, Pallas kernels: 33.4 us -> 36.3 us  [place(): pl.pallas_call(functools.partial(place_kernel, axis_name, tuple(((who, st...]
  transfers between devices with their start and end apart: 42 -> 56, of which waited for: 15 -> 23; matrix products, arithmetic and copies ran while one was open for 1% -> 1% of each run, Pallas kernels for 12% -> 7%
where the time goes in v5:
time: 629 us; the launch traced here: 627 us
  Pallas kernels  409 us (65%)
  waiting for transfers between devices  144 us (23%)
  local copies, waits for them, and re-layouts  43.1 us (7%)
  starting transfers between devices  26.7 us (4%)
    pallas_call x1, Pallas kernels, reduce_gradients(): pl.pallas_call(functools.partial(reduce_kernel, axis_name, half_rows), ou...  330 us
    ppermute x56, waiting for transfers between devices, move(): return lax.ppermute(array, axis_name, pairs)  144 us
    pallas_call x8, Pallas kernels, adam_chunk(): pl.pallas_call(functools.partial(adam_kernel, start), out_shape=(whole, w...  42.9 us
    unnamed x138, local copies, waits for them, and re-layouts  41.9 us
    pallas_call x8, Pallas kernels, place(): pl.pallas_call(functools.partial(place_kernel, axis_name, tuple(((who, st...  36.3 us
    ppermute x56, starting transfers between devices, move(): return lax.ppermute(array, axis_name, pairs)  26.7 us
  transfers between devices with their start and end apart: 56, of which 23 were waited for; matrix products, arithmetic and copies ran while one was open for 1% of the time, Pallas kernels for 7%

profile of v5, /device:TPU:0, one launch (start us, length us, event | category | flops | bytes accessed | tf_op | source)
XLA Modules:
  0.0 627.1 jit_solution(7350490598994115548)
XLA Ops:
  1.3 329.8 %reduce_gradients.1 = (f32[19200,128]{1,0:T(8,128)}, f32[8,24,128]{2,1,0:T(8,128)}, f32[8,128]{1,0:T(8,128)}, bf16[1440,128]{1,0:T(8,128)(2,1)}, bf16[12,9600,128]{2,1,0:T(8,128)(2,1)}) custom-call(f32[1]{0:T(128)} %bitcast.10.lr_ref, bf16[1,19660800]{1,0:T(2,128)(2,1)} %g_ref.1, bf16[1,24320]{1,0:T(2,128)(2,1)} %gv_raw_ref.1, f32[19200,128]{1,0:T(8,128)} %bitcast.20, ...), custom_call_target="tpu_custom_call" | custom-call | tf_op jit(solution)/shard_map/reduce_gradients/pallas_call | solution.py:341
  331.1 4.9 shard_map.144
  336.0 8.5 %shard_map.145 = (f32[19200,128]{1,0:T(8,128)}, f32[19200,128]{1,0:T(8,128)}, f32[19200,128]{1,0:T(8,128)}, bf16[4800,128]{1,0:T(8,128)(2,1)}) custom-call(f32[1]{0:T(128)} %bitcast.12.lr_ref, f32[8,128]{1,0:T(8,128)} %get-tuple-element.42.clip_ref, ...), custom_call_target="tpu_custom_call", output_to_operand_aliasing={{0}: (6, {}), {1}: (7, {}), {2}: (8, {})} | custom-call | flops 36864000 | bytes 18432000 | tf_op jit(solution)/shard_map/pallas_call | solution.py:444
  344.6 8.5 %shard_map.146 = (f32[19200,128]{1,0:T(8,128)}, f32[19200,128]{1,0:T(8,128)}, f32[19200,128]{1,0:T(8,128)}, bf16[4800,128]{1,0:T(8,128)(2,1)}) custom-call(f32[1]{0:T(128)} %bitcast.13.lr_ref, f32[8,128]{1,0:T(8,128)} %get-tuple-element.42.clip_ref, ...), custom_call_target="tpu_custom_call", output_to_operand_aliasing={{0}: (6, {}), {1}: (7, {}), {2}: (8, {})} | custom-call | flops 36864000 | bytes 18432000 | tf_op jit(solution)/shard_map/pallas_call | solution.py:444
  353.1 4.9 shard_map.147
  358.0 4.2 shard_map.148
  362.2 3.8 shard_map.149
  366.2 1.5 collective-permute-start.31
  368.2 3.8 shard_map.150
  372.5 1.2 collective-permute-start.36
  377.5 1.5 collective-permute-start.3
  379.0 2.6 collective-permute-done.36.refs_21_
  381.6 2.2 collective-permute-done.38.refs_23_
  383.8 1.5 collective-permute-start.26
  385.8 3.7 collective-permute-done.1.refs_2_
  389.5 2.2 collective-permute-done.3.refs_4_
  392.9 3.5 collective-permute-done.26.refs_9_
  396.4 1.7 collective-permute-done.28.refs_11_
  399.6 1.5 collective-permute-start.52
  403.7 1.2 collective-permute-start.6
  406.4 2.3 collective-permute-done.52.refs_1_
  408.7 2.0 collective-permute-done.54.refs_3_
  411.2 1.2 collective-permute-start.23
  412.4 9.3 %collective-permute-done.6.refs_8_ = bf16[2400,128]{1,0:T(8,128)(2,1)S(1)} collective-permute-done((bf16[2400,128]{1,0:T(8,128)(2,1)}, bf16[2400,128]{1,0:T(8,128)(2,1)S(1)}, u32[]{:S(2)}, u32[]{:S(2)}) %collective-permute-start.6) | collective-permute-done | bytes 614432 | tf_op jit(solution)/shard_map/ppermute | solution.py:516
  421.8 2.0 collective-permute-done.8.refs_10_
  425.2 9.3 %collective-permute-done.21.refs_3_ = bf16[2400,128]{1,0:T(8,128)(2,1)S(1)} collective-permute-done((bf16[2400,128]{1,0:T(8,128)(2,1)}, bf16[2400,128]{1,0:T(8,128)(2,1)S(1)}, u32[]{:S(2)}, u32[]{:S(2)}) %collective-permute-start.21) | collective-permute-done | bytes 614432 | tf_op jit(solution)/shard_map/ppermute | solution.py:516
  434.5 1.7 collective-permute-done.23.refs_5_
  439.5 1.5 collective-permute-start.11
  441.0 7.5 %collective-permute-done.48.refs_1_ = bf16[1440,128]{1,0:T(8,128)(2,1)} collective-permute-done((bf16[1440,128]{1,0:T(8,128)(2,1)S(1)}, bf16[1440,128]{1,0:T(8,128)(2,1)}, u32[]{:S(2)}, u32[]{:S(2)}) %collective-permute-start.48) | collective-permute-done | bytes 368672 | tf_op jit(solution)/shard_map/ppermute | solution.py:516
  449.8 8.5 %collective-permute-done.50.refs_3_ = bf16[1440,128]{1,0:T(8,128)(2,1)} collective-permute-done((bf16[1440,128]{1,0:T(8,128)(2,1)S(1)}, bf16[1440,128]{1,0:T(8,128)(2,1)}, u32[]{:S(2)}, u32[]{:S(2)}) %collective-permute-start.50) | collective-permute-done | bytes 368672 | tf_op jit(solution)/shard_map/ppermute | solution.py:516
  459.7 1.2 collective-permute-start.16
  461.9 12.8 %collective-permute-done.11.refs_3_ = bf16[4800,128]{1,0:T(8,128)(2,1)S(1)} collective-permute-done((bf16[4800,128]{1,0:T(8,128)(2,1)}, bf16[4800,128]{1,0:T(8,128)(2,1)S(1)}, u32[]{:S(2)}, u32[]{:S(2)}) %collective-permute-start.11) | collective-permute-done | bytes 1228832 | tf_op jit(solution)/shard_map/ppermute | solution.py:516
  475.6 12.8 %collective-permute-done.13.refs_5_ = bf16[4800,128]{1,0:T(8,128)(2,1)S(1)} collective-permute-done((bf16[4800,128]{1,0:T(8,128)(2,1)}, bf16[4800,128]{1,0:T(8,128)(2,1)S(1)}, u32[]{:S(2)}, u32[]{:S(2)}) %collective-permute-start.13) | collective-permute-done | bytes 1228832 | tf_op jit(solution)/shard_map/ppermute | solution.py:516
  489.0 11.7 %collective-permute-done.16.refs_3_ = bf16[4800,128]{1,0:T(8,128)(2,1)S(1)} collective-permute-done((bf16[4800,128]{1,0:T(8,128)(2,1)}, bf16[4800,128]{1,0:T(8,128)(2,1)S(1)}, u32[]{:S(2)}, u32[]{:S(2)}) %collective-permute-start.16) | collective-permute-done | bytes 1228832 | tf_op jit(solution)/shard_map/ppermute | solution.py:516
  500.6 14.1 %collective-permute-done.18.refs_5_ = bf16[4800,128]{1,0:T(8,128)(2,1)S(1)} collective-permute-done((bf16[4800,128]{1,0:T(8,128)(2,1)}, bf16[4800,128]{1,0:T(8,128)(2,1)S(1)}, u32[]{:S(2)}, u32[]{:S(2)}) %collective-permute-start.18) | collective-permute-done | bytes 1228832 | tf_op jit(solution)/shard_map/ppermute | solution.py:516
  519.8 8.1 %collective-permute-done.44.refs_1_ = bf16[2400,128]{1,0:T(8,128)(2,1)S(1)} collective-permute-done((bf16[2400,128]{1,0:T(8,128)(2,1)S(1)}, bf16[2400,128]{1,0:T(8,128)(2,1)S(1)}, u32[]{:S(2)}, u32[]{:S(2)}) %collective-permute-start.44) | collective-permute-done | bytes 614432 | tf_op jit(solution)/shard_map/ppermute | solution.py:516
  528.8 23.0 %collective-permute-done.46.refs_3_ = bf16[2400,128]{1,0:T(8,128)(2,1)} collective-permute-done((bf16[2400,128]{1,0:T(8,128)(2,1)S(1)}, bf16[2400,128]{1,0:T(8,128)(2,1)}, u32[]{:S(2)}, u32[]{:S(2)}) %collective-permute-start.46) | collective-permute-done | bytes 614432 | tf_op jit(solution)/shard_map/ppermute | solution.py:516
  558.6 1.4 collective-permute-done.41.refs_2_
  563.0 2.4 multiply_subtract_fusion
  565.5 4.2 shard_map.151
  569.7 5.2 shard_map.152.refs_0_
  574.8 6.0 shard_map.153.refs_0_
  580.9 6.0 shard_map.154.refs_0_
  607.8 9.3 %shard_map.155.refs_0_ = bf16[153600,128]{1,0:T(8,128)(2,1)} custom-call(bf16[153600,128]{1,0:T(8,128)(2,1)} %shard_map.154.refs_0_, bf16[2400,128]{1,0:T(8,128)(2,1)S(1)} %copy-done.8, bf16[2400,128]{1,0:T(8,128)(2,1)S(1)} %copy-done.10, bf16[2400,128]{1,0:T(8,128)(2,1)S(1)} %copy-done.12, ...), custom_call_target="tpu_custom_call", output_to_operand_aliasing={{}: (0, {})} | custom-call | flops 66355200 | bytes 17694720 | tf_op jit(solution)/shard_map/pallas_call | solution.py:496
  617.2 2.3 shard_map.156.refs_0_
  619.5 2.7 shard_map.157.refs_0_
  622.3 2.5 shard_map.158.refs_0_
  624.8 2.3 shard_map.159
  (221 shorter events, 59.2 us)
Async XLA Ops:
  366.0 6.5 %collective-permute-start.30 = (bf16[960,128]{1,0:T(8,128)(2,1)}, bf16[960,128]{1,0:T(8,128)(2,1)}, u32[]{:S(2)}, u32[]{:S(2)}) collective-permute-start(bf16[960,128]{1,0:T(8,128)(2,1)} %get-tuple-element.75.refs_13_), channel_id=1, source_target_pairs={{0,1},{1,0},{2,3},{3,2},{4,5},{5,4},{6,7},{7,6}} | collective-permute-start | bytes 737288 | tf_op jit(solution)/shard_map/ppermute | solution.py:516
  366.2 8.6 %collective-permute-start.31 = (bf16[960,128]{1,0:T(8,128)(2,1)}, bf16[960,128]{1,0:T(8,128)(2,1)}, u32[]{:S(2)}, u32[]{:S(2)}) collective-permute-start(bf16[960,128]{1,0:T(8,128)(2,1)} %get-tuple-element.75.refs_13_), channel_id=1, source_target_pairs={{0,2},{1,3},{2,0},{3,1},{4,6},{5,7},{6,4},{7,5}} | collective-permute-start | bytes 737288 | tf_op jit(solution)/shard_map/ppermute | solution.py:516
  367.7 8.3 %collective-permute-start.33 = (bf16[960,128]{1,0:T(8,128)(2,1)}, bf16[960,128]{1,0:T(8,128)(2,1)}, u32[]{:S(2)}, u32[]{:S(2)}) collective-permute-start(bf16[960,128]{1,0:T(8,128)(2,1)} %get-tuple-element.75.refs_13_), channel_id=1, source_target_pairs={{0,4},{1,5},{2,6},{3,7},{4,0},{5,1},{6,2},{7,3}} | collective-permute-start | bytes 737288 | tf_op jit(solution)/shard_map/ppermute | solution.py:516
  368.2 17.1 %collective-permute-start = (bf16[1440,128]{1,0:T(8,128)(2,1)}, bf16[1440,128]{1,0:T(8,128)(2,1)}, u32[]{:S(2)}, u32[]{:S(2)}) collective-permute-start(bf16[1440,128]{1,0:T(8,128)(2,1)} %get-tuple-element.69.refs_0_), channel_id=1, source_target_pairs={{0,1},{1,0},{2,3},{3,2},{4,5},{5,4},{6,7},{7,6}} | collective-permute-start | bytes 1105928 | tf_op jit(solution)/shard_map/ppermute | solution.py:516
  372.5 9.0 %collective-permute-start.36 = (bf16[960,128]{1,0:T(8,128)(2,1)}, bf16[960,128]{1,0:T(8,128)(2,1)S(1)}, u32[]{:S(2)}, u32[]{:S(2)}) collective-permute-start(bf16[960,128]{1,0:T(8,128)(2,1)} %get-tuple-element.76.refs_19_), channel_id=1, source_target_pairs={{0,2},{1,3},{2,0},{3,1},{4,6},{5,7},{6,4},{7,5}} | collective-permute-start | bytes 737288 | tf_op jit(solution)/shard_map/ppermute | solution.py:516
  374.7 9.0 %collective-permute-start.38 = (bf16[960,128]{1,0:T(8,128)(2,1)}, bf16[960,128]{1,0:T(8,128)(2,1)S(1)}, u32[]{:S(2)}, u32[]{:S(2)}) collective-permute-start(bf16[960,128]{1,0:T(8,128)(2,1)} %get-tuple-element.76.refs_19_), channel_id=1, source_target_pairs={{0,4},{1,5},{2,6},{3,7},{4,0},{5,1},{6,2},{7,3}} | collective-permute-start | bytes 737288 | tf_op jit(solution)/shard_map/ppermute | solution.py:516
  376.0 13.5 %collective-permute-start.1 = (bf16[1440,128]{1,0:T(8,128)(2,1)}, bf16[1440,128]{1,0:T(8,128)(2,1)S(1)}, u32[]{:S(2)}, u32[]{:S(2)}) collective-permute-start(bf16[1440,128]{1,0:T(8,128)(2,1)} %get-tuple-element.69.refs_0_), channel_id=1, source_target_pairs={{0,2},{1,3},{2,0},{3,1},{4,6},{5,7},{6,4},{7,5}} | collective-permute-start | bytes 1105928 | tf_op jit(solution)/shard_map/ppermute | solution.py:516
  377.5 14.2 %collective-permute-start.3 = (bf16[1440,128]{1,0:T(8,128)(2,1)}, bf16[1440,128]{1,0:T(8,128)(2,1)S(1)}, u32[]{:S(2)}, u32[]{:S(2)}) collective-permute-start(bf16[1440,128]{1,0:T(8,128)(2,1)} %get-tuple-element.69.refs_0_), channel_id=1, source_target_pairs={{0,4},{1,5},{2,6},{3,7},{4,0},{5,1},{6,2},{7,3}} | collective-permute-start | bytes 1105928 | tf_op jit(solution)/shard_map/ppermute | solution.py:516
  381.6 10.1 %collective-permute-start.25 = (bf16[1440,128]{1,0:T(8,128)(2,1)}, bf16[1440,128]{1,0:T(8,128)(2,1)S(1)}, u32[]{:S(2)}, u32[]{:S(2)}) collective-permute-start(bf16[1440,128]{1,0:T(8,128)(2,1)} %get-tuple-element.74.refs_7_), channel_id=1, source_target_pairs={{0,1},{1,0},{2,3},{3,2},{4,5},{5,4},{6,7},{7,6}} | collective-permute-start | bytes 1105928 | tf_op jit(solution)/shard_map/ppermute | solution.py:516
  383.8 12.7 %collective-permute-start.26 = (bf16[1440,128]{1,0:T(8,128)(2,1)}, bf16[1440,128]{1,0:T(8,128)(2,1)S(1)}, u32[]{:S(2)}, u32[]{:S(2)}) collective-permute-start(bf16[1440,128]{1,0:T(8,128)(2,1)} %get-tuple-element.74.refs_7_), channel_id=1, source_target_pairs={{0,2},{1,3},{2,0},{3,1},{4,6},{5,7},{6,4},{7,5}} | collective-permute-start | bytes 1105928 | tf_op jit(solution)/shard_map/ppermute | solution.py:516
  385.3 12.9 %collective-permute-start.28 = (bf16[1440,128]{1,0:T(8,128)(2,1)}, bf16[1440,128]{1,0:T(8,128)(2,1)S(1)}, u32[]{:S(2)}, u32[]{:S(2)}) collective-permute-start(bf16[1440,128]{1,0:T(8,128)(2,1)} %get-tuple-element.74.refs_7_), channel_id=1, source_target_pairs={{0,4},{1,5},{2,6},{3,7},{4,0},{5,1},{6,2},{7,3}} | collective-permute-start | bytes 1105928 | tf_op jit(solution)/shard_map/ppermute | solution.py:516
  389.5 21.8 %collective-permute-start.5 = (bf16[2400,128]{1,0:T(8,128)(2,1)}, bf16[2400,128]{1,0:T(8,128)(2,1)S(1)}, u32[]{:S(2)}, u32[]{:S(2)}) collective-permute-start(bf16[2400,128]{1,0:T(8,128)(2,1)} %get-tuple-element.70.refs_6_), channel_id=1, source_target_pairs={{0,1},{1,0},{2,3},{3,2},{4,5},{5,4},{6,7},{7,6}} | collective-permute-start | bytes 1843208 | tf_op jit(solution)/shard_map/ppermute | solution.py:516
  391.7 7.2 %collective-permute-start.32 = (bf16[960,128]{1,0:T(8,128)(2,1)}, bf16[960,128]{1,0:T(8,128)(2,1)S(1)}, u32[]{:S(2)}, u32[]{:S(2)}) collective-permute-start(bf16[960,128]{1,0:T(8,128)(2,1)} %collective-permute-done.31.refs_15_), channel_id=1, source_target_pairs={{0,1},{1,0},{2,3},{3,2},{4,5},{5,4},{6,7},{7,6}} | collective-permute-start | bytes 737288 | tf_op jit(solution)/shard_map/ppermute | solution.py:516
  392.5 8.6 %collective-permute-start.34 = (bf16[960,128]{1,0:T(8,128)(2,1)}, bf16[960,128]{1,0:T(8,128)(2,1)S(1)}, u32[]{:S(2)}, u32[]{:S(2)}) collective-permute-start(bf16[960,128]{1,0:T(8,128)(2,1)} %collective-permute-done.33.refs_17_), channel_id=1, source_target_pairs={{0,1},{1,0},{2,3},{3,2},{4,5},{5,4},{6,7},{7,6}} | collective-permute-start | bytes 737288 | tf_op jit(solution)/shard_map/ppermute | solution.py:516
  396.4 6.5 %collective-permute-start.37 = (bf16[960,128]{1,0:T(8,128)(2,1)S(1)}, bf16[960,128]{1,0:T(8,128)(2,1)S(1)}, u32[]{:S(2)}, u32[]{:S(2)}) collective-permute-start(bf16[960,128]{1,0:T(8,128)(2,1)S(1)} %collective-permute-done.36.refs_21_), channel_id=1, source_target_pairs={{0,1},{1,0},{2,3},{3,2},{4,5},{5,4},{6,7},{7,6}} | collective-permute-start | bytes 737288 | tf_op jit(solution)/shard_map/ppermute | solution.py:516
  398.1 6.7 %collective-permute-start.39 = (bf16[960,128]{1,0:T(8,128)(2,1)S(1)}, bf16[960,128]{1,0:T(8,128)(2,1)S(1)}, u32[]{:S(2)}, u32[]{:S(2)}) collective-permute-start(bf16[960,128]{1,0:T(8,128)(2,1)S(1)} %collective-permute-done.38.refs_23_), channel_id=1, source_target_pairs={{0,1},{1,0},{2,3},{3,2},{4,5},{5,4},{6,7},{7,6}} | collective-permute-start | bytes 737288 | tf_op jit(solution)/shard_map/ppermute | solution.py:516
  399.6 9.1 %collective-permute-start.52 = (bf16[960,128]{1,0:T(8,128)(2,1)}, bf16[960,128]{1,0:T(8,128)(2,1)}, u32[]{:S(2)}, u32[]{:S(2)}) collective-permute-start(bf16[960,128]{1,0:T(8,128)(2,1)} %collective-permute-done.33.refs_17_), channel_id=1, source_target_pairs={{0,2},{1,3},{2,0},{3,1},{4,6},{5,7},{6,4},{7,5}} | collective-permute-start | bytes 737288 | tf_op jit(solution)/shard_map/ppermute | solution.py:516
  401.8 8.9 %collective-permute-start.54 = (bf16[960,128]{1,0:T(8,128)(2,1)S(1)}, bf16[960,128]{1,0:T(8,128)(2,1)}, u32[]{:S(2)}, u32[]{:S(2)}) collective-permute-start(bf16[960,128]{1,0:T(8,128)(2,1)S(1)} %collective-permute-done.36.refs_21_), channel_id=1, source_target_pairs={{0,4},{1,5},{2,6},{3,7},{4,0},{5,1},{6,2},{7,3}} | collective-permute-start | bytes 737288 | tf_op jit(solution)/shard_map/ppermute | solution.py:516
  403.7 18.1 %collective-permute-start.6 = (bf16[2400,128]{1,0:T(8,128)(2,1)}, bf16[2400,128]{1,0:T(8,128)(2,1)S(1)}, u32[]{:S(2)}, u32[]{:S(2)}) collective-permute-start(bf16[2400,128]{1,0:T(8,128)(2,1)} %get-tuple-element.70.refs_6_), channel_id=1, source_target_pairs={{0,2},{1,3},{2,0},{3,1},{4,6},{5,7},{6,4},{7,5}} | collective-permute-start | bytes 1843208 | tf_op jit(solution)/shard_map/ppermute | solution.py:516
  405.6 18.2 %collective-permute-start.8 = (bf16[2400,128]{1,0:T(8,128)(2,1)}, bf16[2400,128]{1,0:T(8,128)(2,1)S(1)}, u32[]{:S(2)}, u32[]{:S(2)}) collective-permute-start(bf16[2400,128]{1,0:T(8,128)(2,1)} %get-tuple-element.70.refs_6_), channel_id=1, source_target_pairs={{0,4},{1,5},{2,6},{3,7},{4,0},{5,1},{6,2},{7,3}} | collective-permute-start | bytes 1843208 | tf_op jit(solution)/shard_map/ppermute | solution.py:516
  408.7 15.1 %collective-permute-start.20 = (bf16[2400,128]{1,0:T(8,128)(2,1)}, bf16[2400,128]{1,0:T(8,128)(2,1)S(1)}, u32[]{:S(2)}, u32[]{:S(2)}) collective-permute-start(bf16[2400,128]{1,0:T(8,128)(2,1)} %get-tuple-element.73.refs_1_), channel_id=1, source_target_pairs={{0,1},{1,0},{2,3},{3,2},{4,5},{5,4},{6,7},{7,6}} | collective-permute-start | bytes 1843208 | tf_op jit(solution)/shard_map/ppermute | solution.py:516
  410.7 23.8 %collective-permute-start.21 = (bf16[2400,128]{1,0:T(8,128)(2,1)}, bf16[2400,128]{1,0:T(8,128)(2,1)S(1)}, u32[]{:S(2)}, u32[]{:S(2)}) collective-permute-start(bf16[2400,128]{1,0:T(8,128)(2,1)} %get-tuple-element.73.refs_1_), channel_id=1, source_target_pairs={{0,2},{1,3},{2,0},{3,1},{4,6},{5,7},{6,4},{7,5}} | collective-permute-start | bytes 1843208 | tf_op jit(solution)/shard_map/ppermute | solution.py:516
  411.2 24.9 %collective-permute-start.23 = (bf16[2400,128]{1,0:T(8,128)(2,1)}, bf16[2400,128]{1,0:T(8,128)(2,1)S(1)}, u32[]{:S(2)}, u32[]{:S(2)}) collective-permute-start(bf16[2400,128]{1,0:T(8,128)(2,1)} %get-tuple-element.73.refs_1_), channel_id=1, source_target_pairs={{0,4},{1,5},{2,6},{3,7},{4,0},{5,1},{6,2},{7,3}} | collective-permute-start | bytes 1843208 | tf_op jit(solution)/shard_map/ppermute | solution.py:516
  421.8 39.1 %collective-permute-start.10 = (bf16[4800,128]{1,0:T(8,128)(2,1)}, bf16[4800,128]{1,0:T(8,128)(2,1)S(1)}, u32[]{:S(2)}, u32[]{:S(2)}) collective-permute-start(bf16[4800,128]{1,0:T(8,128)(2,1)} %get-tuple-element.71.refs_1_), channel_id=1, source_target_pairs={{0,1},{1,0},{2,3},{3,2},{4,5},{5,4},{6,7},{7,6}} | collective-permute-start | bytes 3686408 | tf_op jit(solution)/shard_map/ppermute | solution.py:516
  423.8 13.2 %collective-permute-start.2 = (bf16[1440,128]{1,0:T(8,128)(2,1)S(1)}, bf16[1440,128]{1,0:T(8,128)(2,1)S(1)}, u32[]{:S(2)}, u32[]{:S(2)}) collective-permute-start(bf16[1440,128]{1,0:T(8,128)(2,1)S(1)} %collective-permute-done.1.refs_2_), channel_id=1, source_target_pairs={{0,1},{1,0},{2,3},{3,2},{4,5},{5,4},{6,7},{7,6}} | collective-permute-start | bytes 1105928 | tf_op jit(solution)/shard_map/ppermute | solution.py:516
  424.7 12.8 %collective-permute-start.4 = (bf16[1440,128]{1,0:T(8,128)(2,1)S(1)}, bf16[1440,128]{1,0:T(8,128)(2,1)S(1)}, u32[]{:S(2)}, u32[]{:S(2)}) collective-permute-start(bf16[1440,128]{1,0:T(8,128)(2,1)S(1)} %collective-permute-done.3.refs_4_), channel_id=1, source_target_pairs={{0,1},{1,0},{2,3},{3,2},{4,5},{5,4},{6,7},{7,6}} | collective-permute-start | bytes 1105928 | tf_op jit(solution)/shard_map/ppermute | solution.py:516
  437.0 11.6 %collective-permute-start.48 = (bf16[1440,128]{1,0:T(8,128)(2,1)S(1)}, bf16[1440,128]{1,0:T(8,128)(2,1)}, u32[]{:S(2)}, u32[]{:S(2)}) collective-permute-start(bf16[1440,128]{1,0:T(8,128)(2,1)S(1)} %collective-permute-done.3.refs_4_), channel_id=1, source_target_pairs={{0,2},{1,3},{2,0},{3,1},{4,6},{5,7},{6,4},{7,5}} | collective-permute-start | bytes 1105928 | tf_op jit(solution)/shard_map/ppermute | solution.py:516
  437.5 21.3 %collective-permute-start.7 = (bf16[2400,128]{1,0:T(8,128)(2,1)S(1)}, bf16[2400,128]{1,0:T(8,128)(2,1)S(1)}, u32[]{:S(2)}, u32[]{:S(2)}) collective-permute-start(bf16[2400,128]{1,0:T(8,128)(2,1)S(1)} %collective-permute-done.6.refs_8_), channel_id=1, source_target_pairs={{0,1},{1,0},{2,3},{3,2},{4,5},{5,4},{6,7},{7,6}} | collective-permute-start | bytes 1843208 | tf_op jit(solution)/shard_map/ppermute | solution.py:516
  438.5 21.2 %collective-permute-start.9 = (bf16[2400,128]{1,0:T(8,128)(2,1)S(1)}, bf16[2400,128]{1,0:T(8,128)(2,1)S(1)}, u32[]{:S(2)}, u32[]{:S(2)}) collective-permute-start(bf16[2400,128]{1,0:T(8,128)(2,1)S(1)} %collective-permute-done.8.refs_10_), channel_id=1, source_target_pairs={{0,1},{1,0},{2,3},{3,2},{4,5},{5,4},{6,7},{7,6}} | collective-permute-start | bytes 1843208 | tf_op jit(solution)/shard_map/ppermute | solution.py:516
  439.5 35.2 %collective-permute-start.11 = (bf16[4800,128]{1,0:T(8,128)(2,1)}, bf16[4800,128]{1,0:T(8,128)(2,1)S(1)}, u32[]{:S(2)}, u32[]{:S(2)}) collective-permute-start(bf16[4800,128]{1,0:T(8,128)(2,1)} %get-tuple-element.71.refs_1_), channel_id=1, source_target_pairs={{0,2},{1,3},{2,0},{3,1},{4,6},{5,7},{6,4},{7,5}} | collective-permute-start | bytes 3686408 | tf_op jit(solution)/shard_map/ppermute | solution.py:516
  448.5 9.8 %collective-permute-start.50 = (bf16[1440,128]{1,0:T(8,128)(2,1)S(1)}, bf16[1440,128]{1,0:T(8,128)(2,1)}, u32[]{:S(2)}, u32[]{:S(2)}) collective-permute-start(bf16[1440,128]{1,0:T(8,128)(2,1)S(1)} %collective-permute-done.26.refs_9_), channel_id=1, source_target_pairs={{0,4},{1,5},{2,6},{3,7},{4,0},{5,1},{6,2},{7,3}} | collective-permute-start | bytes 1105928 | tf_op jit(solution)/shard_map/ppermute | solution.py:516
  458.3 30.1 %collective-permute-start.13 = (bf16[4800,128]{1,0:T(8,128)(2,1)}, bf16[4800,128]{1,0:T(8,128)(2,1)S(1)}, u32[]{:S(2)}, u32[]{:S(2)}) collective-permute-start(bf16[4800,128]{1,0:T(8,128)(2,1)} %get-tuple-element.71.refs_1_), channel_id=1, source_target_pairs={{0,4},{1,5},{2,6},{3,7},{4,0},{5,1},{6,2},{7,3}} | collective-permute-start | bytes 3686408 | tf_op jit(solution)/shard_map/ppermute | solution.py:516
  459.7 28.8 %collective-permute-start.15 = (bf16[4800,128]{1,0:T(8,128)(2,1)}, bf16[4800,128]{1,0:T(8,128)(2,1)S(1)}, u32[]{:S(2)}, u32[]{:S(2)}) collective-permute-start(bf16[4800,128]{1,0:T(8,128)(2,1)} %get-tuple-element.72.refs_1_), channel_id=1, source_target_pairs={{0,1},{1,0},{2,3},{3,2},{4,5},{5,4},{6,7},{7,6}} | collective-permute-start | bytes 3686408 | tf_op jit(solution)/shard_map/ppermute | solution.py:516
  459.7 41.0 %collective-permute-start.16 = (bf16[4800,128]{1,0:T(8,128)(2,1)}, bf16[4800,128]{1,0:T(8,128)(2,1)S(1)}, u32[]{:S(2)}, u32[]{:S(2)}) collective-permute-start(bf16[4800,128]{1,0:T(8,128)(2,1)} %get-tuple-element.72.refs_1_), channel_id=1, source_target_pairs={{0,2},{1,3},{2,0},{3,1},{4,6},{5,7},{6,4},{7,5}} | collective-permute-start | bytes 3686408 | tf_op jit(solution)/shard_map/ppermute | solution.py:516
  460.9 53.8 %collective-permute-start.18 = (bf16[4800,128]{1,0:T(8,128)(2,1)}, bf16[4800,128]{1,0:T(8,128)(2,1)S(1)}, u32[]{:S(2)}, u32[]{:S(2)}) collective-permute-start(bf16[4800,128]{1,0:T(8,128)(2,1)} %get-tuple-element.72.refs_1_), channel_id=1, source_target_pairs={{0,4},{1,5},{2,6},{3,7},{4,0},{5,1},{6,2},{7,3}} | collective-permute-start | bytes 3686408 | tf_op jit(solution)/shard_map/ppermute | solution.py:516
  474.8 40.5 %collective-permute-start.22 = (bf16[2400,128]{1,0:T(8,128)(2,1)S(1)}, bf16[2400,128]{1,0:T(8,128)(2,1)S(1)}, u32[]{:S(2)}, u32[]{:S(2)}) collective-permute-start(bf16[2400,128]{1,0:T(8,128)(2,1)S(1)} %collective-permute-done.21.refs_3_), channel_id=1, source_target_pairs={{0,1},{1,0},{2,3},{3,2},{4,5},{5,4},{6,7},{7,6}} | collective-permute-start | bytes 1843208 | tf_op jit(solution)/shard_map/ppermute | solution.py:516
  488.4 28.9 %collective-permute-start.24 = (bf16[2400,128]{1,0:T(8,128)(2,1)S(1)}, bf16[2400,128]{1,0:T(8,128)(2,1)S(1)}, u32[]{:S(2)}, u32[]{:S(2)}) collective-permute-start(bf16[2400,128]{1,0:T(8,128)(2,1)S(1)} %collective-permute-done.23.refs_5_), channel_id=1, source_target_pairs={{0,1},{1,0},{2,3},{3,2},{4,5},{5,4},{6,7},{7,6}} | collective-permute-start | bytes 1843208 | tf_op jit(solution)/shard_map/ppermute | solution.py:516
  488.4 39.5 %collective-permute-start.44 = (bf16[2400,128]{1,0:T(8,128)(2,1)S(1)}, bf16[2400,128]{1,0:T(8,128)(2,1)S(1)}, u32[]{:S(2)}, u32[]{:S(2)}) collective-permute-start(bf16[2400,128]{1,0:T(8,128)(2,1)S(1)} %collective-permute-done.6.refs_8_), channel_id=1, source_target_pairs={{0,4},{1,5},{2,6},{3,7},{4,0},{5,1},{6,2},{7,3}} | collective-permute-start | bytes 1843208 | tf_op jit(solution)/shard_map/ppermute | solution.py:516
  500.6 52.5 %collective-permute-start.12 = (bf16[4800,128]{1,0:T(8,128)(2,1)S(1)}, bf16[4800,128]{1,0:T(8,128)(2,1)S(1)}, u32[]{:S(2)}, u32[]{:S(2)}) collective-permute-start(bf16[4800,128]{1,0:T(8,128)(2,1)S(1)} %collective-permute-done.11.refs_3_), channel_id=1, source_target_pairs={{0,1},{1,0},{2,3},{3,2},{4,5},{5,4},{6,7},{7,6}} | collective-permute-start | bytes 3686408 | tf_op jit(solution)/shard_map/ppermute | solution.py:516
  514.8 39.4 %collective-permute-start.40 = (bf16[4800,128]{1,0:T(8,128)(2,1)S(1)}, bf16[4800,128]{1,0:T(8,128)(2,1)S(1)}, u32[]{:S(2)}, u32[]{:S(2)}) collective-permute-start(bf16[4800,128]{1,0:T(8,128)(2,1)S(1)} %collective-permute-done.13.refs_5_), channel_id=1, source_target_pairs={{0,2},{1,3},{2,0},{3,1},{4,6},{5,7},{6,4},{7,5}} | collective-permute-start | bytes 3686408 | tf_op jit(solution)/shard_map/ppermute | solution.py:516
  516.1 39.2 %collective-permute-start.42 = (bf16[4800,128]{1,0:T(8,128)(2,1)S(1)}, bf16[4800,128]{1,0:T(8,128)(2,1)S(1)}, u32[]{:S(2)}, u32[]{:S(2)}) collective-permute-start(bf16[4800,128]{1,0:T(8,128)(2,1)S(1)} %collective-permute-done.16.refs_3_), channel_id=1, source_target_pairs={{0,4},{1,5},{2,6},{3,7},{4,0},{5,1},{6,2},{7,3}} | collective-permute-start | bytes 3686408 | tf_op jit(solution)/shard_map/ppermute | solution.py:516
  518.2 33.6 %collective-permute-start.46 = (bf16[2400,128]{1,0:T(8,128)(2,1)S(1)}, bf16[2400,128]{1,0:T(8,128)(2,1)}, u32[]{:S(2)}, u32[]{:S(2)}) collective-permute-start(bf16[2400,128]{1,0:T(8,128)(2,1)S(1)} %collective-permute-done.23.refs_5_), channel_id=1, source_target_pairs={{0,2},{1,3},{2,0},{3,1},{4,6},{5,7},{6,4},{7,5}} | collective-permute-start | bytes 1843208 | tf_op jit(solution)/shard_map/ppermute | solution.py:516
  527.9 23.9 %collective-permute-start.45 = (bf16[2400,128]{1,0:T(8,128)(2,1)S(1)}, bf16[2400,128]{1,0:T(8,128)(2,1)S(1)}, u32[]{:S(2)}, u32[]{:S(2)}) collective-permute-start(bf16[2400,128]{1,0:T(8,128)(2,1)S(1)} %collective-permute-done.44.refs_1_), channel_id=1, source_target_pairs={{0,1},{1,0},{2,3},{3,2},{4,5},{5,4},{6,7},{7,6}} | collective-permute-start | bytes 1843208 | tf_op jit(solution)/shard_map/ppermute | solution.py:516
  558.1 66.7 %collective-permute-start.53 = (bf16[960,128]{1,0:T(8,128)(2,1)}, bf16[960,128]{1,0:T(8,128)(2,1)}, u32[]{:S(2)}, u32[]{:S(2)}) collective-permute-start(bf16[960,128]{1,0:T(8,128)(2,1)} %collective-permute-done.52.refs_1_), channel_id=1, source_target_pairs={{0,1},{1,0},{2,3},{3,2},{4,5},{5,4},{6,7},{7,6}} | collective-permute-start | bytes 737288 | tf_op jit(solution)/shard_map/ppermute | solution.py:516
  558.1 66.7 %collective-permute-start.55 = (bf16[960,128]{1,0:T(8,128)(2,1)}, bf16[960,128]{1,0:T(8,128)(2,1)}, u32[]{:S(2)}, u32[]{:S(2)}) collective-permute-start(bf16[960,128]{1,0:T(8,128)(2,1)} %collective-permute-done.54.refs_3_), channel_id=1, source_target_pairs={{0,1},{1,0},{2,3},{3,2},{4,5},{5,4},{6,7},{7,6}} | collective-permute-start | bytes 737288 | tf_op jit(solution)/shard_map/ppermute | solution.py:516
  558.6 63.7 %collective-permute-start.49 = (bf16[1440,128]{1,0:T(8,128)(2,1)}, bf16[1440,128]{1,0:T(8,128)(2,1)}, u32[]{:S(2)}, u32[]{:S(2)}) collective-permute-start(bf16[1440,128]{1,0:T(8,128)(2,1)} %collective-permute-done.48.refs_1_), channel_id=1, source_target_pairs={{0,1},{1,0},{2,3},{3,2},{4,5},{5,4},{6,7},{7,6}} | collective-permute-start | bytes 1105928 | tf_op jit(solution)/shard_map/ppermute | solution.py:516
  561.1 61.2 %collective-permute-start.51 = (bf16[1440,128]{1,0:T(8,128)(2,1)}, bf16[1440,128]{1,0:T(8,128)(2,1)}, u32[]{:S(2)}, u32[]{:S(2)}) collective-permute-start(bf16[1440,128]{1,0:T(8,128)(2,1)} %collective-permute-done.50.refs_3_), channel_id=1, source_target_pairs={{0,1},{1,0},{2,3},{3,2},{4,5},{5,4},{6,7},{7,6}} | collective-permute-start | bytes 1105928 | tf_op jit(solution)/shard_map/ppermute | solution.py:516
  562.9 56.6 %collective-permute-start.47 = (bf16[2400,128]{1,0:T(8,128)(2,1)}, bf16[2400,128]{1,0:T(8,128)(2,1)}, u32[]{:S(2)}, u32[]{:S(2)}) collective-permute-start(bf16[2400,128]{1,0:T(8,128)(2,1)} %collective-permute-done.46.refs_3_), channel_id=1, source_target_pairs={{0,1},{1,0},{2,3},{3,2},{4,5},{5,4},{6,7},{7,6}} | collective-permute-start | bytes 1843208 | tf_op jit(solution)/shard_map/ppermute | solution.py:516
  (77 other events, 961.7 us)

commit v6 on v5

--- a/solution.py
+++ b/solution.py
@@ -21,7 +21,7 @@
 MESH = pl.DeviceIdType.MESH
 LANES = 128
 DEVICES = 8
-CHUNKS = 12
+CHUNKS = 15
 BLOCK = 160
 ADAM_ROWS = 480
 HEAD_ROWS = 480
@@ -135,8 +135,8 @@
     vsend[...] = vraw[...].astype(jnp.float32).reshape(DEVICES, vec_rows, LANES).astype(jnp.bfloat16)
     vrecv[me] = vsend[me]
 
-    def pack_all(phase, plan, next_plan, c):
-        for h in range(8):
+    def pack_units(phase, plan, next_plan, c, units):
+        for h in units:
             load_raw(plan, h, c).wait()
             pack(plan, h, c)
 
@@ -149,23 +149,23 @@
                 def _():
                     load_raw(next_plan, h, 0).start()
 
-            if 1 <= h <= 6:
+            if h - 1 in units and h <= 6:
                 to_stage(phase, h - 1, c).start()
 
-    def send_all(phase, plan, c):
-        for h in range(6):
+    def send_units(phase, plan, c, units):
+        for h in units:
             to_stage(phase, h, c).wait()
             send(phase, plan, h, c).start()
 
     def step(phase, plan, next_plan):
         def body(c, _):
-            pack_all(phase, plan, next_plan, c)
-            send_all(phase, plan, c)
+            pack_units(phase, plan, next_plan, c, range(8))
+            send_units(phase, plan, c, range(6))
             return 0
 
         return body
 
-    pack_all(0, first_plan, direct_plan, 0)
+    pack_units(0, first_plan, direct_plan, 0, range(4))
 
     pl.semaphore_wait(barrier, DEVICES - 1)
 
@@ -175,19 +175,32 @@
             src_ref=vsend.at[target], dst_ref=vrecv.at[me], send_sem=vec_send.at[o], recv_sem=vec_recv.at[me],
             device_id=(target,), device_id_type=MESH)
 
-    def part_copy(o):
+    partners = [dev(1 - y, 1 - x, core), y_mine, x_mine, sib]
+
+    def part_copy(k):
         return pltpu.make_async_remote_copy(
-            src_ref=vpart, dst_ref=vall.at[me], send_sem=part_send.at[o], recv_sem=part_recv.at[me],
-            device_id=((me + o) % DEVICES,), device_id_type=MESH)
+            src_ref=vpart, dst_ref=vall.at[me], send_sem=part_send.at[k], recv_sem=part_recv.at[me],
+            device_id=(partners[k],), device_id_type=MESH)
+
+    def part_pass(k):
+        return pltpu.make_async_remote_copy(
+            src_ref=vall.at[partners[k]], dst_ref=vall.at[partners[k]], send_sem=part_send.at[4 + k],
+            recv_sem=part_recv.at[partners[k]], device_id=(sib,), device_id_type=MESH)
+
+    def part_landed(src):
+        pltpu.make_async_copy(vall.at[src], vall.at[src], part_recv.at[src]).wait()
 
     def landed(buf, sems, o):
         src = (me + o) % DEVICES
         pltpu.make_async_copy(buf.at[src], buf.at[src], sems.at[src]).wait()
 
+    to_stage(0, 3, 0).start()
+    send_units(0, first_plan, 0, range(4))
     for o in range(1, DEVICES):
         vec_copy(o).start()
 
-    send_all(0, first_plan, 0)
+    pack_units(0, first_plan, direct_plan, 0, range(4, 8))
+    send_units(0, first_plan, 0, range(4, 6))
     lax.fori_loop(1, CHUNKS, step(0, first_plan, direct_plan), 0)
     for o in range(1, DEVICES):
         landed(vrecv, vec_recv, o)
@@ -197,8 +210,8 @@
     vpart[...] = vec_total / DEVICES
     vall[me] = vec_total / DEVICES
     lax.fori_loop(0, CHUNKS, step(1, direct_plan, None), 0)
-    for o in range(1, DEVICES):
-        part_copy(o).start()
+    for k in range(4):
+        part_copy(k).start()
 
     def got_all(ref, sem):
         pltpu.make_async_copy(ref, ref, sem).wait()
@@ -234,8 +247,15 @@
     lax.fori_loop(0, CHUNKS, relay_step, 0)
 
     fsum_copy(1, CHUNKS - 1).start()
-    for o in range(1, DEVICES):
-        landed(vall, part_recv, o)
+    for k in range(3):
+        part_landed(partners[k])
+        part_pass(k).start()
+    part_landed(sib)
+    for side in range(2):
+        for slot in range(3):
+            got_all(direct.at[side, slot], direct_recv.at[side, slot])
+    for other in (x_sib, y_sib, dev(1 - y, 1 - x, 1 - core)):
+        part_landed(other)
     vec_norm = jnp.sum((vall[...] * vall[...]).reshape(-1, 8, LANES), axis=0)
     vec_out = pltpu.make_async_copy(vall, vsum_ref, late_sem.at[0])
     vec_out.start()
@@ -271,9 +291,6 @@
                     out_copy(1, c - 1).start()
         return acc
 
-    for side in range(2):
-        for slot in range(3):
-            got_all(direct.at[side, slot], direct_recv.at[side, slot])
     acc = lax.fori_loop(0, CHUNKS, final_step, jnp.zeros((8, LANES), jnp.float32))
     nsend[...] = acc
     nrecv[me] = acc
@@ -295,7 +312,10 @@
         got_all(psum.at[side], out_sem.at[side])
     for o in range(1, DEVICES):
         vec_copy(o).wait_send()
-        part_copy(o).wait_send()
+    for k in range(4):
+        part_copy(k).wait_send()
+    for k in range(3):
+        part_pass(k).wait_send()
     for o in range(1, DEVICES):
         landed(nrecv, nrm_recv, o)
     tile = vec_norm

time: 629 us -> 629 us (level)
  transfers between devices with their start and end apart: 56 -> 56, of which waited for: 23 -> 24; matrix products, arithmetic and copies ran while one was open for 1% -> 1% of each run, Pallas kernels for 7% -> 7%
where the time goes in v6:
time: 629 us; the launch traced here: 627 us
  Pallas kernels  409 us (65%)
  waiting for transfers between devices  144 us (23%)
  local copies, waits for them, and re-layouts  43.1 us (7%)
  starting transfers between devices  26.6 us (4%)
    pallas_call x1, Pallas kernels, reduce_gradients(): pl.pallas_call(functools.partial(reduce_kernel, axis_name, half_rows), ou...  329 us
    ppermute x56, waiting for transfers between devices, move(): return lax.ppermute(array, axis_name, pairs)  144 us
    pallas_call x8, Pallas kernels, adam_chunk(): pl.pallas_call(functools.partial(adam_kernel, start), out_shape=(whole, w...  42.9 us
    unnamed x138, local copies, waits for them, and re-layouts  41.9 us
    pallas_call x8, Pallas kernels, place(): pl.pallas_call(functools.partial(place_kernel, axis_name, tuple(((who, st...  36.3 us
    ppermute x56, starting transfers between devices, move(): return lax.ppermute(array, axis_name, pairs)  26.6 us
  transfers between devices with their start and end apart: 56, of which 24 were waited for; matrix products, arithmetic and copies ran while one was open for 1% of the time, Pallas kernels for 7%

profile of v6, /device:TPU:0, one launch (start us, length us, event | category | flops | bytes accessed | tf_op | source)
XLA Modules:
  0.0 626.6 jit_solution(247731156150835206)
XLA Ops:
  1.3 329.4 %reduce_gradients.1 = (f32[19200,128]{1,0:T(8,128)}, f32[8,24,128]{2,1,0:T(8,128)}, f32[8,128]{1,0:T(8,128)}, bf16[1440,128]{1,0:T(8,128)(2,1)}, bf16[12,9600,128]{2,1,0:T(8,128)(2,1)}) custom-call(f32[1]{0:T(128)} %bitcast.10.lr_ref, bf16[1,19660800]{1,0:T(2,128)(2,1)} %g_ref.1, bf16[1,24320]{1,0:T(2,128)(2,1)} %gv_raw_ref.1, f32[19200,128]{1,0:T(8,128)} %bitcast.20, ...), custom_call_target="tpu_custom_call" | custom-call | tf_op jit(solution)/shard_map/reduce_gradients/pallas_call | solution.py:361
  330.7 4.9 shard_map.144
  335.6 8.5 %shard_map.145 = (f32[19200,128]{1,0:T(8,128)}, f32[19200,128]{1,0:T(8,128)}, f32[19200,128]{1,0:T(8,128)}, bf16[4800,128]{1,0:T(8,128)(2,1)}) custom-call(f32[1]{0:T(128)} %bitcast.12.lr_ref, f32[8,128]{1,0:T(8,128)} %get-tuple-element.42.clip_ref, ...), custom_call_target="tpu_custom_call", output_to_operand_aliasing={{0}: (6, {}), {1}: (7, {}), {2}: (8, {})} | custom-call | flops 36864000 | bytes 18432000 | tf_op jit(solution)/shard_map/pallas_call | solution.py:464
  344.1 8.5 %shard_map.146 = (f32[19200,128]{1,0:T(8,128)}, f32[19200,128]{1,0:T(8,128)}, f32[19200,128]{1,0:T(8,128)}, bf16[4800,128]{1,0:T(8,128)(2,1)}) custom-call(f32[1]{0:T(128)} %bitcast.13.lr_ref, f32[8,128]{1,0:T(8,128)} %get-tuple-element.42.clip_ref, ...), custom_call_target="tpu_custom_call", output_to_operand_aliasing={{0}: (6, {}), {1}: (7, {}), {2}: (8, {})} | custom-call | flops 36864000 | bytes 18432000 | tf_op jit(solution)/shard_map/pallas_call | solution.py:464
  352.7 4.9 shard_map.147
  357.6 4.2 shard_map.148
  361.8 3.8 shard_map.149
  365.7 1.5 collective-permute-start.31
  367.8 3.8 shard_map.150
  372.1 1.2 collective-permute-start.36
  377.0 1.5 collective-permute-start.3
  378.6 2.6 collective-permute-done.36.refs_21_
  381.1 2.2 collective-permute-done.38.refs_23_
  383.4 1.5 collective-permute-start.26
  385.4 3.7 collective-permute-done.1.refs_2_
  389.0 2.2 collective-permute-done.3.refs_4_
  392.5 3.5 collective-permute-done.26.refs_9_
  396.0 1.7 collective-permute-done.28.refs_11_
  399.1 1.5 collective-permute-start.52
  403.2 1.2 collective-permute-start.6
  406.0 2.3 collective-permute-done.52.refs_1_
  408.3 2.0 collective-permute-done.54.refs_3_
  412.0 9.4 %collective-permute-done.6.refs_8_ = bf16[2400,128]{1,0:T(8,128)(2,1)S(1)} collective-permute-done((bf16[2400,128]{1,0:T(8,128)(2,1)}, bf16[2400,128]{1,0:T(8,128)(2,1)S(1)}, u32[]{:S(2)}, u32[]{:S(2)}) %collective-permute-start.6) | collective-permute-done | bytes 614432 | tf_op jit(solution)/shard_map/ppermute | solution.py:536
  421.4 2.0 collective-permute-done.8.refs_10_
  424.8 9.3 %collective-permute-done.21.refs_3_ = bf16[2400,128]{1,0:T(8,128)(2,1)S(1)} collective-permute-done((bf16[2400,128]{1,0:T(8,128)(2,1)}, bf16[2400,128]{1,0:T(8,128)(2,1)S(1)}, u32[]{:S(2)}, u32[]{:S(2)}) %collective-permute-start.21) | collective-permute-done | bytes 614432 | tf_op jit(solution)/shard_map/ppermute | solution.py:536
  434.1 1.7 collective-permute-done.23.refs_5_
  439.1 1.5 collective-permute-start.11
  440.6 7.5 %collective-permute-done.48.refs_1_ = bf16[1440,128]{1,0:T(8,128)(2,1)} collective-permute-done((bf16[1440,128]{1,0:T(8,128)(2,1)S(1)}, bf16[1440,128]{1,0:T(8,128)(2,1)}, u32[]{:S(2)}, u32[]{:S(2)}) %collective-permute-start.48) | collective-permute-done | bytes 368672 | tf_op jit(solution)/shard_map/ppermute | solution.py:536
  449.4 8.5 %collective-permute-done.50.refs_3_ = bf16[1440,128]{1,0:T(8,128)(2,1)} collective-permute-done((bf16[1440,128]{1,0:T(8,128)(2,1)S(1)}, bf16[1440,128]{1,0:T(8,128)(2,1)}, u32[]{:S(2)}, u32[]{:S(2)}) %collective-permute-start.50) | collective-permute-done | bytes 368672 | tf_op jit(solution)/shard_map/ppermute | solution.py:536
  459.3 1.2 collective-permute-start.16
  461.5 12.9 %collective-permute-done.11.refs_3_ = bf16[4800,128]{1,0:T(8,128)(2,1)S(1)} collective-permute-done((bf16[4800,128]{1,0:T(8,128)(2,1)}, bf16[4800,128]{1,0:T(8,128)(2,1)S(1)}, u32[]{:S(2)}, u32[]{:S(2)}) %collective-permute-start.11) | collective-permute-done | bytes 1228832 | tf_op jit(solution)/shard_map/ppermute | solution.py:536
  475.2 12.8 %collective-permute-done.13.refs_5_ = bf16[4800,128]{1,0:T(8,128)(2,1)S(1)} collective-permute-done((bf16[4800,128]{1,0:T(8,128)(2,1)}, bf16[4800,128]{1,0:T(8,128)(2,1)S(1)}, u32[]{:S(2)}, u32[]{:S(2)}) %collective-permute-start.13) | collective-permute-done | bytes 1228832 | tf_op jit(solution)/shard_map/ppermute | solution.py:536
  488.5 11.7 %collective-permute-done.16.refs_3_ = bf16[4800,128]{1,0:T(8,128)(2,1)S(1)} collective-permute-done((bf16[4800,128]{1,0:T(8,128)(2,1)}, bf16[4800,128]{1,0:T(8,128)(2,1)S(1)}, u32[]{:S(2)}, u32[]{:S(2)}) %collective-permute-start.16) | collective-permute-done | bytes 1228832 | tf_op jit(solution)/shard_map/ppermute | solution.py:536
  500.2 14.1 %collective-permute-done.18.refs_5_ = bf16[4800,128]{1,0:T(8,128)(2,1)S(1)} collective-permute-done((bf16[4800,128]{1,0:T(8,128)(2,1)}, bf16[4800,128]{1,0:T(8,128)(2,1)S(1)}, u32[]{:S(2)}, u32[]{:S(2)}) %collective-permute-start.18) | collective-permute-done | bytes 1228832 | tf_op jit(solution)/shard_map/ppermute | solution.py:536
  519.4 8.1 %collective-permute-done.44.refs_1_ = bf16[2400,128]{1,0:T(8,128)(2,1)S(1)} collective-permute-done((bf16[2400,128]{1,0:T(8,128)(2,1)S(1)}, bf16[2400,128]{1,0:T(8,128)(2,1)S(1)}, u32[]{:S(2)}, u32[]{:S(2)}) %collective-permute-start.44) | collective-permute-done | bytes 614432 | tf_op jit(solution)/shard_map/ppermute | solution.py:536
  528.3 23.0 %collective-permute-done.46.refs_3_ = bf16[2400,128]{1,0:T(8,128)(2,1)} collective-permute-done((bf16[2400,128]{1,0:T(8,128)(2,1)S(1)}, bf16[2400,128]{1,0:T(8,128)(2,1)}, u32[]{:S(2)}, u32[]{:S(2)}) %collective-permute-start.46) | collective-permute-done | bytes 614432 | tf_op jit(solution)/shard_map/ppermute | solution.py:536
  556.5 1.2 slice.7
  558.2 1.4 collective-permute-done.41.refs_2_
  562.6 2.4 multiply_subtract_fusion
  565.1 4.2 shard_map.151
  569.2 5.2 shard_map.152.refs_0_
  574.4 6.0 shard_map.153.refs_0_
  580.5 6.0 shard_map.154.refs_0_
  607.4 9.3 %shard_map.155.refs_0_ = bf16[153600,128]{1,0:T(8,128)(2,1)} custom-call(bf16[153600,128]{1,0:T(8,128)(2,1)} %shard_map.154.refs_0_, bf16[2400,128]{1,0:T(8,128)(2,1)S(1)} %copy-done.8, bf16[2400,128]{1,0:T(8,128)(2,1)S(1)} %copy-done.10, bf16[2400,128]{1,0:T(8,128)(2,1)S(1)} %copy-done.12, ...), custom_call_target="tpu_custom_call", output_to_operand_aliasing={{}: (0, {})} | custom-call | flops 66355200 | bytes 17694720 | tf_op jit(solution)/shard_map/pallas_call | solution.py:516
  616.8 2.3 shard_map.156.refs_0_
  619.1 2.7 shard_map.157.refs_0_
  621.9 2.5 shard_map.158.refs_0_
  624.4 2.3 shard_map.159
  (221 shorter events, 59.2 us)
Async XLA Ops:
  365.6 6.5 %collective-permute-start.30 = (bf16[960,128]{1,0:T(8,128)(2,1)}, bf16[960,128]{1,0:T(8,128)(2,1)}, u32[]{:S(2)}, u32[]{:S(2)}) collective-permute-start(bf16[960,128]{1,0:T(8,128)(2,1)} %get-tuple-element.75.refs_13_), channel_id=1, source_target_pairs={{0,1},{1,0},{2,3},{3,2},{4,5},{5,4},{6,7},{7,6}} | collective-permute-start | bytes 737288 | tf_op jit(solution)/shard_map/ppermute | solution.py:536
  365.7 8.6 %collective-permute-start.31 = (bf16[960,128]{1,0:T(8,128)(2,1)}, bf16[960,128]{1,0:T(8,128)(2,1)}, u32[]{:S(2)}, u32[]{:S(2)}) collective-permute-start(bf16[960,128]{1,0:T(8,128)(2,1)} %get-tuple-element.75.refs_13_), channel_id=1, source_target_pairs={{0,2},{1,3},{2,0},{3,1},{4,6},{5,7},{6,4},{7,5}} | collective-permute-start | bytes 737288 | tf_op jit(solution)/shard_map/ppermute | solution.py:536
  367.2 8.3 %collective-permute-start.33 = (bf16[960,128]{1,0:T(8,128)(2,1)}, bf16[960,128]{1,0:T(8,128)(2,1)}, u32[]{:S(2)}, u32[]{:S(2)}) collective-permute-start(bf16[960,128]{1,0:T(8,128)(2,1)} %get-tuple-element.75.refs_13_), channel_id=1, source_target_pairs={{0,4},{1,5},{2,6},{3,7},{4,0},{5,1},{6,2},{7,3}} | collective-permute-start | bytes 737288 | tf_op jit(solution)/shard_map/ppermute | solution.py:536
  367.8 17.1 %collective-permute-start = (bf16[1440,128]{1,0:T(8,128)(2,1)}, bf16[1440,128]{1,0:T(8,128)(2,1)}, u32[]{:S(2)}, u32[]{:S(2)}) collective-permute-start(bf16[1440,128]{1,0:T(8,128)(2,1)} %get-tuple-element.69.refs_0_), channel_id=1, source_target_pairs={{0,1},{1,0},{2,3},{3,2},{4,5},{5,4},{6,7},{7,6}} | collective-permute-start | bytes 1105928 | tf_op jit(solution)/shard_map/ppermute | solution.py:536
  372.1 9.0 %collective-permute-start.36 = (bf16[960,128]{1,0:T(8,128)(2,1)}, bf16[960,128]{1,0:T(8,128)(2,1)S(1)}, u32[]{:S(2)}, u32[]{:S(2)}) collective-permute-start(bf16[960,128]{1,0:T(8,128)(2,1)} %get-tuple-element.76.refs_19_), channel_id=1, source_target_pairs={{0,2},{1,3},{2,0},{3,1},{4,6},{5,7},{6,4},{7,5}} | collective-permute-start | bytes 737288 | tf_op jit(solution)/shard_map/ppermute | solution.py:536
  374.3 9.0 %collective-permute-start.38 = (bf16[960,128]{1,0:T(8,128)(2,1)}, bf16[960,128]{1,0:T(8,128)(2,1)S(1)}, u32[]{:S(2)}, u32[]{:S(2)}) collective-permute-start(bf16[960,128]{1,0:T(8,128)(2,1)} %get-tuple-element.76.refs_19_), channel_id=1, source_target_pairs={{0,4},{1,5},{2,6},{3,7},{4,0},{5,1},{6,2},{7,3}} | collective-permute-start | bytes 737288 | tf_op jit(solution)/shard_map/ppermute | solution.py:536
  375.5 13.5 %collective-permute-start.1 = (bf16[1440,128]{1,0:T(8,128)(2,1)}, bf16[1440,128]{1,0:T(8,128)(2,1)S(1)}, u32[]{:S(2)}, u32[]{:S(2)}) collective-permute-start(bf16[1440,128]{1,0:T(8,128)(2,1)} %get-tuple-element.69.refs_0_), channel_id=1, source_target_pairs={{0,2},{1,3},{2,0},{3,1},{4,6},{5,7},{6,4},{7,5}} | collective-permute-start | bytes 1105928 | tf_op jit(solution)/shard_map/ppermute | solution.py:536
  377.0 14.2 %collective-permute-start.3 = (bf16[1440,128]{1,0:T(8,128)(2,1)}, bf16[1440,128]{1,0:T(8,128)(2,1)S(1)}, u32[]{:S(2)}, u32[]{:S(2)}) collective-permute-start(bf16[1440,128]{1,0:T(8,128)(2,1)} %get-tuple-element.69.refs_0_), channel_id=1, source_target_pairs={{0,4},{1,5},{2,6},{3,7},{4,0},{5,1},{6,2},{7,3}} | collective-permute-start | bytes 1105928 | tf_op jit(solution)/shard_map/ppermute | solution.py:536
  381.1 10.1 %collective-permute-start.25 = (bf16[1440,128]{1,0:T(8,128)(2,1)}, bf16[1440,128]{1,0:T(8,128)(2,1)S(1)}, u32[]{:S(2)}, u32[]{:S(2)}) collective-permute-start(bf16[1440,128]{1,0:T(8,128)(2,1)} %get-tuple-element.74.refs_7_), channel_id=1, source_target_pairs={{0,1},{1,0},{2,3},{3,2},{4,5},{5,4},{6,7},{7,6}} | collective-permute-start | bytes 1105928 | tf_op jit(solution)/shard_map/ppermute | solution.py:536
  383.4 12.7 %collective-permute-start.26 = (bf16[1440,128]{1,0:T(8,128)(2,1)}, bf16[1440,128]{1,0:T(8,128)(2,1)S(1)}, u32[]{:S(2)}, u32[]{:S(2)}) collective-permute-start(bf16[1440,128]{1,0:T(8,128)(2,1)} %get-tuple-element.74.refs_7_), channel_id=1, source_target_pairs={{0,2},{1,3},{2,0},{3,1},{4,6},{5,7},{6,4},{7,5}} | collective-permute-start | bytes 1105928 | tf_op jit(solution)/shard_map/ppermute | solution.py:536
  384.9 12.9 %collective-permute-start.28 = (bf16[1440,128]{1,0:T(8,128)(2,1)}, bf16[1440,128]{1,0:T(8,128)(2,1)S(1)}, u32[]{:S(2)}, u32[]{:S(2)}) collective-permute-start(bf16[1440,128]{1,0:T(8,128)(2,1)} %get-tuple-element.74.refs_7_), channel_id=1, source_target_pairs={{0,4},{1,5},{2,6},{3,7},{4,0},{5,1},{6,2},{7,3}} | collective-permute-start | bytes 1105928 | tf_op jit(solution)/shard_map/ppermute | solution.py:536
  389.0 21.8 %collective-permute-start.5 = (bf16[2400,128]{1,0:T(8,128)(2,1)}, bf16[2400,128]{1,0:T(8,128)(2,1)S(1)}, u32[]{:S(2)}, u32[]{:S(2)}) collective-permute-start(bf16[2400,128]{1,0:T(8,128)(2,1)} %get-tuple-element.70.refs_6_), channel_id=1, source_target_pairs={{0,1},{1,0},{2,3},{3,2},{4,5},{5,4},{6,7},{7,6}} | collective-permute-start | bytes 1843208 | tf_op jit(solution)/shard_map/ppermute | solution.py:536
  391.3 7.2 %collective-permute-start.32 = (bf16[960,128]{1,0:T(8,128)(2,1)}, bf16[960,128]{1,0:T(8,128)(2,1)S(1)}, u32[]{:S(2)}, u32[]{:S(2)}) collective-permute-start(bf16[960,128]{1,0:T(8,128)(2,1)} %collective-permute-done.31.refs_15_), channel_id=1, source_target_pairs={{0,1},{1,0},{2,3},{3,2},{4,5},{5,4},{6,7},{7,6}} | collective-permute-start | bytes 737288 | tf_op jit(solution)/shard_map/ppermute | solution.py:536
  392.0 8.6 %collective-permute-start.34 = (bf16[960,128]{1,0:T(8,128)(2,1)}, bf16[960,128]{1,0:T(8,128)(2,1)S(1)}, u32[]{:S(2)}, u32[]{:S(2)}) collective-permute-start(bf16[960,128]{1,0:T(8,128)(2,1)} %collective-permute-done.33.refs_17_), channel_id=1, source_target_pairs={{0,1},{1,0},{2,3},{3,2},{4,5},{5,4},{6,7},{7,6}} | collective-permute-start | bytes 737288 | tf_op jit(solution)/shard_map/ppermute | solution.py:536
  396.0 6.5 %collective-permute-start.37 = (bf16[960,128]{1,0:T(8,128)(2,1)S(1)}, bf16[960,128]{1,0:T(8,128)(2,1)S(1)}, u32[]{:S(2)}, u32[]{:S(2)}) collective-permute-start(bf16[960,128]{1,0:T(8,128)(2,1)S(1)} %collective-permute-done.36.refs_21_), channel_id=1, source_target_pairs={{0,1},{1,0},{2,3},{3,2},{4,5},{5,4},{6,7},{7,6}} | collective-permute-start | bytes 737288 | tf_op jit(solution)/shard_map/ppermute | solution.py:536
  397.7 6.7 %collective-permute-start.39 = (bf16[960,128]{1,0:T(8,128)(2,1)S(1)}, bf16[960,128]{1,0:T(8,128)(2,1)S(1)}, u32[]{:S(2)}, u32[]{:S(2)}) collective-permute-start(bf16[960,128]{1,0:T(8,128)(2,1)S(1)} %collective-permute-done.38.refs_23_), channel_id=1, source_target_pairs={{0,1},{1,0},{2,3},{3,2},{4,5},{5,4},{6,7},{7,6}} | collective-permute-start | bytes 737288 | tf_op jit(solution)/shard_map/ppermute | solution.py:536
  399.1 9.1 %collective-permute-start.52 = (bf16[960,128]{1,0:T(8,128)(2,1)}, bf16[960,128]{1,0:T(8,128)(2,1)}, u32[]{:S(2)}, u32[]{:S(2)}) collective-permute-start(bf16[960,128]{1,0:T(8,128)(2,1)} %collective-permute-done.33.refs_17_), channel_id=1, source_target_pairs={{0,2},{1,3},{2,0},{3,1},{4,6},{5,7},{6,4},{7,5}} | collective-permute-start | bytes 737288 | tf_op jit(solution)/shard_map/ppermute | solution.py:536
  401.3 8.9 %collective-permute-start.54 = (bf16[960,128]{1,0:T(8,128)(2,1)S(1)}, bf16[960,128]{1,0:T(8,128)(2,1)}, u32[]{:S(2)}, u32[]{:S(2)}) collective-permute-start(bf16[960,128]{1,0:T(8,128)(2,1)S(1)} %collective-permute-done.36.refs_21_), channel_id=1, source_target_pairs={{0,4},{1,5},{2,6},{3,7},{4,0},{5,1},{6,2},{7,3}} | collective-permute-start | bytes 737288 | tf_op jit(solution)/shard_map/ppermute | solution.py:536
  403.2 18.1 %collective-permute-start.6 = (bf16[2400,128]{1,0:T(8,128)(2,1)}, bf16[2400,128]{1,0:T(8,128)(2,1)S(1)}, u32[]{:S(2)}, u32[]{:S(2)}) collective-permute-start(bf16[2400,128]{1,0:T(8,128)(2,1)} %get-tuple-element.70.refs_6_), channel_id=1, source_target_pairs={{0,2},{1,3},{2,0},{3,1},{4,6},{5,7},{6,4},{7,5}} | collective-permute-start | bytes 1843208 | tf_op jit(solution)/shard_map/ppermute | solution.py:536
  405.1 18.2 %collective-permute-start.8 = (bf16[2400,128]{1,0:T(8,128)(2,1)}, bf16[2400,128]{1,0:T(8,128)(2,1)S(1)}, u32[]{:S(2)}, u32[]{:S(2)}) collective-permute-start(bf16[2400,128]{1,0:T(8,128)(2,1)} %get-tuple-element.70.refs_6_), channel_id=1, source_target_pairs={{0,4},{1,5},{2,6},{3,7},{4,0},{5,1},{6,2},{7,3}} | collective-permute-start | bytes 1843208 | tf_op jit(solution)/shard_map/ppermute | solution.py:536
  408.3 15.1 %collective-permute-start.20 = (bf16[2400,128]{1,0:T(8,128)(2,1)}, bf16[2400,128]{1,0:T(8,128)(2,1)S(1)}, u32[]{:S(2)}, u32[]{:S(2)}) collective-permute-start(bf16[2400,128]{1,0:T(8,128)(2,1)} %get-tuple-element.73.refs_1_), channel_id=1, source_target_pairs={{0,1},{1,0},{2,3},{3,2},{4,5},{5,4},{6,7},{7,6}} | collective-permute-start | bytes 1843208 | tf_op jit(solution)/shard_map/ppermute | solution.py:536
  410.3 23.8 %collective-permute-start.21 = (bf16[2400,128]{1,0:T(8,128)(2,1)}, bf16[2400,128]{1,0:T(8,128)(2,1)S(1)}, u32[]{:S(2)}, u32[]{:S(2)}) collective-permute-start(bf16[2400,128]{1,0:T(8,128)(2,1)} %get-tuple-element.73.refs_1_), channel_id=1, source_target_pairs={{0,2},{1,3},{2,0},{3,1},{4,6},{5,7},{6,4},{7,5}} | collective-permute-start | bytes 1843208 | tf_op jit(solution)/shard_map/ppermute | solution.py:536
  410.8 24.9 %collective-permute-start.23 = (bf16[2400,128]{1,0:T(8,128)(2,1)}, bf16[2400,128]{1,0:T(8,128)(2,1)S(1)}, u32[]{:S(2)}, u32[]{:S(2)}) collective-permute-start(bf16[2400,128]{1,0:T(8,128)(2,1)} %get-tuple-element.73.refs_1_), channel_id=1, source_target_pairs={{0,4},{1,5},{2,6},{3,7},{4,0},{5,1},{6,2},{7,3}} | collective-permute-start | bytes 1843208 | tf_op jit(solution)/shard_map/ppermute | solution.py:536
  421.4 39.1 %collective-permute-start.10 = (bf16[4800,128]{1,0:T(8,128)(2,1)}, bf16[4800,128]{1,0:T(8,128)(2,1)S(1)}, u32[]{:S(2)}, u32[]{:S(2)}) collective-permute-start(bf16[4800,128]{1,0:T(8,128)(2,1)} %get-tuple-element.71.refs_1_), channel_id=1, source_target_pairs={{0,1},{1,0},{2,3},{3,2},{4,5},{5,4},{6,7},{7,6}} | collective-permute-start | bytes 3686408 | tf_op jit(solution)/shard_map/ppermute | solution.py:536
  423.3 13.2 %collective-permute-start.2 = (bf16[1440,128]{1,0:T(8,128)(2,1)S(1)}, bf16[1440,128]{1,0:T(8,128)(2,1)S(1)}, u32[]{:S(2)}, u32[]{:S(2)}) collective-permute-start(bf16[1440,128]{1,0:T(8,128)(2,1)S(1)} %collective-permute-done.1.refs_2_), channel_id=1, source_target_pairs={{0,1},{1,0},{2,3},{3,2},{4,5},{5,4},{6,7},{7,6}} | collective-permute-start | bytes 1105928 | tf_op jit(solution)/shard_map/ppermute | solution.py:536
  424.3 12.8 %collective-permute-start.4 = (bf16[1440,128]{1,0:T(8,128)(2,1)S(1)}, bf16[1440,128]{1,0:T(8,128)(2,1)S(1)}, u32[]{:S(2)}, u32[]{:S(2)}) collective-permute-start(bf16[1440,128]{1,0:T(8,128)(2,1)S(1)} %collective-permute-done.3.refs_4_), channel_id=1, source_target_pairs={{0,1},{1,0},{2,3},{3,2},{4,5},{5,4},{6,7},{7,6}} | collective-permute-start | bytes 1105928 | tf_op jit(solution)/shard_map/ppermute | solution.py:536
  436.5 11.6 %collective-permute-start.48 = (bf16[1440,128]{1,0:T(8,128)(2,1)S(1)}, bf16[1440,128]{1,0:T(8,128)(2,1)}, u32[]{:S(2)}, u32[]{:S(2)}) collective-permute-start(bf16[1440,128]{1,0:T(8,128)(2,1)S(1)} %collective-permute-done.3.refs_4_), channel_id=1, source_target_pairs={{0,2},{1,3},{2,0},{3,1},{4,6},{5,7},{6,4},{7,5}} | collective-permute-start | bytes 1105928 | tf_op jit(solution)/shard_map/ppermute | solution.py:536
  437.1 21.3 %collective-permute-start.7 = (bf16[2400,128]{1,0:T(8,128)(2,1)S(1)}, bf16[2400,128]{1,0:T(8,128)(2,1)S(1)}, u32[]{:S(2)}, u32[]{:S(2)}) collective-permute-start(bf16[2400,128]{1,0:T(8,128)(2,1)S(1)} %collective-permute-done.6.refs_8_), channel_id=1, source_target_pairs={{0,1},{1,0},{2,3},{3,2},{4,5},{5,4},{6,7},{7,6}} | collective-permute-start | bytes 1843208 | tf_op jit(solution)/shard_map/ppermute | solution.py:536
  438.1 21.2 %collective-permute-start.9 = (bf16[2400,128]{1,0:T(8,128)(2,1)S(1)}, bf16[2400,128]{1,0:T(8,128)(2,1)S(1)}, u32[]{:S(2)}, u32[]{:S(2)}) collective-permute-start(bf16[2400,128]{1,0:T(8,128)(2,1)S(1)} %collective-permute-done.8.refs_10_), channel_id=1, source_target_pairs={{0,1},{1,0},{2,3},{3,2},{4,5},{5,4},{6,7},{7,6}} | collective-permute-start | bytes 1843208 | tf_op jit(solution)/shard_map/ppermute | solution.py:536
  439.1 35.2 %collective-permute-start.11 = (bf16[4800,128]{1,0:T(8,128)(2,1)}, bf16[4800,128]{1,0:T(8,128)(2,1)S(1)}, u32[]{:S(2)}, u32[]{:S(2)}) collective-permute-start(bf16[4800,128]{1,0:T(8,128)(2,1)} %get-tuple-element.71.refs_1_), channel_id=1, source_target_pairs={{0,2},{1,3},{2,0},{3,1},{4,6},{5,7},{6,4},{7,5}} | collective-permute-start | bytes 3686408 | tf_op jit(solution)/shard_map/ppermute | solution.py:536
  448.1 9.8 %collective-permute-start.50 = (bf16[1440,128]{1,0:T(8,128)(2,1)S(1)}, bf16[1440,128]{1,0:T(8,128)(2,1)}, u32[]{:S(2)}, u32[]{:S(2)}) collective-permute-start(bf16[1440,128]{1,0:T(8,128)(2,1)S(1)} %collective-permute-done.26.refs_9_), channel_id=1, source_target_pairs={{0,4},{1,5},{2,6},{3,7},{4,0},{5,1},{6,2},{7,3}} | collective-permute-start | bytes 1105928 | tf_op jit(solution)/shard_map/ppermute | solution.py:536
  457.9 30.1 %collective-permute-start.13 = (bf16[4800,128]{1,0:T(8,128)(2,1)}, bf16[4800,128]{1,0:T(8,128)(2,1)S(1)}, u32[]{:S(2)}, u32[]{:S(2)}) collective-permute-start(bf16[4800,128]{1,0:T(8,128)(2,1)} %get-tuple-element.71.refs_1_), channel_id=1, source_target_pairs={{0,4},{1,5},{2,6},{3,7},{4,0},{5,1},{6,2},{7,3}} | collective-permute-start | bytes 3686408 | tf_op jit(solution)/shard_map/ppermute | solution.py:536
  459.2 28.8 %collective-permute-start.15 = (bf16[4800,128]{1,0:T(8,128)(2,1)}, bf16[4800,128]{1,0:T(8,128)(2,1)S(1)}, u32[]{:S(2)}, u32[]{:S(2)}) collective-permute-start(bf16[4800,128]{1,0:T(8,128)(2,1)} %get-tuple-element.72.refs_1_), channel_id=1, source_target_pairs={{0,1},{1,0},{2,3},{3,2},{4,5},{5,4},{6,7},{7,6}} | collective-permute-start | bytes 3686408 | tf_op jit(solution)/shard_map/ppermute | solution.py:536
  459.3 41.0 %collective-permute-start.16 = (bf16[4800,128]{1,0:T(8,128)(2,1)}, bf16[4800,128]{1,0:T(8,128)(2,1)S(1)}, u32[]{:S(2)}, u32[]{:S(2)}) collective-permute-start(bf16[4800,128]{1,0:T(8,128)(2,1)} %get-tuple-element.72.refs_1_), channel_id=1, source_target_pairs={{0,2},{1,3},{2,0},{3,1},{4,6},{5,7},{6,4},{7,5}} | collective-permute-start | bytes 3686408 | tf_op jit(solution)/shard_map/ppermute | solution.py:536
  460.4 53.9 %collective-permute-start.18 = (bf16[4800,128]{1,0:T(8,128)(2,1)}, bf16[4800,128]{1,0:T(8,128)(2,1)S(1)}, u32[]{:S(2)}, u32[]{:S(2)}) collective-permute-start(bf16[4800,128]{1,0:T(8,128)(2,1)} %get-tuple-element.72.refs_1_), channel_id=1, source_target_pairs={{0,4},{1,5},{2,6},{3,7},{4,0},{5,1},{6,2},{7,3}} | collective-permute-start | bytes 3686408 | tf_op jit(solution)/shard_map/ppermute | solution.py:536
  474.3 40.5 %collective-permute-start.22 = (bf16[2400,128]{1,0:T(8,128)(2,1)S(1)}, bf16[2400,128]{1,0:T(8,128)(2,1)S(1)}, u32[]{:S(2)}, u32[]{:S(2)}) collective-permute-start(bf16[2400,128]{1,0:T(8,128)(2,1)S(1)} %collective-permute-done.21.refs_3_), channel_id=1, source_target_pairs={{0,1},{1,0},{2,3},{3,2},{4,5},{5,4},{6,7},{7,6}} | collective-permute-start | bytes 1843208 | tf_op jit(solution)/shard_map/ppermute | solution.py:536
  488.0 28.9 %collective-permute-start.24 = (bf16[2400,128]{1,0:T(8,128)(2,1)S(1)}, bf16[2400,128]{1,0:T(8,128)(2,1)S(1)}, u32[]{:S(2)}, u32[]{:S(2)}) collective-permute-start(bf16[2400,128]{1,0:T(8,128)(2,1)S(1)} %collective-permute-done.23.refs_5_), channel_id=1, source_target_pairs={{0,1},{1,0},{2,3},{3,2},{4,5},{5,4},{6,7},{7,6}} | collective-permute-start | bytes 1843208 | tf_op jit(solution)/shard_map/ppermute | solution.py:536
  488.0 39.5 %collective-permute-start.44 = (bf16[2400,128]{1,0:T(8,128)(2,1)S(1)}, bf16[2400,128]{1,0:T(8,128)(2,1)S(1)}, u32[]{:S(2)}, u32[]{:S(2)}) collective-permute-start(bf16[2400,128]{1,0:T(8,128)(2,1)S(1)} %collective-permute-done.6.refs_8_), channel_id=1, source_target_pairs={{0,4},{1,5},{2,6},{3,7},{4,0},{5,1},{6,2},{7,3}} | collective-permute-start | bytes 1843208 | tf_op jit(solution)/shard_map/ppermute | solution.py:536
  500.2 52.5 %collective-permute-start.12 = (bf16[4800,128]{1,0:T(8,128)(2,1)S(1)}, bf16[4800,128]{1,0:T(8,128)(2,1)S(1)}, u32[]{:S(2)}, u32[]{:S(2)}) collective-permute-start(bf16[4800,128]{1,0:T(8,128)(2,1)S(1)} %collective-permute-done.11.refs_3_), channel_id=1, source_target_pairs={{0,1},{1,0},{2,3},{3,2},{4,5},{5,4},{6,7},{7,6}} | collective-permute-start | bytes 3686408 | tf_op jit(solution)/shard_map/ppermute | solution.py:536
  514.3 39.4 %collective-permute-start.40 = (bf16[4800,128]{1,0:T(8,128)(2,1)S(1)}, bf16[4800,128]{1,0:T(8,128)(2,1)S(1)}, u32[]{:S(2)}, u32[]{:S(2)}) collective-permute-start(bf16[4800,128]{1,0:T(8,128)(2,1)S(1)} %collective-permute-done.13.refs_5_), channel_id=1, source_target_pairs={{0,2},{1,3},{2,0},{3,1},{4,6},{5,7},{6,4},{7,5}} | collective-permute-start | bytes 3686408 | tf_op jit(solution)/shard_map/ppermute | solution.py:536
  515.7 39.2 %collective-permute-start.42 = (bf16[4800,128]{1,0:T(8,128)(2,1)S(1)}, bf16[4800,128]{1,0:T(8,128)(2,1)S(1)}, u32[]{:S(2)}, u32[]{:S(2)}) collective-permute-start(bf16[4800,128]{1,0:T(8,128)(2,1)S(1)} %collective-permute-done.16.refs_3_), channel_id=1, source_target_pairs={{0,4},{1,5},{2,6},{3,7},{4,0},{5,1},{6,2},{7,3}} | collective-permute-start | bytes 3686408 | tf_op jit(solution)/shard_map/ppermute | solution.py:536
  517.7 33.7 %collective-permute-start.46 = (bf16[2400,128]{1,0:T(8,128)(2,1)S(1)}, bf16[2400,128]{1,0:T(8,128)(2,1)}, u32[]{:S(2)}, u32[]{:S(2)}) collective-permute-start(bf16[2400,128]{1,0:T(8,128)(2,1)S(1)} %collective-permute-done.23.refs_5_), channel_id=1, source_target_pairs={{0,2},{1,3},{2,0},{3,1},{4,6},{5,7},{6,4},{7,5}} | collective-permute-start | bytes 1843208 | tf_op jit(solution)/shard_map/ppermute | solution.py:536
  527.5 23.9 %collective-permute-start.45 = (bf16[2400,128]{1,0:T(8,128)(2,1)S(1)}, bf16[2400,128]{1,0:T(8,128)(2,1)S(1)}, u32[]{:S(2)}, u32[]{:S(2)}) collective-permute-start(bf16[2400,128]{1,0:T(8,128)(2,1)S(1)} %collective-permute-done.44.refs_1_), channel_id=1, source_target_pairs={{0,1},{1,0},{2,3},{3,2},{4,5},{5,4},{6,7},{7,6}} | collective-permute-start | bytes 1843208 | tf_op jit(solution)/shard_map/ppermute | solution.py:536
  557.6 66.7 %collective-permute-start.53 = (bf16[960,128]{1,0:T(8,128)(2,1)}, bf16[960,128]{1,0:T(8,128)(2,1)}, u32[]{:S(2)}, u32[]{:S(2)}) collective-permute-start(bf16[960,128]{1,0:T(8,128)(2,1)} %collective-permute-done.52.refs_1_), channel_id=1, source_target_pairs={{0,1},{1,0},{2,3},{3,2},{4,5},{5,4},{6,7},{7,6}} | collective-permute-start | bytes 737288 | tf_op jit(solution)/shard_map/ppermute | solution.py:536
  557.7 66.7 %collective-permute-start.55 = (bf16[960,128]{1,0:T(8,128)(2,1)}, bf16[960,128]{1,0:T(8,128)(2,1)}, u32[]{:S(2)}, u32[]{:S(2)}) collective-permute-start(bf16[960,128]{1,0:T(8,128)(2,1)} %collective-permute-done.54.refs_3_), channel_id=1, source_target_pairs={{0,1},{1,0},{2,3},{3,2},{4,5},{5,4},{6,7},{7,6}} | collective-permute-start | bytes 737288 | tf_op jit(solution)/shard_map/ppermute | solution.py:536
  558.2 63.7 %collective-permute-start.49 = (bf16[1440,128]{1,0:T(8,128)(2,1)}, bf16[1440,128]{1,0:T(8,128)(2,1)}, u32[]{:S(2)}, u32[]{:S(2)}) collective-permute-start(bf16[1440,128]{1,0:T(8,128)(2,1)} %collective-permute-done.48.refs_1_), channel_id=1, source_target_pairs={{0,1},{1,0},{2,3},{3,2},{4,5},{5,4},{6,7},{7,6}} | collective-permute-start | bytes 1105928 | tf_op jit(solution)/shard_map/ppermute | solution.py:536
  560.6 61.2 %collective-permute-start.51 = (bf16[1440,128]{1,0:T(8,128)(2,1)}, bf16[1440,128]{1,0:T(8,128)(2,1)}, u32[]{:S(2)}, u32[]{:S(2)}) collective-permute-start(bf16[1440,128]{1,0:T(8,128)(2,1)} %collective-permute-done.50.refs_3_), channel_id=1, source_target_pairs={{0,1},{1,0},{2,3},{3,2},{4,5},{5,4},{6,7},{7,6}} | collective-permute-start | bytes 1105928 | tf_op jit(solution)/shard_map/ppermute | solution.py:536
  562.5 56.6 %collective-permute-start.47 = (bf16[2400,128]{1,0:T(8,128)(2,1)}, bf16[2400,128]{1,0:T(8,128)(2,1)}, u32[]{:S(2)}, u32[]{:S(2)}) collective-permute-start(bf16[2400,128]{1,0:T(8,128)(2,1)} %collective-permute-done.46.refs_3_), channel_id=1, source_target_pairs={{0,1},{1,0},{2,3},{3,2},{4,5},{5,4},{6,7},{7,6}} | collective-permute-start | bytes 1843208 | tf_op jit(solution)/shard_map/ppermute | solution.py:536
  (77 other events, 961.7 us)
